TPU v7x, 128 devices: a whole 4x4x4 slice. The times are simulated.
128 devices in a mesh: row: 16 (over y_hi, x, core), col: 8 (over y_lo, z).
Axes of the slice: x: 4, y: 4 (y_hi: 2, y_lo: 2; y = y_hi * 2 + y_lo), z: 4, core: 2. Of those that a mesh axis runs over, the one named last changes fastest.
Arguments:
- queries: bfloat16 [1024, 32, 128], P(('row', 'col')), may hold values from -1 to 1
- documents: bfloat16 [1024, 128, 128], P(('row', 'col')), may hold values from -1 to 1
- lengths: int32 [1024], P(('row', 'col')), may hold values from 1 to 128
- positives: int32 [1024], P(('row', 'col')), may hold values from 0 to 1023
Outputs:
- query_loss: float32 [1024], P(('row', 'col'))
All inputs are finite; a program needn't handle non-finite values.
Results may differ from a plain program's by a relative error of at most 0.0003.
Values may be sent and summed in bfloat16 or wider, within the bound.
No kernel may reach another device: no remote copies, remote signals or barrier semaphores. Data moves between devices by JAX's collectives and lax.ppermute only.
A program may use at most 64 MiB of HBM per device.

v0:
```python
import jax
import jax.numpy as jnp
from jax import lax
from jax.sharding import PartitionSpec as P

neg_fill = -1e30


def copy_for_each(x, axis):
    length = lax.axis_size(axis)
    return lax.all_to_all(jnp.broadcast_to(x[None], (length, *x.shape)), axis, 0, 0, tiled=True)


def in_order(tiles, dim):
    tiles = jnp.moveaxis(tiles, 0, dim)
    shape = tiles.shape
    return tiles.reshape(*shape[:dim], shape[dim] * shape[dim + 1], *shape[dim + 2 :])


def collect(x, axis, dim):
    tiles = copy_for_each(x, axis)
    return in_order(tiles, dim)


def in_one_piece(arrays, axis, dim, along):
    columns = [a.reshape(*a.shape[:along], -1) for a in arrays]
    both = jnp.concatenate(columns, axis=along)
    filled, at, finished = (collect(both, axis, dim), 0, [])
    for a, column in zip(arrays, columns):
        slab = filled[..., at : at + column.shape[along]]
        finished.append(slab.reshape(*slab.shape[:along], *a.shape[along:]))
        at += column.shape[along]
    return tuple(finished)


def maxsim(query_rows, doc_rows, doc_lengths, group_docs):
    query_count = query_rows.shape[0]
    query_tokens = query_rows.shape[1]
    query_flat = query_rows.reshape(query_count * query_tokens, query_rows.shape[2])
    doc_count = doc_rows.shape[0]
    slot_count = doc_rows.shape[1]
    group_count = doc_count // group_docs
    grouped_docs = doc_rows.reshape(group_count, group_docs * slot_count, doc_rows.shape[2])
    grouped_lengths = doc_lengths.astype(jnp.float32).reshape(group_count, group_docs)
    token_slots = jnp.arange(slot_count, dtype=jnp.float32)

    def one_group(group_pair):
        block_docs, block_lengths = group_pair
        similar = lax.dot_general(
            query_flat, block_docs, (((1,), (1,)), ((), ())), preferred_element_type=jnp.float32
        )
        similar = similar.reshape(query_count * query_tokens, group_docs, slot_count)
        valid = token_slots[None, :] < block_lengths[:, None]
        similar = jnp.where(valid[None, :, :], similar, neg_fill)
        best = jnp.max(similar, axis=2).reshape(query_count, query_tokens, group_docs)
        return jnp.sum(best, axis=1)

    block_scores = lax.map(one_group, (grouped_docs, grouped_lengths))
    return jnp.transpose(block_scores, (1, 0, 2)).reshape(query_count, doc_count)


def finish(owner_scores, doc_ids, positives):
    peak_score = jnp.max(owner_scores, axis=1, keepdims=True)
    log_total = peak_score[:, 0] + jnp.log(jnp.sum(jnp.exp(owner_scores - peak_score), axis=1))
    positive_score = jnp.sum(
        jnp.where(doc_ids[None, :] == positives[:, None], owner_scores, 0.0), axis=1
    )
    return log_total - positive_score


def local(queries, documents, lengths, positives):
    per_device = queries.shape[0]
    row_count = lax.axis_size("row")
    col_count = lax.axis_size("col")
    length_wire = lengths.astype(jnp.bfloat16)
    doc_group, length_group = in_one_piece((documents, length_wire), "col", 0, 1)
    block_scores = maxsim(collect(queries, "row", 0), doc_group, length_group, per_device)
    owner_scores = lax.all_to_all(block_scores, "row", split_axis=0, concat_axis=1, tiled=True)
    doc_ids = jnp.arange(row_count * col_count * per_device, dtype=jnp.int32)
    query_loss = finish(owner_scores, doc_ids, positives)
    return query_loss


def solution(mesh):
    placed = (
        P(("row", "col"), None, None),
        P(("row", "col"), None, None),
        P(("row", "col")),
        P(("row", "col")),
    )
    return jax.shard_map(
        local, mesh=mesh, in_specs=placed, out_specs=P(("row", "col")), check_vma=False
    )
```

profile of v0, /device:TPU:0, one launch (start us, length us, event | category | flops | bytes accessed | tf_op | source)
XLA Modules:
  0.0 111.0 jit_solution(8719308056382183870)
XLA Ops:
  0.0 0.7 convert_bitcast_fusion
  0.7 0.1 copy.12
  0.8 1.1 %copy.16 = bf16[1,8,128,128]{3,1,2,0:T(8,128)(2,1)S(1)} copy(bf16[1,8,128,128]{3,2,1,0:T(8,128)(2,1)} %bitcast.49) | data formatting | bytes 524288
  1.9 0.1 broadcast_in_dim.42
  2.1 0.0 copy-start
  2.1 34.0 %all_to_all.26 = bf16[8,8,16385]{2,1,0:T(8,128)(2,1)S(1)} all-to-all(bf16[8,8,16385]{2,1,0:T(8,128)(2,1)S(1)} %broadcast_in_dim.42), channel_id=1, replica_groups=mesh['row'=16,'col'=8] {'col'}, dimensions={0} | all-to-all | bytes 4194560 | tf_op jit(solution)/shard_map/all_to_all | solution.py:11
  36.1 0.0 copy-done
  36.1 1.2 %broadcast_in_dim.43 = bf16[16,8,32,128]{3,2,1,0:T(8,128)(2,1)} broadcast(bf16[8,32,128]{2,1,0:T(8,128)(2,1)S(1)} %copy-done), dimensions={1,2,3} | broadcast | bytes 1114112 | tf_op jit(solution)/shard_map/broadcast_in_dim | solution.py:11
  37.3 6.8 %all-to-all-start.1 = ((bf16[16,8,32,128]{3,2,1,0:T(8,128)(2,1)}), bf16[16,8,32,128]{3,2,1,0:T(8,128)(2,1)}, u32[]{:S(2)}, u32[]{:S(2)}) async-start(bf16[16,8,32,128]{3,2,1,0:T(8,128)(2,1)} %broadcast_in_dim.43), calls=%async_computation.1 | async-start | bytes 2097152 | tf_op jit(solution)/shard_map/all_to_all | solution.py:11
  44.1 1.5 %slice.9 = bf16[64,16384]{1,0:T(8,128)(2,1)} slice(bf16[64,16385]{1,0:T(8,128)(2,1)S(1)} %bitcast.46), slice={[0:64], [0:16384]} | slice | bytes 4194304 | tf_op jit(solution)/shard_map/slice | solution.py:30
  45.6 0.1 convert_reduce_fusion
  45.7 0.1 reshape.81
  45.8 2.9 %reshape_reshape.6 = bf16[8,1024,128]{2,1,0:T(8,128)(2,1)S(1)} reshape(bf16[64,16384]{1,0:T(8,128)(2,1)} %slice.9) | data formatting | bytes 4194304 | tf_op jit(solution)/shard_map/reshape;reshape | solution.py:43
  48.7 13.4 %all-to-all-done.1 = bf16[16,8,32,128]{3,2,1,0:T(8,128)(2,1)} async-done(((bf16[16,8,32,128]{3,2,1,0:T(8,128)(2,1)}), bf16[16,8,32,128]{3,2,1,0:T(8,128)(2,1)}, u32[]{:S(2)}, u32[]{:S(2)}) %all-to-all-start.1) | async-done | bytes 1048608 | tf_op jit(solution)/shard_map/all_to_all | solution.py:11
  62.1 0.0 copy-start.1
  62.1 34.4 %while.11 = (s32[]{:T(128)}, f32[8,128,8]{1,2,0:T(8,128)S(1)}, f32[8,8]{1,0:T(8,128)S(1)}, bf16[8,1024,128]{2,1,0:T(8,128)(2,1)S(1)}, bf16[4096,128]{1,0:T(8,128)(2,1)}, /*index=5*/s32[]{:T(128)}, f32[]{:T(128)}) while((s32[]{:T(128)}, f32[8,128,8]{1,2,0:T(8,128)S(1)}, f32[8,8]{1,0:T(8,128)S(1)}, ...), condition=%wide.region_3.4_spmd.clone, body=%wide.region_0.3_spmd.clone.sunk | while | flops 1082130432 | bytes 1849541 | solution.py:58
  62.1 0.1 iota_compare_fusion.2
  62.2 3.8 %select_reduce_fusion.2 = f32[4096,8]{0,1:T(8,128)S(1)} fusion(pred[8,128]{1,0:T(8,128)(4,1)S(1)} %iota_compare_fusion.2, bf16[4096,128]{1,0:T(8,128)(2,1)} %get-tuple-element.111, bf16[8,1024,128]{2,1,0:T(8,128)(2,1)S(1)} %get-tuple-element.110, s32[]{:T(128)S(6)} %copy.20), kind=kOutput, calls=%fused_computation.1.clone.1 | convolution fusion | flops 1082097664 | bytes 1442820 | tf_op jit(solution)/shard_map/while/body/eval_jaxpr/dot_general | solution.py:49
  66.0 0.2 reshape.88
  66.2 0.2 reduce_sum.33
  66.4 0.1 iota_compare_fusion.2
  66.5 3.8 %select_reduce_fusion.2 = f32[4096,8]{0,1:T(8,128)S(1)} fusion(pred[8,128]{1,0:T(8,128)(4,1)S(1)} %iota_compare_fusion.2, bf16[4096,128]{1,0:T(8,128)(2,1)} %get-tuple-element.111, bf16[8,1024,128]{2,1,0:T(8,128)(2,1)S(1)} %get-tuple-element.110, s32[]{:T(128)S(6)} %copy.20), kind=kOutput, calls=%fused_computation.1.clone.1 | convolution fusion | flops 1082097664 | bytes 1442820 | tf_op jit(solution)/shard_map/while/body/eval_jaxpr/dot_general | solution.py:49
  70.3 0.2 reshape.88
  70.5 0.2 reduce_sum.33
  70.7 0.1 iota_compare_fusion.2
  70.8 3.8 %select_reduce_fusion.2 = f32[4096,8]{0,1:T(8,128)S(1)} fusion(pred[8,128]{1,0:T(8,128)(4,1)S(1)} %iota_compare_fusion.2, bf16[4096,128]{1,0:T(8,128)(2,1)} %get-tuple-element.111, bf16[8,1024,128]{2,1,0:T(8,128)(2,1)S(1)} %get-tuple-element.110, s32[]{:T(128)S(6)} %copy.20), kind=kOutput, calls=%fused_computation.1.clone.1 | convolution fusion | flops 1082097664 | bytes 1442820 | tf_op jit(solution)/shard_map/while/body/eval_jaxpr/dot_general | solution.py:49
  74.6 0.2 reshape.88
  74.7 0.2 reduce_sum.33
  75.0 0.1 iota_compare_fusion.2
  75.1 3.8 %select_reduce_fusion.2 = f32[4096,8]{0,1:T(8,128)S(1)} fusion(pred[8,128]{1,0:T(8,128)(4,1)S(1)} %iota_compare_fusion.2, bf16[4096,128]{1,0:T(8,128)(2,1)} %get-tuple-element.111, bf16[8,1024,128]{2,1,0:T(8,128)(2,1)S(1)} %get-tuple-element.110, s32[]{:T(128)S(6)} %copy.20), kind=kOutput, calls=%fused_computation.1.clone.1 | convolution fusion | flops 1082097664 | bytes 1442820 | tf_op jit(solution)/shard_map/while/body/eval_jaxpr/dot_general | solution.py:49
  78.9 0.2 reshape.88
  79.0 0.2 reduce_sum.33
  79.3 0.1 iota_compare_fusion.2
  79.4 3.8 %select_reduce_fusion.2 = f32[4096,8]{0,1:T(8,128)S(1)} fusion(pred[8,128]{1,0:T(8,128)(4,1)S(1)} %iota_compare_fusion.2, bf16[4096,128]{1,0:T(8,128)(2,1)} %get-tuple-element.111, bf16[8,1024,128]{2,1,0:T(8,128)(2,1)S(1)} %get-tuple-element.110, s32[]{:T(128)S(6)} %copy.20), kind=kOutput, calls=%fused_computation.1.clone.1 | convolution fusion | flops 1082097664 | bytes 1442820 | tf_op jit(solution)/shard_map/while/body/eval_jaxpr/dot_general | solution.py:49
  83.2 0.2 reshape.88
  83.3 0.2 reduce_sum.33
  83.6 0.1 iota_compare_fusion.2
  83.7 3.8 %select_reduce_fusion.2 = f32[4096,8]{0,1:T(8,128)S(1)} fusion(pred[8,128]{1,0:T(8,128)(4,1)S(1)} %iota_compare_fusion.2, bf16[4096,128]{1,0:T(8,128)(2,1)} %get-tuple-element.111, bf16[8,1024,128]{2,1,0:T(8,128)(2,1)S(1)} %get-tuple-element.110, s32[]{:T(128)S(6)} %copy.20), kind=kOutput, calls=%fused_computation.1.clone.1 | convolution fusion | flops 1082097664 | bytes 1442820 | tf_op jit(solution)/shard_map/while/body/eval_jaxpr/dot_general | solution.py:49
  87.5 0.2 reshape.88
  87.6 0.2 reduce_sum.33
  87.9 0.1 iota_compare_fusion.2
  88.0 3.8 %select_reduce_fusion.2 = f32[4096,8]{0,1:T(8,128)S(1)} fusion(pred[8,128]{1,0:T(8,128)(4,1)S(1)} %iota_compare_fusion.2, bf16[4096,128]{1,0:T(8,128)(2,1)} %get-tuple-element.111, bf16[8,1024,128]{2,1,0:T(8,128)(2,1)S(1)} %get-tuple-element.110, s32[]{:T(128)S(6)} %copy.20), kind=kOutput, calls=%fused_computation.1.clone.1 | convolution fusion | flops 1082097664 | bytes 1442820 | tf_op jit(solution)/shard_map/while/body/eval_jaxpr/dot_general | solution.py:49
  91.8 0.2 reshape.88
  91.9 0.2 reduce_sum.33
  92.2 0.1 iota_compare_fusion.2
  92.3 3.8 %select_reduce_fusion.2 = f32[4096,8]{0,1:T(8,128)S(1)} fusion(pred[8,128]{1,0:T(8,128)(4,1)S(1)} %iota_compare_fusion.2, bf16[4096,128]{1,0:T(8,128)(2,1)} %get-tuple-element.111, bf16[8,1024,128]{2,1,0:T(8,128)(2,1)S(1)} %get-tuple-element.110, s32[]{:T(128)S(6)} %copy.20), kind=kOutput, calls=%fused_computation.1.clone.1 | convolution fusion | flops 1082097664 | bytes 1442820 | tf_op jit(solution)/shard_map/while/body/eval_jaxpr/dot_general | solution.py:49
  96.1 0.2 reshape.88
  96.2 0.2 reduce_sum.33
  96.5 0.3 all_to_all.20
  96.8 0.2 copy.13
  97.0 0.7 reshape.85
  97.7 3.5 %all-to-all-start.2 = ((f32[16,1,512]{2,1,0:T(1,128)}), f32[16,1,512]{2,1,0:T(1,128)S(1)}, u32[]{:S(2)}, u32[]{:S(2)}) async-start(f32[16,1,512]{2,1,0:T(1,128)} %reshape.85), calls=%async_computation.2 | async-start | bytes 65536 | tf_op jit(solution)/shard_map/all_to_all | solution.py:78
  101.2 7.5 %all-to-all-done.2 = f32[16,1,512]{2,1,0:T(1,128)S(1)} async-done(((f32[16,1,512]{2,1,0:T(1,128)}), f32[16,1,512]{2,1,0:T(1,128)S(1)}, u32[]{:S(2)}, u32[]{:S(2)}) %all-to-all-start.2) | async-done | bytes 32800 | tf_op jit(solution)/shard_map/all_to_all | solution.py:78
  108.8 0.5 broadcast.39
  109.3 0.7 reduce.6
  110.0 0.1 reshape.86
  110.1 0.1 reduce_max.18
  110.2 0.0 copy-done.1
  110.2 0.2 fusion.8
  110.4 0.5 add_subtract_fusion
  (19 shorter events, 0.1 us)
Async XLA Ops:
  2.1 34.1 %copy-start = (bf16[8,32,128]{2,1,0:T(8,128)(2,1)S(1)}, bf16[8,32,128]{2,1,0:T(8,128)(2,1)}, u32[]{:S(2)}) copy-start(bf16[8,32,128]{2,1,0:T(8,128)(2,1)} %param.6) | copy-start | bytes 196612
  37.3 24.8 %all-to-all-start.1 = ((bf16[16,8,32,128]{3,2,1,0:T(8,128)(2,1)}), bf16[16,8,32,128]{3,2,1,0:T(8,128)(2,1)}, u32[]{:S(2)}, u32[]{:S(2)}) async-start(bf16[16,8,32,128]{3,2,1,0:T(8,128)(2,1)} %broadcast_in_dim.43), calls=%async_computation.1 | async-start | bytes 2097152 | tf_op jit(solution)/shard_map/all_to_all | solution.py:11
  62.1 48.1 %copy-start.1 = (s32[8]{0:T(128)S(1)}, s32[8]{0:T(128)}, u32[]{:S(2)}) copy-start(s32[8]{0:T(128)} %param.9) | copy-start | bytes 100
  97.7 11.1 %all-to-all-start.2 = ((f32[16,1,512]{2,1,0:T(1,128)}), f32[16,1,512]{2,1,0:T(1,128)S(1)}, u32[]{:S(2)}, u32[]{:S(2)}) async-start(f32[16,1,512]{2,1,0:T(1,128)} %reshape.85), calls=%async_computation.2 | async-start | bytes 65536 | tf_op jit(solution)/shard_map/all_to_all | solution.py:78
where the time goes:
time: 113 us; the launch traced here: 111 us
  blocking collectives  34 us (30%)
  matrix products  30.3 us (27%)
  waiting for transfers between devices  20.9 us (18%)
  local copies, waits for them, and re-layouts  10.3 us (9%)
  starting transfers between devices  10.3 us (9%)
  other arithmetic  4.66 us (4%)
    all_to_all x1, blocking collectives, copy_for_each(): lax.all_to_all(jnp.broadcast_to(x[None], (length, *x.shape)), axis, 0, 0,...  34 us
    dot_general x8, matrix products, one_group(): lax.dot_general(query_flat, block_docs, (((1,), (1,)), ((), ())), preferr...  30.3 us
    all_to_all x1, waiting for transfers between devices, copy_for_each(): lax.all_to_all(jnp.broadcast_to(x[None], (length, *x.shape)), axis, 0, 0,...  13.4 us
    all_to_all x1, waiting for transfers between devices, local(): lax.all_to_all(block_scores, 'row', split_axis=0, concat_axis=1, tiled=True)  7.54 us
    all_to_all x1, starting transfers between devices, copy_for_each(): lax.all_to_all(jnp.broadcast_to(x[None], (length, *x.shape)), axis, 0, 0,...  6.79 us
    all_to_all x1, starting transfers between devices, local(): lax.all_to_all(block_scores, 'row', split_axis=0, concat_axis=1, tiled=True)  3.5 us
    another operation x1, local copies, waits for them, and re-layouts, maxsim(): doc_rows.reshape(group_count, group_docs * slot_count, doc_rows.shape[2])  2.89 us
  transfers between devices with their start and end apart: 2, of which 2 were waited for; matrix products, arithmetic and copies ran while one was open for 4% of the time, Pallas kernels for 0%

commit v1 on v0

v1 whole, which is shorter than its diff:
```python
import functools

import jax
import jax.numpy as jnp
from jax import lax
from jax.experimental import pallas as pl
from jax.experimental.pallas import tpu as pltpu
from jax.sharding import Mesh, PartitionSpec as P

neg_fill = -1e30
QUERIES, TOKENS, DOCS, SLOTS, DIM = 8, 32, 8, 128, 128
PAY = DOCS * SLOTS + 16
ROWS = 512


def index(x, y, z, core):
    return (((y // 2 * 4 + x) * 2 + core) * 2 + y % 2) * 4 + z


def everywhere():
    return [(x, y, z, c) for x in range(4) for y in range(4) for z in range(4) for c in range(2)]


def across(dim, place):
    axis = "xyz".index(dim[0])
    moved = list(place)
    moved[axis] = place[axis] ^ 1 if dim[1] == "a" else 3 - place[axis]
    return tuple(moved)


def side(dim, place):
    at = place["xyz".index(dim[0])]
    return ((0, 1, 1, 0) if dim[1] == "a" else (0, 0, 1, 1))[at]


DOC_STEPS = (("yb", "zb"), ("zb", "yb"))
QUERY_STEPS = (("xa", "xb", "ya", "za"), ("ya", "za", "xa", "xb"))


def swap(array, steps, at):
    pairs = [(index(*p), index(*across(steps[p[3]][at], p))) for p in everywhere()]
    return lax.ppermute(array, "d", pairs)


def swap_cores(array):
    pairs = [(index(x, y, z, c), index(x, y, z, 1 - c)) for x, y, z, c in everywhere()]
    return lax.ppermute(array, "d", pairs)


def member(place):
    return sum(side(dim, place) << k for k, dim in enumerate(QUERY_STEPS[place[3]]))


def owner_groups():
    groups = {}
    for p in everywhere():
        groups.setdefault((p[3], side("yb", p), side("zb", p)), []).append(p)
    return [[index(*p) for p in sorted(g, key=member)] for g in groups.values()]


def spec(space):
    return pl.BlockSpec(memory_space=space)


def pack_kernel(place_ref, lengths_ref, docs_ref, queries_ref, doc_out, query_out, wide):
    row = lax.broadcasted_iota(jnp.int32, (SLOTS, DIM), 0)
    for d in range(DOCS):
        doc = docs_ref[d].astype(jnp.float32)
        doc = jnp.where(row < lengths_ref[d], doc, doc[:1, :])
        doc_out[d * SLOTS : (d + 1) * SLOTS, :] = doc.astype(jnp.bfloat16)
    row = lax.broadcasted_iota(jnp.int32, (16, DIM), 0)
    lane = lax.broadcasted_iota(jnp.int32, (16, DIM), 1)
    facts = jnp.zeros((16, DIM), jnp.int32) + place_ref[0]
    for d in range(DOCS):
        facts = jnp.where((row == 0) & (lane == d), lengths_ref[d], facts)
    doc_out[DOCS * SLOTS :, :] = facts.astype(jnp.float32).astype(jnp.bfloat16)
    for q in range(QUERIES):
        wide[q * TOKENS : (q + 1) * TOKENS, :] = queries_ref[q].astype(jnp.float32)
    for t in range(0, TOKENS, 2):
        pair = [wide[pl.ds(t + k, QUERIES, stride=TOKENS), :] for k in range(2)]
        query_out[t * QUERIES : (t + 2) * QUERIES, :] = jnp.concatenate(pair).astype(jnp.bfloat16)


def pack(place, lengths, docs, queries):
    return pl.pallas_call(
        pack_kernel,
        out_shape=(
            jax.ShapeDtypeStruct((PAY, DIM), jnp.bfloat16),
            jax.ShapeDtypeStruct((QUERIES * TOKENS, DIM), jnp.bfloat16),
        ),
        in_specs=[spec(pltpu.SMEM), spec(pltpu.SMEM), spec(pltpu.VMEM), spec(pltpu.VMEM)],
        out_specs=(spec(pltpu.VMEM), spec(pltpu.VMEM)),
        scratch_shapes=[pltpu.VMEM((QUERIES * TOKENS, DIM), jnp.float32)],
        name="pack",
    )(place, lengths, docs, queries)


def merge(a, b, shift, axis):
    at = lax.broadcasted_iota(jnp.int32, (8, 128), axis)
    low = (at // shift) % 2 == 0
    mine = jnp.where(low, a, b)
    other = pltpu.roll(jnp.where(low, b, a), shift, axis)
    return mine + other if axis else jnp.maximum(mine, other)


def score_kernel(sizes, blocks, facts_ref, place_ref, *refs):
    doc_refs, (query_ref, out_ref, rows, best, owner, carry, scores) = refs[: len(sizes)], refs[len(sizes) :]
    doc_count = DOCS * sum(sizes)
    groups = ROWS // 16
    total = jnp.int32(0)
    first = 0
    for size, doc_ref in zip(sizes, doc_refs):
        for p in range(size):

            def copy_doc(d, at, doc_ref=doc_ref, p=p, part=first + p):
                source = pl.multiple_of(p * PAY + d * SLOTS, 16)
                rows[pl.ds(pl.multiple_of(at * 16, 16), SLOTS), :] = doc_ref[pl.ds(source, SLOTS), :]
                for k in range(SLOTS // 16):
                    owner[at + k] = part * DOCS + d
                return at + (facts_ref[part * 16 + d] + 15) // 16

            total = lax.fori_loop(0, DOCS, copy_doc, total, unroll=True)
        first += size
    for k in range(groups):
        owner[total + k] = doc_count
    carry[...] = jnp.full_like(carry, neg_fill)

    def body(i, last):
        base = i * groups
        ids = [owner[base + g] for g in range(groups)]
        drop = [jnp.where(a == b, 0.0, neg_fill) for a, b in zip(ids, [last] + ids[:-1])]
        block_rows = rows[pl.ds(pl.multiple_of(base * 16, 16), ROWS), :]
        for b in range(blocks):
            similar = lax.dot_general(
                block_rows,
                query_ref[b * 256 : (b + 1) * 256, :],
                (((1,), (1,)), ((), ())),
                preferred_element_type=jnp.float32,
            )
            for h in range(2):
                run = carry[2 * b + h]
                for g in range(groups):
                    tile = similar[16 * g : 16 * g + 16, 128 * h : 128 * h + 128]
                    run = jnp.maximum(jnp.maximum(tile[:8], tile[8:]), run + drop[g])
                    best[2 * b + h, pl.ds(pl.multiple_of(ids[g] * 8, 8), 8), :] = run
                carry[2 * b + h] = run
        return ids[-1]

    lax.fori_loop(0, (total + groups - 1) // groups, body, jnp.int32(-1))

    def reduce(part, carried):
        columns = []
        for b in range(blocks):
            halves = []
            for h in range(2):
                v = [best[2 * b + h, pl.ds(pl.multiple_of(part * 64 + d * 8, 8), 8), :] for d in range(8)]
                for shift in (1, 2, 4):
                    v = [merge(v[2 * k], v[2 * k + 1], shift, 0) for k in range(len(v) // 2)]
                halves.append(v[0])
            columns.append(halves[0] + halves[1])
        for shift in (8, 16, 32, 64):
            columns = [merge(columns[2 * k], columns[2 * k + 1], shift, 1) for k in range(len(columns) // 2)]
        scores[pl.ds(pl.multiple_of(part * 8, 8), 8), :] = columns[0]
        ids = facts_ref[part * 16 + 8] * DOCS + lax.broadcasted_iota(jnp.int32, (8, 128), 0)
        scores[pl.ds(pl.multiple_of(doc_count + part * 8, 8), 8), :] = ids.astype(jnp.float32)
        return carried

    lax.fori_loop(0, doc_count // 8, reduce, 0, unroll=True)
    turned = scores[...].T
    for b in range(blocks):
        out_ref[b ^ place_ref[1]] = turned[b * 8 : (b + 1) * 8, :]


def score(facts, place, docs, queries):
    sizes = [d.shape[0] // PAY for d in docs]
    doc_count = DOCS * sum(sizes)
    blocks = queries.shape[0] // 256
    return pl.pallas_call(
        functools.partial(score_kernel, sizes, blocks),
        out_shape=jax.ShapeDtypeStruct((blocks, 8, 128), jnp.float32),
        in_specs=[spec(pltpu.SMEM), spec(pltpu.SMEM)] + [spec(pltpu.VMEM)] * (len(docs) + 1),
        out_specs=spec(pltpu.VMEM),
        scratch_shapes=[
            pltpu.VMEM((doc_count * SLOTS + ROWS, DIM), jnp.bfloat16),
            pltpu.VMEM((blocks * 2, (doc_count + 1) * 8, 128), jnp.float32),
            pltpu.SMEM((doc_count * 8 + ROWS // 16,), jnp.int32),
            pltpu.VMEM((blocks * 2, 8, 128), jnp.float32),
            pltpu.VMEM((2 * doc_count, 128), jnp.float32),
        ],
        compiler_params=pltpu.CompilerParams(vmem_limit_bytes=40 * 2**20),
        name="score",
    )(facts, place, *docs, queries)


def finish_kernel(positives_ref, given_ref, out_ref):
    lane = lax.broadcasted_iota(jnp.int32, (8, 128), 1)
    row = lax.broadcasted_iota(jnp.int32, (8, 128), 0)
    wanted = jnp.zeros((8, 128), jnp.int32)
    for q in range(QUERIES):
        wanted = jnp.where(row == q, positives_ref[q], wanted)
    wanted = wanted.astype(jnp.float32)
    count = given_ref.shape[0]
    given = [given_ref[k] for k in range(count)]
    real = [jnp.where(lane < 64, g, neg_fill) for g in given]
    peak = jnp.max(functools.reduce(jnp.maximum, real), axis=1, keepdims=True)
    total = jnp.sum(sum(jnp.where(lane < 64, jnp.exp(r - peak), 0.0) for r in real), axis=1, keepdims=True)
    chosen = [jnp.where((lane < 64) & (pltpu.roll(g, 64, 1) == wanted), g, 0.0) for g in given]
    loss = peak + jnp.log(total) - jnp.sum(sum(chosen), axis=1, keepdims=True)
    out_ref[...] = jnp.sum(jnp.where(row == lane, loss, 0.0), axis=0, keepdims=True)


def finish(positives, given):
    return pl.pallas_call(
        finish_kernel,
        out_shape=jax.ShapeDtypeStruct((1, 128), jnp.float32),
        in_specs=[spec(pltpu.SMEM), spec(pltpu.VMEM)],
        out_specs=spec(pltpu.VMEM),
        name="finish",
    )(positives, given)


def local(queries, documents, lengths, positives):
    here = lax.axis_index("d")
    members = [0] * 128
    for p in everywhere():
        members[index(*p)] = member(p)
    place = jnp.stack([here, jnp.asarray(members, jnp.int32)[here]])
    own, query = pack(place, lengths, documents, queries)
    for at in range(4):
        query = jnp.concatenate([query, swap(query, QUERY_STEPS, at)])
        if at == 0:
            near = swap(own, DOC_STEPS, 0)
        if at == 1:
            far = swap(jnp.concatenate([own, near]), DOC_STEPS, 1)
    docs = [own, near, far] + [swap_cores(d) for d in (own, near, far)]
    facts = jnp.stack(
        [d[k * PAY + DOCS * SLOTS : k * PAY + DOCS * SLOTS + 2, :8] for d in docs for k in range(d.shape[0] // PAY)]
    )
    facts = facts.astype(jnp.int32).reshape(-1)
    given = score(facts, place, docs, query)
    given = lax.all_to_all(given, "d", 0, 0, tiled=True, axis_index_groups=owner_groups())
    return finish(positives, given)[0, :QUERIES]


def solution(mesh):
    flat = Mesh(mesh.devices.reshape(-1), ("d",))
    placed = P("d")
    return jax.shard_map(local, mesh=flat, in_specs=(placed,) * 4, out_specs=placed, check_vma=False)
```

time: 113 us -> 66.8 us (0.59); the launches traced: 111 us -> 66.1 us
  matrix products: 30.3 us -> 0 us
  blocking collectives: 34 us -> 12.4 us
  Pallas kernels: 0 us -> 17.8 us
  local copies, waits for them, and re-layouts: 10.3 us -> 4.21 us
  waiting for transfers between devices: 20.9 us -> 15.2 us
  starting transfers between devices: 10.3 us -> 13.2 us
  other arithmetic: 4.66 us -> 3.07 us
    dot_general x8 -> x0, matrix products: 30.3 us -> none  [one_group(): lax.dot_general(query_flat, block_docs, (((1,), (1,)), ((), ())), preferr...]
    all_to_all x1, blocking collectives: 34 us -> 12.4 us  [local(): lax.all_to_all(given, 'd', 0, 0, tiled=True, axis_index_groups=owner_grou...]
    all_to_all x2 -> x0, waiting for transfers between devices: 20.9 us -> none  [the longest x1 13.4 us: copy_for_each(): lax.all_to_all(jnp.broadcast_to(x[None], (length, *x.shape)), axis, 0, 0,...]
    pallas_call x0 -> x3, Pallas kernels: none -> 17.8 us  [the longest x1 14.4 us: score(): pl.pallas_call(functools.partial(score_kernel, sizes, blocks), out_shape=...]
    ppermute x0 -> x9, waiting for transfers between devices: none -> 15.2 us  [the longest x6 15.2 us: swap(): return lax.ppermute(array, 'd', pairs)]
    ppermute x0 -> x9, starting transfers between devices: none -> 13.2 us  [the longest x6 12.6 us: swap(): return lax.ppermute(array, 'd', pairs)]
    all_to_all x2 -> x0, starting transfers between devices: 10.3 us -> none  [the longest x1 6.79 us: copy_for_each(): lax.all_to_all(jnp.broadcast_to(x[None], (length, *x.shape)), axis, 0, 0,...]
    another operation x1, local copies, waits for them, and re-layouts: 2.89 us -> 0.01 us  [local(): jnp.stack([d[k * PAY + DOCS * SLOTS:k * PAY + DOCS * SLOTS + 2, :8] for d...]
  transfers between devices with their start and end apart: 2 -> 9, of which waited for: 2 -> 5; matrix products, arithmetic and copies ran while one was open for 4% -> 5% of each run, Pallas kernels for 0% -> 0%
where the time goes in v1:
time: 66.8 us; the launch traced here: 66.1 us
  Pallas kernels  17.8 us (27%)
  waiting for transfers between devices  15.2 us (23%)
  starting transfers between devices  13.2 us (20%)
  blocking collectives  12.4 us (19%)
  local copies, waits for them, and re-layouts  4.21 us (6%)
  other arithmetic  3.07 us (5%)
    ppermute x6, waiting for transfers between devices, swap(): return lax.ppermute(array, 'd', pairs)  15.2 us
    pallas_call x1, Pallas kernels, score(): pl.pallas_call(functools.partial(score_kernel, sizes, blocks), out_shape=...  14.4 us
    ppermute x6, starting transfers between devices, swap(): return lax.ppermute(array, 'd', pairs)  12.6 us
    all_to_all x1, blocking collectives, local(): lax.all_to_all(given, 'd', 0, 0, tiled=True, axis_index_groups=owner_grou...  12.4 us
    pallas_call x1, Pallas kernels, pack(): pl.pallas_call(pack_kernel, out_shape=(jax.ShapeDtypeStruct((PAY, DIM), j...  1.77 us
    concatenate x3, other arithmetic, local(): query = jnp.concatenate([query, swap(query, QUERY_STEPS, at)])  1.74 us
    unnamed x17, local copies, waits for them, and re-layouts  1.65 us
    pallas_call x1, Pallas kernels, finish(): pl.pallas_call(finish_kernel, out_shape=jax.ShapeDtypeStruct((1, 128), jn...  1.59 us
  transfers between devices with their start and end apart: 9, of which 5 were waited for; matrix products, arithmetic and copies ran while one was open for 5% of the time, Pallas kernels for 0%

profile of v1, /device:TPU:0, one launch (start us, length us, event | category | flops | bytes accessed | tf_op | source)
XLA Modules:
  0.0 66.1 jit_solution(12488304033060761320)
XLA Ops:
  0.0 1.3 %dynamic_slice.3 = s32[1]{0:T(128)} dynamic-slice(s32[128]{0:T(128)} %constant.10.clone, s32[]{:T(128)S(6)} %select_n.3), dynamic_slice_sizes={1} | dynamic-slice | bytes 12 | tf_op jit(solution)/shard_map/dynamic_slice | solution.py:227
  1.3 1.3 %pad_add_fusion.place_ref = s32[2]{0:T(128)} fusion(s32[1]{0:T(128)} %dynamic_slice.3, s32[1]{0:T(128)} %bitcast), kind=kLoop, calls=%fused_computation.24 | loop fusion | flops 2 | bytes 16 | tf_op jit(solution)/shard_map/stack | solution.py:227
  2.5 1.8 %pack.1 = (bf16[1040,128]{1,0:T(8,128)(2,1)}, bf16[256,128]{1,0:T(8,128)(2,1)}) custom-call(s32[2]{0:T(128)} %pad_add_fusion.place_ref, s32[8]{0:T(128)} %lengths_ref.1, bf16[8,128,128]{2,1,0:T(8,128)(2,1)} %docs_ref.1, bf16[8,32,128]{2,1,0:T(8,128)(2,1)} %queries_ref.1), custom_call_target="tpu_custom_call" | custom-call | tf_op jit(solution)/shard_map/pack/pallas_call | solution.py:85
  4.3 0.0 copy-start
  4.3 3.1 %collective-permute-start = (bf16[1040,128]{1,0:T(8,128)(2,1)}, bf16[1040,128]{1,0:T(8,128)(2,1)S(1)}, u32[]{:S(2)}, u32[]{:S(2)}) collective-permute-start(bf16[1040,128]{1,0:T(8,128)(2,1)} %get-tuple-element.7.refs_0_), channel_id=1, source_target_pairs={{0,68},{8,11},{1,69},{9,10},{2,70},{10,9},{3,71},{11,8},{4,64},{12... | collective-permute-start | bytes 798728 | tf_op jit(solution)/shard_map/ppermute | solution.py:42
  7.4 0.6 collective-permute-start.2
  8.0 1.5 %collective-permute-start.5 = (bf16[256,128]{1,0:T(8,128)(2,1)}, bf16[256,128]{1,0:T(8,128)(2,1)S(1)}, u32[]{:S(2)}, u32[]{:S(2)}) collective-permute-start(bf16[256,128]{1,0:T(8,128)(2,1)} %get-tuple-element.8), channel_id=1, source_target_pairs={{0,16},{8,12},{1,17},{9,13},{2,18},{10,14},{3,19},{11,15},{4,20},{... | collective-permute-start | bytes 196616 | tf_op jit(solution)/shard_map/ppermute | solution.py:42
  9.5 0.7 %constant_dynamic-update-slice_fusion.7 = bf16[8,2,8]{2,1,0:T(2,128)(2,1)S(1)} fusion(bf16[1040,128]{1,0:T(8,128)(2,1)} %get-tuple-element.7.refs_0_), kind=kLoop, calls=%fused_computation.11 | loop fusion | bytes 544
  10.2 2.3 %collective-permute-done.5 = bf16[256,128]{1,0:T(8,128)(2,1)S(1)} collective-permute-done((bf16[256,128]{1,0:T(8,128)(2,1)}, bf16[256,128]{1,0:T(8,128)(2,1)S(1)}, u32[]{:S(2)}, u32[]{:S(2)}) %collective-permute-start.5) | collective-permute-done | bytes 65568 | tf_op jit(solution)/shard_map/ppermute | solution.py:42
  12.5 0.8 %pad_maximum_fusion.3 = bf16[512,128]{1,0:T(8,128)(2,1)S(1)} fusion(bf16[256,128]{1,0:T(8,128)(2,1)S(1)} %collective-permute-done.5, bf16[256,128]{1,0:T(8,128)(2,1)} %get-tuple-element.8), kind=kLoop, calls=%fused_computation.3 | loop fusion | flops 262144 | bytes 262144 | tf_op jit(solution)/shard_map/concatenate | solution.py:230
  13.4 0.0 copy-start.2
  13.4 2.8 %collective-permute-start.6 = (bf16[512,128]{1,0:T(8,128)(2,1)S(1)}, bf16[512,128]{1,0:T(8,128)(2,1)S(1)}, u32[]{:S(2)}, u32[]{:S(2)}) collective-permute-start(bf16[512,128]{1,0:T(8,128)(2,1)S(1)} %pad_maximum_fusion.3), channel_id=1, source_target_pairs={{0,48},{8,9},{1,49},{9,8},{2,50},{10,11},{3,51},{11,10},{4,52},{12... | collective-permute-start | bytes 393224 | tf_op jit(solution)/shard_map/ppermute | solution.py:42
  16.2 0.8 %constant_dynamic-update-slice_fusion.12 = bf16[4096,128]{1,0:T(8,128)(2,1)S(1)} fusion(bf16[256,128]{1,0:T(8,128)(2,1)} %get-tuple-element.8), kind=kLoop, calls=%fused_computation.16 | loop fusion | bytes 131072
  17.1 2.6 %collective-permute-done.6 = bf16[512,128]{1,0:T(8,128)(2,1)S(1)} collective-permute-done((bf16[512,128]{1,0:T(8,128)(2,1)S(1)}, bf16[512,128]{1,0:T(8,128)(2,1)S(1)}, u32[]{:S(2)}, u32[]{:S(2)}) %collective-permute-start.6) | collective-permute-done | bytes 131104 | tf_op jit(solution)/shard_map/ppermute | solution.py:42
  19.6 0.9 %pad_maximum_fusion.2 = bf16[1024,128]{1,0:T(8,128)(2,1)S(1)} fusion(bf16[512,128]{1,0:T(8,128)(2,1)S(1)} %collective-permute-done.6, bf16[256,128]{1,0:T(8,128)(2,1)S(1)} %collective-permute-done.5, bf16[256,128]{1,0:T(8,128)(2,1)} %get-tuple-element.8), kind=kLoop, calls=%fused_computation.2 | loop fusion | flops 786432 | bytes 524288 | tf_op jit(solution)/shard_map/concatenate | solution.py:230
  20.5 1.7 %collective-permute-start.7 = (bf16[1024,128]{1,0:T(8,128)(2,1)S(1)}, bf16[1024,128]{1,0:T(8,128)(2,1)S(1)}, u32[]{:S(2)}, u32[]{:S(2)}) collective-permute-start(bf16[1024,128]{1,0:T(8,128)(2,1)S(1)} %pad_maximum_fusion.2), channel_id=1, source_target_pairs={{0,4},{8,24},{1,5},{9,25},{2,6},{10,26},{3,7},{11,27},{4,0},{12,28... | collective-permute-start | bytes 786440 | tf_op jit(solution)/shard_map/ppermute | solution.py:42
  22.2 0.0 collective-permute-done.refs_1_
  22.2 0.0 copy-done
  22.2 2.1 %collective-permute-start.1 = (bf16[2080,128]{1,0:T(8,128)(2,1)S(1)}, bf16[2080,128]{1,0:T(8,128)(2,1)S(1)}, u32[]{:S(2)}, u32[]{:S(2)}) collective-permute-start(bf16[2080,128]{1,0:T(8,128)(2,1)S(1)} %pad_maximum_fusion), channel_id=1, source_target_pairs={{0,3},{8,76},{1,2},{9,77},{2,1},{10,78},{3,0},{11,79},{4,7},{12,72... | collective-permute-start | bytes 1597448 | tf_op jit(solution)/shard_map/ppermute | solution.py:42
  24.3 0.0 collective-permute-start.3
  24.3 2.6 %collective-permute-done.7 = bf16[1024,128]{1,0:T(8,128)(2,1)S(1)} collective-permute-done((bf16[1024,128]{1,0:T(8,128)(2,1)S(1)}, bf16[1024,128]{1,0:T(8,128)(2,1)S(1)}, u32[]{:S(2)}, u32[]{:S(2)}) %collective-permute-start.7) | collective-permute-done | bytes 262176 | tf_op jit(solution)/shard_map/ppermute | solution.py:42
  26.9 0.0 copy-done.2
  27.0 0.0 copy-start.1
  27.0 1.4 %collective-permute-start.8 = (bf16[2048,128]{1,0:T(8,128)(2,1)S(1)}, bf16[2048,128]{1,0:T(8,128)(2,1)S(1)}, u32[]{:S(2)}, u32[]{:S(2)}) collective-permute-start(bf16[2048,128]{1,0:T(8,128)(2,1)S(1)} %pad_maximum_fusion.1), channel_id=1, source_target_pairs={{0,1},{8,56},{1,0},{9,57},{2,3},{10,58},{3,2},{11,59},{4,5},{12,60... | collective-permute-start | bytes 1572872 | tf_op jit(solution)/shard_map/ppermute | solution.py:42
  28.4 4.3 %collective-permute-done.1.refs_2_ = bf16[2080,128]{1,0:T(8,128)(2,1)S(1)} collective-permute-done((bf16[2080,128]{1,0:T(8,128)(2,1)S(1)}, bf16[2080,128]{1,0:T(8,128)(2,1)S(1)}, u32[]{:S(2)}, u32[]{:S(2)}) %collective-permute-start.1) | collective-permute-done | bytes 532512 | tf_op jit(solution)/shard_map/ppermute | solution.py:42
  32.8 0.0 collective-permute-start.4
  32.8 0.0 collective-permute-done.2.refs_3_
  32.8 0.0 collective-permute-done.3.refs_4_
  32.8 3.4 %collective-permute-done.8 = bf16[2048,128]{1,0:T(8,128)(2,1)S(1)} collective-permute-done((bf16[2048,128]{1,0:T(8,128)(2,1)S(1)}, bf16[2048,128]{1,0:T(8,128)(2,1)S(1)}, u32[]{:S(2)}, u32[]{:S(2)}) %collective-permute-start.8) | collective-permute-done | bytes 524320 | tf_op jit(solution)/shard_map/ppermute | solution.py:42
  36.2 0.1 constant_dynamic-update-slice_fusion.8.refs_6_
  36.3 0.0 collective-permute-done.4.refs_5_
  36.4 0.1 reshape.4.facts_ref
  36.5 0.0 copy-done.1
  36.5 14.4 %score.1 = f32[16,8,128]{2,1,0:T(8,128)S(1)} custom-call(s32[128]{0:T(128)S(1)} %reshape.4.facts_ref, s32[2]{0:T(128)S(1)} %copy-done.1, bf16[1040,128]{1,0:T(8,128)(2,1)S(1)} %copy-done, bf16[1040,128]{1,0:T(8,128)(2,1)S(1)} %collective-permute-done.refs_1_, bf16[2080,128]{1,0:T(8,128)(2,1)S(1)} %collective-permute-done.1.refs_2_, ...), custom_call_target="tpu_custom_call" | custom-call | tf_op jit(solution)/shard_map/score/pallas_call | solution.py:178
  50.9 12.4 %all_to_all.5.given_ref = f32[16,8,128]{2,1,0:T(8,128)} all-to-all(f32[16,8,128]{2,1,0:T(8,128)S(1)} %score.1), channel_id=1, replica_groups={{0,16,48,32,4,20,52,36,1,17,49,33,5,21,53,37},{8,12,9,13,24,28,25,29,56..., dimensions={0} | all-to-all | bytes 131072 | tf_op jit(solution)/shard_map/all_to_all | solution.py:241
  63.4 1.6 %finish.1 = f32[1,128]{1,0:T(1,128)} custom-call(s32[8]{0:T(128)} %positives_ref.1, f32[16,8,128]{2,1,0:T(8,128)} %all_to_all.5.given_ref), custom_call_target="tpu_custom_call" | custom-call | tf_op jit(solution)/shard_map/finish/pallas_call | solution.py:213
  64.9 1.1 %slice_bitcast_fusion.7 = f32[8]{0:T(128)} fusion(f32[1,128]{1,0:T(1,128)} %finish.1), kind=kLoop, calls=%fused_computation.25 | loop fusion | bytes 64 | tf_op jit(solution)/shard_map/squeeze | solution.py:242
  (13 shorter events, 0.2 us)
Async XLA Ops:
  4.3 17.9 %copy-start = (bf16[1040,128]{1,0:T(8,128)(2,1)S(1)}, bf16[1040,128]{1,0:T(8,128)(2,1)}, u32[]{:S(2)}) copy-start(bf16[1040,128]{1,0:T(8,128)(2,1)} %get-tuple-element.7.refs_0_) | copy-start | bytes 798724
  4.3 17.8 %collective-permute-start = (bf16[1040,128]{1,0:T(8,128)(2,1)}, bf16[1040,128]{1,0:T(8,128)(2,1)S(1)}, u32[]{:S(2)}, u32[]{:S(2)}) collective-permute-start(bf16[1040,128]{1,0:T(8,128)(2,1)} %get-tuple-element.7.refs_0_), channel_id=1, source_target_pairs={{0,68},{8,11},{1,69},{9,10},{2,70},{10,9},{3,71},{11,8},{4,64},{12... | collective-permute-start | bytes 798728 | tf_op jit(solution)/shard_map/ppermute | solution.py:42
  7.4 25.4 %collective-permute-start.2 = (bf16[1040,128]{1,0:T(8,128)(2,1)}, bf16[1040,128]{1,0:T(8,128)(2,1)S(1)}, u32[]{:S(2)}, u32[]{:S(2)}) collective-permute-start(bf16[1040,128]{1,0:T(8,128)(2,1)} %get-tuple-element.7.refs_0_), channel_id=1, source_target_pairs={{0,8},{8,0},{1,9},{9,1},{2,10},{10,2},{3,11},{11,3},{4,12},{12,4},... | collective-permute-start | bytes 798728 | tf_op jit(solution)/shard_map/ppermute | solution.py:47
  8.0 4.5 %collective-permute-start.5 = (bf16[256,128]{1,0:T(8,128)(2,1)}, bf16[256,128]{1,0:T(8,128)(2,1)S(1)}, u32[]{:S(2)}, u32[]{:S(2)}) collective-permute-start(bf16[256,128]{1,0:T(8,128)(2,1)} %get-tuple-element.8), channel_id=1, source_target_pairs={{0,16},{8,12},{1,17},{9,13},{2,18},{10,14},{3,19},{11,15},{4,20},{... | collective-permute-start | bytes 196616 | tf_op jit(solution)/shard_map/ppermute | solution.py:42
  13.4 13.6 %copy-start.2 = (bf16[256,128]{1,0:T(8,128)(2,1)S(1)}, bf16[256,128]{1,0:T(8,128)(2,1)}, u32[]{:S(2)}) copy-start(bf16[256,128]{1,0:T(8,128)(2,1)} %get-tuple-element.8) | copy-start | bytes 196612
  13.4 6.3 %collective-permute-start.6 = (bf16[512,128]{1,0:T(8,128)(2,1)S(1)}, bf16[512,128]{1,0:T(8,128)(2,1)S(1)}, u32[]{:S(2)}, u32[]{:S(2)}) collective-permute-start(bf16[512,128]{1,0:T(8,128)(2,1)S(1)} %pad_maximum_fusion.3), channel_id=1, source_target_pairs={{0,48},{8,9},{1,49},{9,8},{2,50},{10,11},{3,51},{11,10},{4,52},{12... | collective-permute-start | bytes 393224 | tf_op jit(solution)/shard_map/ppermute | solution.py:42
  20.5 6.5 %collective-permute-start.7 = (bf16[1024,128]{1,0:T(8,128)(2,1)S(1)}, bf16[1024,128]{1,0:T(8,128)(2,1)S(1)}, u32[]{:S(2)}, u32[]{:S(2)}) collective-permute-start(bf16[1024,128]{1,0:T(8,128)(2,1)S(1)} %pad_maximum_fusion.2), channel_id=1, source_target_pairs={{0,4},{8,24},{1,5},{9,25},{2,6},{10,26},{3,7},{11,27},{4,0},{12,28... | collective-permute-start | bytes 786440 | tf_op jit(solution)/shard_map/ppermute | solution.py:42
  22.2 10.6 %collective-permute-start.1 = (bf16[2080,128]{1,0:T(8,128)(2,1)S(1)}, bf16[2080,128]{1,0:T(8,128)(2,1)S(1)}, u32[]{:S(2)}, u32[]{:S(2)}) collective-permute-start(bf16[2080,128]{1,0:T(8,128)(2,1)S(1)} %pad_maximum_fusion), channel_id=1, source_target_pairs={{0,3},{8,76},{1,2},{9,77},{2,1},{10,78},{3,0},{11,79},{4,7},{12,72... | collective-permute-start | bytes 1597448 | tf_op jit(solution)/shard_map/ppermute | solution.py:42
  24.3 8.5 %collective-permute-start.3 = (bf16[1040,128]{1,0:T(8,128)(2,1)S(1)}, bf16[1040,128]{1,0:T(8,128)(2,1)S(1)}, u32[]{:S(2)}, u32[]{:S(2)}) collective-permute-start(bf16[1040,128]{1,0:T(8,128)(2,1)S(1)} %collective-permute-done.refs_1_), channel_id=1, source_target_pairs={{0,8},{8,0},{1,9},{9,1},{2,10},{10,2},{3,11},{11,3},{4,12},{12,4},... | collective-permute-start | bytes 798728 | tf_op jit(solution)/shard_map/ppermute | solution.py:47
  27.0 9.5 %copy-start.1 = (s32[2]{0:T(128)S(1)}, s32[2]{0:T(128)}, u32[]{:S(2)}) copy-start(s32[2]{0:T(128)} %pad_add_fusion.place_ref) | copy-start | bytes 28
  27.0 9.3 %collective-permute-start.8 = (bf16[2048,128]{1,0:T(8,128)(2,1)S(1)}, bf16[2048,128]{1,0:T(8,128)(2,1)S(1)}, u32[]{:S(2)}, u32[]{:S(2)}) collective-permute-start(bf16[2048,128]{1,0:T(8,128)(2,1)S(1)} %pad_maximum_fusion.1), channel_id=1, source_target_pairs={{0,1},{8,56},{1,0},{9,57},{2,3},{10,58},{3,2},{11,59},{4,5},{12,60... | collective-permute-start | bytes 1572872 | tf_op jit(solution)/shard_map/ppermute | solution.py:42
  32.8 3.5 %collective-permute-start.4 = (bf16[2080,128]{1,0:T(8,128)(2,1)S(1)}, bf16[2080,128]{1,0:T(8,128)(2,1)S(1)}, u32[]{:S(2)}, u32[]{:S(2)}) collective-permute-start(bf16[2080,128]{1,0:T(8,128)(2,1)S(1)} %collective-permute-done.1.refs_2_), channel_id=1, source_target_pairs={{0,8},{8,0},{1,9},{9,1},{2,10},{10,2},{3,11},{11,3},{4,12},{12,4},... | collective-permute-start | bytes 1597448 | tf_op jit(solution)/shard_map/ppermute | solution.py:47

commit v2 on v1

v2 whole, which is shorter than its diff:
```python
import functools

import jax
import jax.numpy as jnp
from jax import lax
from jax.experimental import pallas as pl
from jax.experimental.pallas import tpu as pltpu
from jax.sharding import Mesh, PartitionSpec as P

neg_fill = -1e30
QUERIES, TOKENS, DOCS, SLOTS, DIM = 8, 32, 8, 128, 128
PAY = DOCS * SLOTS + 16
LARGE, SMALL = 64, 16


def index(x, y, z, core):
    return (((y // 2 * 4 + x) * 2 + core) * 2 + y % 2) * 4 + z


def everywhere():
    return [(x, y, z, c) for x in range(4) for y in range(4) for z in range(4) for c in range(2)]


def across(dim, place):
    axis = "xyz".index(dim[0])
    moved = list(place)
    moved[axis] = place[axis] ^ 1 if dim[1] == "a" else 3 - place[axis]
    return tuple(moved)


def side(dim, place):
    at = place["xyz".index(dim[0])]
    return ((0, 1, 1, 0) if dim[1] == "a" else (0, 0, 1, 1))[at]


DOC_STEPS = (("yb", "zb"), ("zb", "yb"))
QUERY_STEPS = (("xb", "xa", "ya", "za"), ("xb", "ya", "za", "xa"))


def swap(array, steps, at):
    pairs = [(index(*p), index(*across(steps[p[3]][at], p))) for p in everywhere()]
    return lax.ppermute(array, "d", pairs)


def swap_cores(array):
    pairs = [(index(x, y, z, c), index(x, y, z, 1 - c)) for x, y, z, c in everywhere()]
    return lax.ppermute(array, "d", pairs)


def member(place):
    return sum(side(dim, place) << k for k, dim in enumerate(QUERY_STEPS[place[3]]))


def owner_groups():
    groups = {}
    for p in everywhere():
        groups.setdefault((p[3], side("yb", p), side("zb", p)), []).append(p)
    return [[index(*p) for p in sorted(g, key=member)] for g in groups.values()]


def spec(space):
    return pl.BlockSpec(memory_space=space)


def pack_docs_kernel(lengths_ref, docs_ref, out_ref):
    row = lax.broadcasted_iota(jnp.int32, (SLOTS, DIM), 0)
    for d in range(DOCS):
        doc = docs_ref[d].astype(jnp.float32)
        doc = jnp.where(row < lengths_ref[d], doc, doc[:1, :])
        out_ref[d * SLOTS : (d + 1) * SLOTS, :] = doc.astype(jnp.bfloat16)
    lane = lax.broadcasted_iota(jnp.int32, (16, DIM), 1)
    facts = jnp.zeros((16, DIM), jnp.int32)
    for d in range(DOCS):
        facts = jnp.where(lane == d, lengths_ref[d], facts)
    out_ref[DOCS * SLOTS :, :] = facts.astype(jnp.float32).astype(jnp.bfloat16)


def pack_docs(lengths, docs):
    return pl.pallas_call(
        pack_docs_kernel,
        out_shape=jax.ShapeDtypeStruct((PAY, DIM), jnp.bfloat16),
        in_specs=[spec(pltpu.SMEM), spec(pltpu.VMEM)],
        out_specs=spec(pltpu.VMEM),
        cost_estimate=pl.CostEstimate(flops=10**6, bytes_accessed=10**6, transcendentals=0),
        name="pack_docs",
    )(lengths, docs)


def pack_queries_kernel(queries_ref, out_ref, wide):
    for q in range(QUERIES):
        wide[q * TOKENS : (q + 1) * TOKENS, :] = queries_ref[q].astype(jnp.float32)
    for t in range(0, TOKENS, 2):
        pair = [wide[pl.ds(t + k, QUERIES, stride=TOKENS), :] for k in range(2)]
        out_ref[t * QUERIES : (t + 2) * QUERIES, :] = jnp.concatenate(pair).astype(jnp.bfloat16)


def pack_queries(queries):
    return pl.pallas_call(
        pack_queries_kernel,
        out_shape=jax.ShapeDtypeStruct((QUERIES * TOKENS, DIM), jnp.bfloat16),
        in_specs=[spec(pltpu.VMEM)],
        out_specs=spec(pltpu.VMEM),
        scratch_shapes=[pltpu.VMEM((QUERIES * TOKENS, DIM), jnp.float32)],
        name="pack_queries",
    )(queries)


def merge(a, b, shift, axis):
    at = lax.broadcasted_iota(jnp.int32, (8, 128), axis)
    low = (at // shift) % 2 == 0
    mine = jnp.where(low, a, b)
    other = pltpu.roll(jnp.where(low, b, a), shift, axis)
    return mine + other if axis else jnp.maximum(mine, other)


def doc_sources(me):
    core = (me >> 3) & 1
    y_pair, z_pair = 68, 3
    one = jnp.where(core == 0, y_pair, z_pair)
    two = jnp.where(core == 0, z_pair, y_pair)
    both = y_pair ^ z_pair
    masks = [0, one, two, both, 8, 8 ^ two, 8 ^ one, 8 ^ both]
    return [me ^ m for m in masks]


def my_member(me):
    yh, x1, x0, core, yl, z1, z0 = [(me >> k) & 1 for k in (6, 5, 4, 3, 2, 1, 0)]
    bits = {"xb": x1, "xa": x0 ^ x1, "ya": yl ^ yh, "za": z0 ^ z1}
    places = [sum(bits[dim] << k for k, dim in enumerate(steps)) for steps in QUERY_STEPS]
    return jnp.where(core == 0, places[0], places[1])


def score_kernel(sizes, blocks, first_block, aliased, facts_ref, *refs):
    doc_refs, rest = refs[: len(sizes)], refs[len(sizes) + aliased :]
    query_ref, out_ref, rows, best, owner, carry, scores = rest
    me = lax.axis_index("d")
    doc_count = DOCS * sum(sizes)
    total = jnp.int32(0)
    first = 0
    for size, doc_ref in zip(sizes, doc_refs):
        for p in range(size):
            part = first + p
            for d in range(DOCS):
                source = p * PAY + d * SLOTS
                rows[pl.ds(pl.multiple_of(total * 16, 16), SLOTS), :] = doc_ref[source : source + SLOTS, :]
                for k in range(SLOTS // 16):
                    owner[total + k] = part * DOCS + d
                total = total + (facts_ref[part * 8 + d] + 15) // 16
        first += size
    for k in range(SMALL):
        owner[total + k] = doc_count
    carry[...] = jnp.full_like(carry, neg_fill)

    def step(groups, base, last):
        ids = [owner[base + g] for g in range(groups)]
        drop = [jnp.where(a == b, 0.0, neg_fill) for a, b in zip(ids, [last] + ids[:-1])]
        block_rows = rows[pl.ds(pl.multiple_of(base * 16, 16), groups * 16), :]
        for b in range(blocks):
            similar = lax.dot_general(
                block_rows,
                query_ref[b * 256 : (b + 1) * 256, :],
                (((1,), (1,)), ((), ())),
                preferred_element_type=jnp.float32,
            )
            for h in range(2):
                run = carry[2 * b + h]
                for g in range(groups):
                    tile = similar[16 * g : 16 * g + 16, 128 * h : 128 * h + 128]
                    run = jnp.maximum(jnp.maximum(tile[:8], tile[8:]), run + drop[g])
                    best[2 * b + h, pl.ds(pl.multiple_of(ids[g] * 8, 8), 8), :] = run
                carry[2 * b + h] = run
        return ids[-1]

    large = total // LARGE
    last = lax.fori_loop(0, large, lambda i, last: step(LARGE, i * LARGE, last), jnp.int32(-1))
    small = (total - large * LARGE + SMALL - 1) // SMALL
    lax.fori_loop(0, small, lambda i, last: step(SMALL, large * LARGE + i * SMALL, last), last)

    for part, source in enumerate(doc_sources(me)):
        columns = []
        for b in range(blocks):
            halves = []
            for h in range(2):
                v = [best[2 * b + h, (part * 8 + d) * 8 : (part * 8 + d + 1) * 8, :] for d in range(8)]
                for shift in (1, 2, 4):
                    v = [merge(v[2 * k], v[2 * k + 1], shift, 0) for k in range(len(v) // 2)]
                halves.append(v[0])
            columns.append(halves[0] + halves[1])
        for shift in (8, 16, 32, 64):
            if len(columns) > 1:
                columns = [merge(columns[2 * k], columns[2 * k + 1], shift, 1) for k in range(len(columns) // 2)]
            else:
                columns = [columns[0] + pltpu.roll(columns[0], shift, 1)]
        scores[part * 8 : part * 8 + 8, :] = columns[0]
        ids = source * DOCS + lax.broadcasted_iota(jnp.int32, (8, 128), 0)
        scores[doc_count + part * 8 : doc_count + part * 8 + 8, :] = ids.astype(jnp.float32)
    turned = scores[...].T
    at = my_member(me)
    for b in range(blocks):
        out_ref[(b + first_block) ^ at] = turned[b * 8 : (b + 1) * 8, :]


def score(facts, docs, queries, first_block, so_far=None):
    sizes = [d.shape[0] // PAY for d in docs]
    doc_count = DOCS * sum(sizes)
    blocks = queries.shape[0] // 256
    extra = [] if so_far is None else [so_far]
    return pl.pallas_call(
        functools.partial(score_kernel, sizes, blocks, first_block, len(extra)),
        out_shape=jax.ShapeDtypeStruct((16, 8, 128), jnp.float32),
        in_specs=[spec(pltpu.SMEM)]
        + [spec(pltpu.VMEM)] * len(docs)
        + [spec(pltpu.VMEM)] * len(extra)
        + [spec(pltpu.VMEM)],
        out_specs=spec(pltpu.VMEM),
        input_output_aliases={1 + len(docs): 0} if extra else {},
        scratch_shapes=[
            pltpu.VMEM((doc_count * SLOTS + SMALL * 16, DIM), jnp.bfloat16),
            pltpu.VMEM((blocks * 2, (doc_count + 1) * 8, 128), jnp.float32),
            pltpu.SMEM((doc_count * 8 + SMALL,), jnp.int32),
            pltpu.VMEM((blocks * 2, 8, 128), jnp.float32),
            pltpu.VMEM((2 * doc_count, 128), jnp.float32),
        ],
        compiler_params=pltpu.CompilerParams(vmem_limit_bytes=24 * 2**20),
        cost_estimate=pl.CostEstimate(flops=6 * 10**9, bytes_accessed=10**6, transcendentals=0),
        name="score",
    )(facts, *docs, *extra, queries)


def finish_kernel(positives_ref, given_ref, out_ref):
    lane = lax.broadcasted_iota(jnp.int32, (8, 128), 1)
    row = lax.broadcasted_iota(jnp.int32, (8, 128), 0)
    wanted = jnp.zeros((8, 128), jnp.int32)
    for q in range(QUERIES):
        wanted = jnp.where(row == q, positives_ref[q], wanted)
    wanted = wanted.astype(jnp.float32)
    count = given_ref.shape[0]
    given = [given_ref[k] for k in range(count)]
    real = [jnp.where(lane < 64, g, neg_fill) for g in given]
    peak = jnp.max(functools.reduce(jnp.maximum, real), axis=1, keepdims=True)
    total = jnp.sum(sum(jnp.where(lane < 64, jnp.exp(r - peak), 0.0) for r in real), axis=1, keepdims=True)
    chosen = [jnp.where((lane < 64) & (pltpu.roll(g, 64, 1) == wanted), g, 0.0) for g in given]
    loss = peak + jnp.log(total) - jnp.sum(sum(chosen), axis=1, keepdims=True)
    out_ref[...] = jnp.sum(jnp.where(row == lane, loss, 0.0), axis=0)[:QUERIES]


def finish(positives, given):
    return pl.pallas_call(
        finish_kernel,
        out_shape=jax.ShapeDtypeStruct((QUERIES,), jnp.float32),
        in_specs=[spec(pltpu.SMEM), spec(pltpu.VMEM)],
        out_specs=spec(pltpu.VMEM),
        name="finish",
    )(positives, given)


def local(queries, documents, lengths, positives):
    query = [pack_queries(queries)]
    own = pack_docs(lengths, documents)
    for at in range(4):
        held = query[0] if at == 0 else jnp.concatenate(query)
        query = [held, swap(held, QUERY_STEPS, at)]
        if at == 0:
            near = swap(own, DOC_STEPS, 0)
        if at == 1:
            far = swap(jnp.concatenate([own, near]), DOC_STEPS, 1)
    docs = [own, near, far] + [swap_cores(d) for d in (own, near, far)]
    facts = jnp.stack([d[(k + 1) * PAY - 16, :8] for d in docs for k in range(d.shape[0] // PAY)])
    facts = facts.astype(jnp.int32).reshape(-1)
    given = score(facts, docs, query[0], 0)
    given = score(facts, docs, query[1], 8, given)
    given = lax.all_to_all(given, "d", 0, 0, tiled=True, axis_index_groups=owner_groups())
    return finish(positives, given)


def solution(mesh):
    flat = Mesh(mesh.devices.reshape(-1), ("d",))
    placed = P("d")
    return jax.shard_map(local, mesh=flat, in_specs=(placed,) * 4, out_specs=placed, check_vma=False)
```

time: 66.8 us -> 60.1 us (0.90)
  waiting for transfers between devices: 15.2 us -> 10.2 us
  local copies, waits for them, and re-layouts: 4.21 us -> 0.14 us
  Pallas kernels: 17.8 us -> 21.1 us
  other arithmetic: 3.07 us -> 1.06 us
  blocking collectives: 12.4 us -> 14.4 us
    ppermute x6, waiting for transfers between devices: 15.2 us -> 10.2 us  [swap(): return lax.ppermute(array, 'd', pairs)]
    pallas_call x3 -> x5, Pallas kernels: 17.8 us -> 21.1 us  [the longest x2 16.2 us: score(): pl.pallas_call(functools.partial(score_kernel, sizes, blocks, first_block...]
    all_to_all x1, blocking collectives: 12.4 us -> 14.4 us  [local(): lax.all_to_all(given, 'd', 0, 0, tiled=True, axis_index_groups=owner_grou...]
    concatenate x3, other arithmetic: 1.74 us -> 0.06 us  [local(): held = query[0] if at == 0 else jnp.concatenate(query)]
    unnamed x17 -> x4, local copies, waits for them, and re-layouts: 1.65 us -> 0.01 us
    another operation x1 -> x0, other arithmetic: 1.29 us -> none  [local(): place = jnp.stack([here, jnp.asarray(members, jnp.int32)[here]])]
    dynamic_slice x1 -> x0, local copies, waits for them, and re-layouts: 1.26 us -> none  [local(): place = jnp.stack([here, jnp.asarray(members, jnp.int32)[here]])]
    squeeze x1 -> x0, local copies, waits for them, and re-layouts: 1.13 us -> none  [local(): return finish(positives, given)[0, :QUERIES]]
  transfers between devices with their start and end apart: 9 -> 9, of which waited for: 5 -> 5; matrix products, arithmetic and copies ran while one was open for 5% -> 2% of each run, Pallas kernels for 0% -> 16%
where the time goes in v2:
time: 60.1 us; the launch traced here: 59.7 us
  Pallas kernels  21.1 us (35%)
  blocking collectives  14.4 us (24%)
  starting transfers between devices  12.7 us (21%)
  waiting for transfers between devices  10.2 us (17%)
  other arithmetic  1.06 us (2%)
    pallas_call x2, Pallas kernels, score(): pl.pallas_call(functools.partial(score_kernel, sizes, blocks, first_block...  16.2 us
    all_to_all x1, blocking collectives, local(): lax.all_to_all(given, 'd', 0, 0, tiled=True, axis_index_groups=owner_grou...  14.4 us
    ppermute x6, starting transfers between devices, swap(): return lax.ppermute(array, 'd', pairs)  12.2 us
    ppermute x6, waiting for transfers between devices, swap(): return lax.ppermute(array, 'd', pairs)  10.2 us
    pallas_call x1, Pallas kernels, pack_docs(): pl.pallas_call(pack_docs_kernel, out_shape=jax.ShapeDtypeStruct((PAY, DIM...  1.73 us
    pallas_call x1, Pallas kernels, finish(): pl.pallas_call(finish_kernel, out_shape=jax.ShapeDtypeStruct((QUERIES,),...  1.57 us
    pallas_call x1, Pallas kernels, pack_queries(): pl.pallas_call(pack_queries_kernel, out_shape=jax.ShapeDtypeStruct((QUERI...  1.54 us
  transfers between devices with their start and end apart: 9, of which 5 were waited for; matrix products, arithmetic and copies ran while one was open for 2% of the time, Pallas kernels for 16%

profile of v2, /device:TPU:0, one launch (start us, length us, event | category | flops | bytes accessed | tf_op | source)
XLA Modules:
  0.0 59.7 jit_solution(7078982488621767984)
XLA Ops:
  0.0 1.7 %pack_docs.1.refs_0_ = bf16[1040,128]{1,0:T(8,128)(2,1)} custom-call(s32[8]{0:T(128)} %lengths_ref.1, bf16[8,128,128]{2,1,0:T(8,128)(2,1)} %docs_ref.1), custom_call_target="tpu_custom_call" | custom-call | flops 1000000 | bytes 1000000 | tf_op jit(solution)/shard_map/pack_docs/pallas_call | solution.py:79
  1.7 3.1 %collective-permute-start = (bf16[1040,128]{1,0:T(8,128)(2,1)}, bf16[1040,128]{1,0:T(8,128)(2,1)S(1)}, u32[]{:S(2)}, u32[]{:S(2)}) collective-permute-start(bf16[1040,128]{1,0:T(8,128)(2,1)} %pack_docs.1.refs_0_), channel_id=1, source_target_pairs={{0,68},{8,11},{1,69},{9,10},{2,70},{10,9},{3,71},{11,8},{4,64},{12... | collective-permute-start | bytes 798728 | tf_op jit(solution)/shard_map/ppermute | solution.py:42
  4.9 1.5 %pack_queries.1 = bf16[256,128]{1,0:T(8,128)(2,1)} custom-call(bf16[8,32,128]{2,1,0:T(8,128)(2,1)} %queries_ref.1), custom_call_target="tpu_custom_call" | custom-call | tf_op jit(solution)/shard_map/pack_queries/pallas_call | solution.py:98
  6.4 0.0 copy-start.1
  6.4 0.0 copy-start
  6.4 2.8 %collective-permute-start.5 = (bf16[256,128]{1,0:T(8,128)(2,1)}, bf16[256,128]{1,0:T(8,128)(2,1)S(1)}, u32[]{:S(2)}, u32[]{:S(2)}) collective-permute-start(bf16[256,128]{1,0:T(8,128)(2,1)} %pack_queries.1), channel_id=1, source_target_pairs={{0,48},{8,56},{1,49},{9,57},{2,50},{10,58},{3,51},{11,59},{4,52},{... | collective-permute-start | bytes 196616 | tf_op jit(solution)/shard_map/ppermute | solution.py:42
  9.2 0.4 collective-permute-done.refs_1_
  9.6 1.0 %pad_maximum_fusion = bf16[2080,128]{1,0:T(8,128)(2,1)S(1)} fusion(bf16[1040,128]{1,0:T(8,128)(2,1)S(1)} %collective-permute-done.refs_1_, bf16[1040,128]{1,0:T(8,128)(2,1)} %pack_docs.1.refs_0_), kind=kLoop, calls=%fused_computation | loop fusion | flops 1064960 | bytes 1064960 | tf_op jit(solution)/shard_map/concatenate | solution.py:266
  10.6 4.2 %collective-permute-start.1 = (bf16[2080,128]{1,0:T(8,128)(2,1)S(1)}, bf16[2080,128]{1,0:T(8,128)(2,1)S(1)}, u32[]{:S(2)}, u32[]{:S(2)}) collective-permute-start(bf16[2080,128]{1,0:T(8,128)(2,1)S(1)} %pad_maximum_fusion), channel_id=1, source_target_pairs={{0,3},{8,76},{1,2},{9,77},{2,1},{10,78},{3,0},{11,79},{4,7},{12,72... | collective-permute-start | bytes 1597448 | tf_op jit(solution)/shard_map/ppermute | solution.py:42
  14.8 0.0 collective-permute-done.5
  14.8 0.0 copy-done.1
  14.8 1.6 %collective-permute-start.6 = (bf16[512,128]{1,0:T(8,128)(2,1)S(1)}, bf16[512,128]{1,0:T(8,128)(2,1)S(1)}, u32[]{:S(2)}, u32[]{:S(2)}) collective-permute-start(bf16[512,128]{1,0:T(8,128)(2,1)S(1)} %pad_maximum_fusion.3), channel_id=1, source_target_pairs={{0,16},{8,12},{1,17},{9,13},{2,18},{10,14},{3,19},{11,15},{4,20},{... | collective-permute-start | bytes 393224 | tf_op jit(solution)/shard_map/ppermute | solution.py:42
  16.4 0.0 copy-done
  16.4 0.0 collective-permute-start.2
  16.4 3.5 %collective-permute-done.6 = bf16[512,128]{1,0:T(8,128)(2,1)S(1)} collective-permute-done((bf16[512,128]{1,0:T(8,128)(2,1)S(1)}, bf16[512,128]{1,0:T(8,128)(2,1)S(1)}, u32[]{:S(2)}, u32[]{:S(2)}) %collective-permute-start.6) | collective-permute-done | bytes 131104 | tf_op jit(solution)/shard_map/ppermute | solution.py:42
  19.9 0.4 collective-permute-start.7
  20.3 1.7 %collective-permute-done.1.refs_2_ = bf16[2080,128]{1,0:T(8,128)(2,1)S(1)} collective-permute-done((bf16[2080,128]{1,0:T(8,128)(2,1)S(1)}, bf16[2080,128]{1,0:T(8,128)(2,1)S(1)}, u32[]{:S(2)}, u32[]{:S(2)}) %collective-permute-start.1) | collective-permute-done | bytes 532512 | tf_op jit(solution)/shard_map/ppermute | solution.py:42
  22.0 0.0 collective-permute-start.4
  22.0 0.5 collective-permute-start.3
  22.6 0.0 collective-permute-done.2.refs_3_
  22.6 3.8 %collective-permute-done.7 = bf16[1024,128]{1,0:T(8,128)(2,1)S(1)} collective-permute-done((bf16[1024,128]{1,0:T(8,128)(2,1)S(1)}, bf16[1024,128]{1,0:T(8,128)(2,1)S(1)}, u32[]{:S(2)}, u32[]{:S(2)}) %collective-permute-start.7) | collective-permute-done | bytes 262176 | tf_op jit(solution)/shard_map/ppermute | solution.py:42
  26.4 0.1 collective-permute-start.8
  26.5 0.0 collective-permute-done.3.refs_4_
  26.5 0.0 collective-permute-done.4.refs_5_
  26.6 0.1 reshape.4.facts_ref
  26.6 8.1 %score.2.refs_6_ = f32[16,8,128]{2,1,0:T(8,128)S(1)} custom-call(s32[64]{0:T(128)S(1)} %reshape.4.facts_ref, bf16[1040,128]{1,0:T(8,128)(2,1)S(1)} %copy-done, bf16[1040,128]{1,0:T(8,128)(2,1)S(1)} %collective-permute-done.refs_1_, bf16[2080,128]{1,0:T(8,128)(2,1)S(1)} %collective-permute-done.1.refs_2_, ...), custom_call_target="tpu_custom_call" | custom-call | flops 6000000000 | bytes 1000000 | tf_op jit(solution)/shard_map/score/pallas_call | solution.py:208
  34.8 0.9 %collective-permute-done.8.refs_7_ = bf16[2048,128]{1,0:T(8,128)(2,1)S(1)} collective-permute-done((bf16[2048,128]{1,0:T(8,128)(2,1)S(1)}, bf16[2048,128]{1,0:T(8,128)(2,1)S(1)}, u32[]{:S(2)}, u32[]{:S(2)}) %collective-permute-start.8) | collective-permute-done | bytes 524320 | tf_op jit(solution)/shard_map/ppermute | solution.py:42
  35.6 8.1 %score.3 = f32[16,8,128]{2,1,0:T(8,128)S(1)} custom-call(s32[64]{0:T(128)S(1)} %reshape.4.facts_ref, bf16[1040,128]{1,0:T(8,128)(2,1)S(1)} %copy-done, bf16[1040,128]{1,0:T(8,128)(2,1)S(1)} %collective-permute-done.refs_1_, bf16[2080,128]{1,0:T(8,128)(2,1)S(1)} %collective-permute-done.1.refs_2_, ...), custom_call_target="tpu_custom_call", output_to_operand_aliasing={{}: (7, {})} | custom-call | flops 6000000000 | bytes 1000000 | tf_op jit(solution)/shard_map/score/pallas_call | solution.py:208
  43.7 14.4 %all_to_all.5.given_ref = f32[16,8,128]{2,1,0:T(8,128)} all-to-all(f32[16,8,128]{2,1,0:T(8,128)S(1)} %score.3), channel_id=1, replica_groups={{0,48,16,32,4,52,20,36,1,49,17,33,5,53,21,37},{8,56,12,60,9,57,13,61,24..., dimensions={0} | all-to-all | bytes 131072 | tf_op jit(solution)/shard_map/all_to_all | solution.py:272
  58.1 1.6 %finish.1 = f32[8]{0:T(128)} custom-call(s32[8]{0:T(128)} %positives_ref.1, f32[16,8,128]{2,1,0:T(8,128)} %all_to_all.5.given_ref), custom_call_target="tpu_custom_call" | custom-call | tf_op jit(solution)/shard_map/finish/pallas_call | solution.py:248
  (11 shorter events, 0.1 us)
Async XLA Ops:
  1.7 7.8 %collective-permute-start = (bf16[1040,128]{1,0:T(8,128)(2,1)}, bf16[1040,128]{1,0:T(8,128)(2,1)S(1)}, u32[]{:S(2)}, u32[]{:S(2)}) collective-permute-start(bf16[1040,128]{1,0:T(8,128)(2,1)} %pack_docs.1.refs_0_), channel_id=1, source_target_pairs={{0,68},{8,11},{1,69},{9,10},{2,70},{10,9},{3,71},{11,8},{4,64},{12... | collective-permute-start | bytes 798728 | tf_op jit(solution)/shard_map/ppermute | solution.py:42
  6.4 8.4 %copy-start.1 = (bf16[256,128]{1,0:T(8,128)(2,1)S(1)}, bf16[256,128]{1,0:T(8,128)(2,1)}, u32[]{:S(2)}) copy-start(bf16[256,128]{1,0:T(8,128)(2,1)} %pack_queries.1) | copy-start | bytes 196612
  6.4 10.0 %copy-start = (bf16[1040,128]{1,0:T(8,128)(2,1)S(1)}, bf16[1040,128]{1,0:T(8,128)(2,1)}, u32[]{:S(2)}) copy-start(bf16[1040,128]{1,0:T(8,128)(2,1)} %pack_docs.1.refs_0_) | copy-start | bytes 798724
  6.4 8.4 %collective-permute-start.5 = (bf16[256,128]{1,0:T(8,128)(2,1)}, bf16[256,128]{1,0:T(8,128)(2,1)S(1)}, u32[]{:S(2)}, u32[]{:S(2)}) collective-permute-start(bf16[256,128]{1,0:T(8,128)(2,1)} %pack_queries.1), channel_id=1, source_target_pairs={{0,48},{8,56},{1,49},{9,57},{2,50},{10,58},{3,51},{11,59},{4,52},{... | collective-permute-start | bytes 196616 | tf_op jit(solution)/shard_map/ppermute | solution.py:42
  10.6 11.5 %collective-permute-start.1 = (bf16[2080,128]{1,0:T(8,128)(2,1)S(1)}, bf16[2080,128]{1,0:T(8,128)(2,1)S(1)}, u32[]{:S(2)}, u32[]{:S(2)}) collective-permute-start(bf16[2080,128]{1,0:T(8,128)(2,1)S(1)} %pad_maximum_fusion), channel_id=1, source_target_pairs={{0,3},{8,76},{1,2},{9,77},{2,1},{10,78},{3,0},{11,79},{4,7},{12,72... | collective-permute-start | bytes 1597448 | tf_op jit(solution)/shard_map/ppermute | solution.py:42
  14.8 5.0 %collective-permute-start.6 = (bf16[512,128]{1,0:T(8,128)(2,1)S(1)}, bf16[512,128]{1,0:T(8,128)(2,1)S(1)}, u32[]{:S(2)}, u32[]{:S(2)}) collective-permute-start(bf16[512,128]{1,0:T(8,128)(2,1)S(1)} %pad_maximum_fusion.3), channel_id=1, source_target_pairs={{0,16},{8,12},{1,17},{9,13},{2,18},{10,14},{3,19},{11,15},{4,20},{... | collective-permute-start | bytes 393224 | tf_op jit(solution)/shard_map/ppermute | solution.py:42
  16.4 6.2 %collective-permute-start.2 = (bf16[1040,128]{1,0:T(8,128)(2,1)S(1)}, bf16[1040,128]{1,0:T(8,128)(2,1)S(1)}, u32[]{:S(2)}, u32[]{:S(2)}) collective-permute-start(bf16[1040,128]{1,0:T(8,128)(2,1)S(1)} %copy-done), channel_id=1, source_target_pairs={{0,8},{8,0},{1,9},{9,1},{2,10},{10,2},{3,11},{11,3},{4,12},{12,4},... | collective-permute-start | bytes 798728 | tf_op jit(solution)/shard_map/ppermute | solution.py:47
  19.9 6.5 %collective-permute-start.7 = (bf16[1024,128]{1,0:T(8,128)(2,1)S(1)}, bf16[1024,128]{1,0:T(8,128)(2,1)S(1)}, u32[]{:S(2)}, u32[]{:S(2)}) collective-permute-start(bf16[1024,128]{1,0:T(8,128)(2,1)S(1)} %pad_maximum_fusion.2), channel_id=1, source_target_pairs={{0,4},{8,9},{1,5},{9,8},{2,6},{10,11},{3,7},{11,10},{4,0},{12,13},... | collective-permute-start | bytes 786440 | tf_op jit(solution)/shard_map/ppermute | solution.py:42
  22.0 4.5 %collective-permute-start.4 = (bf16[2080,128]{1,0:T(8,128)(2,1)S(1)}, bf16[2080,128]{1,0:T(8,128)(2,1)S(1)}, u32[]{:S(2)}, u32[]{:S(2)}) collective-permute-start(bf16[2080,128]{1,0:T(8,128)(2,1)S(1)} %collective-permute-done.1.refs_2_), channel_id=1, source_target_pairs={{0,8},{8,0},{1,9},{9,1},{2,10},{10,2},{3,11},{11,3},{4,12},{12,4},... | collective-permute-start | bytes 1597448 | tf_op jit(solution)/shard_map/ppermute | solution.py:47
  22.0 4.4 %collective-permute-start.3 = (bf16[1040,128]{1,0:T(8,128)(2,1)S(1)}, bf16[1040,128]{1,0:T(8,128)(2,1)S(1)}, u32[]{:S(2)}, u32[]{:S(2)}) collective-permute-start(bf16[1040,128]{1,0:T(8,128)(2,1)S(1)} %collective-permute-done.refs_1_), channel_id=1, source_target_pairs={{0,8},{8,0},{1,9},{9,1},{2,10},{10,2},{3,11},{11,3},{4,12},{12,4},... | collective-permute-start | bytes 798728 | tf_op jit(solution)/shard_map/ppermute | solution.py:47
  26.4 9.3 %collective-permute-start.8 = (bf16[2048,128]{1,0:T(8,128)(2,1)S(1)}, bf16[2048,128]{1,0:T(8,128)(2,1)S(1)}, u32[]{:S(2)}, u32[]{:S(2)}) collective-permute-start(bf16[2048,128]{1,0:T(8,128)(2,1)S(1)} %pad_maximum_fusion.1.refs_6_), channel_id=1, source_target_pairs={{0,1},{8,24},{1,0},{9,25},{2,3},{10,26},{3,2},{11,27},{4,5},{12,28... | collective-permute-start | bytes 1572872 | tf_op jit(solution)/shard_map/ppermute | solution.py:42

commit v3 on v2

--- a/solution.py
+++ b/solution.py
@@ -86,31 +86,17 @@
     )(lengths, docs)
 
 
-def pack_queries_kernel(queries_ref, out_ref, wide):
-    for q in range(QUERIES):
-        wide[q * TOKENS : (q + 1) * TOKENS, :] = queries_ref[q].astype(jnp.float32)
-    for t in range(0, TOKENS, 2):
-        pair = [wide[pl.ds(t + k, QUERIES, stride=TOKENS), :] for k in range(2)]
-        out_ref[t * QUERIES : (t + 2) * QUERIES, :] = jnp.concatenate(pair).astype(jnp.bfloat16)
-
-
-def pack_queries(queries):
-    return pl.pallas_call(
-        pack_queries_kernel,
-        out_shape=jax.ShapeDtypeStruct((QUERIES * TOKENS, DIM), jnp.bfloat16),
-        in_specs=[spec(pltpu.VMEM)],
-        out_specs=spec(pltpu.VMEM),
-        scratch_shapes=[pltpu.VMEM((QUERIES * TOKENS, DIM), jnp.float32)],
-        name="pack_queries",
-    )(queries)
-
-
-def merge(a, b, shift, axis):
-    at = lax.broadcasted_iota(jnp.int32, (8, 128), axis)
-    low = (at // shift) % 2 == 0
-    mine = jnp.where(low, a, b)
-    other = pltpu.roll(jnp.where(low, b, a), shift, axis)
-    return mine + other if axis else jnp.maximum(mine, other)
+def lower_half(shift, axis):
+    return (lax.broadcasted_iota(jnp.int32, (8, 128), axis) // shift) % 2 == 0
+
+
+def merge_max(a, b, shift):
+    low = lower_half(shift, 0)
+    return jnp.maximum(jnp.where(low, a, b), pltpu.roll(jnp.where(low, b, a), shift, 0))
+
+
+def merge_sum(a, b, shift):
+    return jnp.where(lower_half(shift, 1), a + pltpu.roll(a, 128 - shift, 1), b + pltpu.roll(b, shift, 1))
 
 
 def doc_sources(me):
@@ -132,7 +118,7 @@
 
 def score_kernel(sizes, blocks, first_block, aliased, facts_ref, *refs):
     doc_refs, rest = refs[: len(sizes)], refs[len(sizes) + aliased :]
-    query_ref, out_ref, rows, best, owner, carry, scores = rest
+    query_ref, out_ref, rows, best, owner, carry, scores, turned = rest
     me = lax.axis_index("d")
     doc_count = DOCS * sum(sizes)
     total = jnp.int32(0)
@@ -145,7 +131,7 @@
                 rows[pl.ds(pl.multiple_of(total * 16, 16), SLOTS), :] = doc_ref[source : source + SLOTS, :]
                 for k in range(SLOTS // 16):
                     owner[total + k] = part * DOCS + d
-                total = total + (facts_ref[part * 8 + d] + 15) // 16
+                total = total + ((facts_ref[part * 8 + d] + 15) >> 4)
         first += size
     for k in range(SMALL):
         owner[total + k] = doc_count
@@ -171,33 +157,28 @@
                 carry[2 * b + h] = run
         return ids[-1]
 
-    large = total // LARGE
+    large = total >> 6
     last = lax.fori_loop(0, large, lambda i, last: step(LARGE, i * LARGE, last), jnp.int32(-1))
-    small = (total - large * LARGE + SMALL - 1) // SMALL
+    small = (total - large * LARGE + SMALL - 1) >> 4
     lax.fori_loop(0, small, lambda i, last: step(SMALL, large * LARGE + i * SMALL, last), last)
 
     for part, source in enumerate(doc_sources(me)):
         columns = []
-        for b in range(blocks):
-            halves = []
-            for h in range(2):
-                v = [best[2 * b + h, (part * 8 + d) * 8 : (part * 8 + d + 1) * 8, :] for d in range(8)]
-                for shift in (1, 2, 4):
-                    v = [merge(v[2 * k], v[2 * k + 1], shift, 0) for k in range(len(v) // 2)]
-                halves.append(v[0])
-            columns.append(halves[0] + halves[1])
-        for shift in (8, 16, 32, 64):
-            if len(columns) > 1:
-                columns = [merge(columns[2 * k], columns[2 * k + 1], shift, 1) for k in range(len(columns) // 2)]
-            else:
-                columns = [columns[0] + pltpu.roll(columns[0], shift, 1)]
+        for half in range(2 * blocks):
+            v = [best[half, (part * 8 + d) * 8 : (part * 8 + d + 1) * 8, :] for d in range(8)]
+            for shift in (1, 2, 4):
+                v = [merge_max(v[2 * k], v[2 * k + 1], shift) for k in range(len(v) // 2)]
+            columns.append(v[0])
+        for shift in (1, 2, 4, 8, 16):
+            columns = [merge_sum(a, b, shift) for a, b in zip(columns[::2], columns[-1:] if len(columns) == 1 else columns[1::2])]
         scores[part * 8 : part * 8 + 8, :] = columns[0]
         ids = source * DOCS + lax.broadcasted_iota(jnp.int32, (8, 128), 0)
         scores[doc_count + part * 8 : doc_count + part * 8 + 8, :] = ids.astype(jnp.float32)
-    turned = scores[...].T
+    turned[...] = scores[...].T
     at = my_member(me)
     for b in range(blocks):
-        out_ref[(b + first_block) ^ at] = turned[b * 8 : (b + 1) * 8, :]
+        quarters = [turned[pl.ds(2 * b + h, 4, stride=32), :] for h in range(2)]
+        out_ref[(b + first_block) ^ at] = jnp.concatenate(quarters)
 
 
 def score(facts, docs, queries, first_block, so_far=None):
@@ -220,6 +201,7 @@
             pltpu.SMEM((doc_count * 8 + SMALL,), jnp.int32),
             pltpu.VMEM((blocks * 2, 8, 128), jnp.float32),
             pltpu.VMEM((2 * doc_count, 128), jnp.float32),
+            pltpu.VMEM((128, 128), jnp.float32),
         ],
         compiler_params=pltpu.CompilerParams(vmem_limit_bytes=24 * 2**20),
         cost_estimate=pl.CostEstimate(flops=6 * 10**9, bytes_accessed=10**6, transcendentals=0),
@@ -255,7 +237,7 @@
 
 
 def local(queries, documents, lengths, positives):
-    query = [pack_queries(queries)]
+    query = [queries.reshape(QUERIES * TOKENS, DIM)]
     own = pack_docs(lengths, documents)
     for at in range(4):
         held = query[0] if at == 0 else jnp.concatenate(query)

time: 60.1 us -> 59.4 us (0.988)
  waiting for transfers between devices: 10.2 us -> 11.5 us
  Pallas kernels: 21.1 us -> 20.1 us
    pallas_call x1 -> x0, Pallas kernels: 1.54 us -> none  [pack_queries(): pl.pallas_call(pack_queries_kernel, out_shape=jax.ShapeDtypeStruct((QUERI...]
    ppermute x6, waiting for transfers between devices: 10.2 us -> 11.5 us  [swap(): return lax.ppermute(array, 'd', pairs)]
    pallas_call x2, Pallas kernels: 16.2 us -> 16.8 us  [score(): pl.pallas_call(functools.partial(score_kernel, sizes, blocks, first_block...]
  transfers between devices with their start and end apart: 9 -> 9, of which waited for: 5 -> 5; matrix products, arithmetic and copies ran while one was open for 2% -> 2% of each run, Pallas kernels for 16% -> 14%
where the time goes in v3:
time: 59.4 us; the launch traced here: 59.6 us
  Pallas kernels  20.1 us (34%)
  blocking collectives  13.9 us (23%)
  starting transfers between devices  12.7 us (21%)
  waiting for transfers between devices  11.5 us (19%)
  other arithmetic  1.06 us (2%)
    pallas_call x2, Pallas kernels, score(): pl.pallas_call(functools.partial(score_kernel, sizes, blocks, first_block...  16.8 us
    all_to_all x1, blocking collectives, local(): lax.all_to_all(given, 'd', 0, 0, tiled=True, axis_index_groups=owner_grou...  13.9 us
    ppermute x6, starting transfers between devices, swap(): return lax.ppermute(array, 'd', pairs)  12.2 us
    ppermute x6, waiting for transfers between devices, swap(): return lax.ppermute(array, 'd', pairs)  11.5 us
    pallas_call x1, Pallas kernels, pack_docs(): pl.pallas_call(pack_docs_kernel, out_shape=jax.ShapeDtypeStruct((PAY, DIM...  1.73 us
    pallas_call x1, Pallas kernels, finish(): pl.pallas_call(finish_kernel, out_shape=jax.ShapeDtypeStruct((QUERIES,),...  1.57 us
  transfers between devices with their start and end apart: 9, of which 5 were waited for; matrix products, arithmetic and copies ran while one was open for 2% of the time, Pallas kernels for 14%

profile of v3, /device:TPU:0, one launch (start us, length us, event | category | flops | bytes accessed | tf_op | source)
XLA Modules:
  0.0 59.6 jit_solution(17940944333224646100)
XLA Ops:
  0.0 1.7 %pack_docs.1.refs_0_ = bf16[1040,128]{1,0:T(8,128)(2,1)} custom-call(s32[8]{0:T(128)} %lengths_ref.1, bf16[8,128,128]{2,1,0:T(8,128)(2,1)} %docs_ref.1), custom_call_target="tpu_custom_call" | custom-call | flops 1000000 | bytes 1000000 | tf_op jit(solution)/shard_map/pack_docs/pallas_call | solution.py:79
  1.7 3.1 %collective-permute-start = (bf16[1040,128]{1,0:T(8,128)(2,1)}, bf16[1040,128]{1,0:T(8,128)(2,1)S(1)}, u32[]{:S(2)}, u32[]{:S(2)}) collective-permute-start(bf16[1040,128]{1,0:T(8,128)(2,1)} %pack_docs.1.refs_0_), channel_id=1, source_target_pairs={{0,68},{8,11},{1,69},{9,10},{2,70},{10,9},{3,71},{11,8},{4,64},{12... | collective-permute-start | bytes 798728 | tf_op jit(solution)/shard_map/ppermute | solution.py:42
  4.9 0.0 copy-start.1
  4.9 0.0 copy-start
  4.9 2.8 %collective-permute-start.5 = (bf16[256,128]{1,0:T(8,128)(2,1)}, bf16[256,128]{1,0:T(8,128)(2,1)S(1)}, u32[]{:S(2)}, u32[]{:S(2)}) collective-permute-start(bf16[256,128]{1,0:T(8,128)(2,1)} %bitcast.1), channel_id=1, source_target_pairs={{0,48},{8,56},{1,49},{9,57},{2,50},{10,58},{3,51},{11,59},{4,52},{... | collective-permute-start | bytes 196616 | tf_op jit(solution)/shard_map/ppermute | solution.py:42
  7.6 1.9 %collective-permute-done.refs_1_ = bf16[1040,128]{1,0:T(8,128)(2,1)S(1)} collective-permute-done((bf16[1040,128]{1,0:T(8,128)(2,1)}, bf16[1040,128]{1,0:T(8,128)(2,1)S(1)}, u32[]{:S(2)}, u32[]{:S(2)}) %collective-permute-start) | collective-permute-done | bytes 266272 | tf_op jit(solution)/shard_map/ppermute | solution.py:42
  9.6 1.0 %pad_maximum_fusion = bf16[2080,128]{1,0:T(8,128)(2,1)S(1)} fusion(bf16[1040,128]{1,0:T(8,128)(2,1)S(1)} %collective-permute-done.refs_1_, bf16[1040,128]{1,0:T(8,128)(2,1)} %pack_docs.1.refs_0_), kind=kLoop, calls=%fused_computation | loop fusion | flops 1064960 | bytes 1064960 | tf_op jit(solution)/shard_map/concatenate | solution.py:248
  10.6 4.2 %collective-permute-start.1 = (bf16[2080,128]{1,0:T(8,128)(2,1)S(1)}, bf16[2080,128]{1,0:T(8,128)(2,1)S(1)}, u32[]{:S(2)}, u32[]{:S(2)}) collective-permute-start(bf16[2080,128]{1,0:T(8,128)(2,1)S(1)} %pad_maximum_fusion), channel_id=1, source_target_pairs={{0,3},{8,76},{1,2},{9,77},{2,1},{10,78},{3,0},{11,79},{4,7},{12,72... | collective-permute-start | bytes 1597448 | tf_op jit(solution)/shard_map/ppermute | solution.py:42
  14.8 0.0 collective-permute-done.5
  14.8 0.0 copy-done.1
  14.8 1.6 %collective-permute-start.6 = (bf16[512,128]{1,0:T(8,128)(2,1)S(1)}, bf16[512,128]{1,0:T(8,128)(2,1)S(1)}, u32[]{:S(2)}, u32[]{:S(2)}) collective-permute-start(bf16[512,128]{1,0:T(8,128)(2,1)S(1)} %pad_maximum_fusion.3), channel_id=1, source_target_pairs={{0,16},{8,12},{1,17},{9,13},{2,18},{10,14},{3,19},{11,15},{4,20},{... | collective-permute-start | bytes 393224 | tf_op jit(solution)/shard_map/ppermute | solution.py:42
  16.4 0.0 copy-done
  16.4 0.0 collective-permute-start.2
  16.4 3.5 %collective-permute-done.6 = bf16[512,128]{1,0:T(8,128)(2,1)S(1)} collective-permute-done((bf16[512,128]{1,0:T(8,128)(2,1)S(1)}, bf16[512,128]{1,0:T(8,128)(2,1)S(1)}, u32[]{:S(2)}, u32[]{:S(2)}) %collective-permute-start.6) | collective-permute-done | bytes 131104 | tf_op jit(solution)/shard_map/ppermute | solution.py:42
  19.9 0.4 collective-permute-start.7
  20.3 1.7 %collective-permute-done.1.refs_2_ = bf16[2080,128]{1,0:T(8,128)(2,1)S(1)} collective-permute-done((bf16[2080,128]{1,0:T(8,128)(2,1)S(1)}, bf16[2080,128]{1,0:T(8,128)(2,1)S(1)}, u32[]{:S(2)}, u32[]{:S(2)}) %collective-permute-start.1) | collective-permute-done | bytes 532512 | tf_op jit(solution)/shard_map/ppermute | solution.py:42
  22.0 0.0 collective-permute-start.4
  22.0 0.5 collective-permute-start.3
  22.6 0.0 collective-permute-done.2.refs_3_
  22.6 3.8 %collective-permute-done.7 = bf16[1024,128]{1,0:T(8,128)(2,1)S(1)} collective-permute-done((bf16[1024,128]{1,0:T(8,128)(2,1)S(1)}, bf16[1024,128]{1,0:T(8,128)(2,1)S(1)}, u32[]{:S(2)}, u32[]{:S(2)}) %collective-permute-start.7) | collective-permute-done | bytes 262176 | tf_op jit(solution)/shard_map/ppermute | solution.py:42
  26.4 0.1 collective-permute-start.8
  26.5 0.0 collective-permute-done.3.refs_4_
  26.5 0.0 collective-permute-done.4.refs_5_
  26.6 0.1 reshape.8.facts_ref
  26.6 8.4 %score.2.refs_6_ = f32[16,8,128]{2,1,0:T(8,128)S(1)} custom-call(s32[64]{0:T(128)S(1)} %reshape.8.facts_ref, bf16[1040,128]{1,0:T(8,128)(2,1)S(1)} %copy-done, bf16[1040,128]{1,0:T(8,128)(2,1)S(1)} %collective-permute-done.refs_1_, bf16[2080,128]{1,0:T(8,128)(2,1)S(1)} %collective-permute-done.1.refs_2_, ...), custom_call_target="tpu_custom_call" | custom-call | flops 6000000000 | bytes 1000000 | tf_op jit(solution)/shard_map/score/pallas_call | solution.py:189
  35.1 0.6 collective-permute-done.8.refs_7_
  35.6 8.4 %score.3 = f32[16,8,128]{2,1,0:T(8,128)S(1)} custom-call(s32[64]{0:T(128)S(1)} %reshape.8.facts_ref, bf16[1040,128]{1,0:T(8,128)(2,1)S(1)} %copy-done, bf16[1040,128]{1,0:T(8,128)(2,1)S(1)} %collective-permute-done.refs_1_, bf16[2080,128]{1,0:T(8,128)(2,1)S(1)} %collective-permute-done.1.refs_2_, ...), custom_call_target="tpu_custom_call", output_to_operand_aliasing={{}: (7, {})} | custom-call | flops 6000000000 | bytes 1000000 | tf_op jit(solution)/shard_map/score/pallas_call | solution.py:189
  44.1 13.9 %all_to_all.5.given_ref = f32[16,8,128]{2,1,0:T(8,128)} all-to-all(f32[16,8,128]{2,1,0:T(8,128)S(1)} %score.3), channel_id=1, replica_groups={{0,48,16,32,4,52,20,36,1,49,17,33,5,53,21,37},{8,56,12,60,9,57,13,61,24..., dimensions={0} | all-to-all | bytes 131072 | tf_op jit(solution)/shard_map/all_to_all | solution.py:254
  58.0 1.6 %finish.1 = f32[8]{0:T(128)} custom-call(s32[8]{0:T(128)} %positives_ref.1, f32[16,8,128]{2,1,0:T(8,128)} %all_to_all.5.given_ref), custom_call_target="tpu_custom_call" | custom-call | tf_op jit(solution)/shard_map/finish/pallas_call | solution.py:230
  (11 shorter events, 0.1 us)
Async XLA Ops:
  1.7 7.8 %collective-permute-start = (bf16[1040,128]{1,0:T(8,128)(2,1)}, bf16[1040,128]{1,0:T(8,128)(2,1)S(1)}, u32[]{:S(2)}, u32[]{:S(2)}) collective-permute-start(bf16[1040,128]{1,0:T(8,128)(2,1)} %pack_docs.1.refs_0_), channel_id=1, source_target_pairs={{0,68},{8,11},{1,69},{9,10},{2,70},{10,9},{3,71},{11,8},{4,64},{12... | collective-permute-start | bytes 798728 | tf_op jit(solution)/shard_map/ppermute | solution.py:42
  4.9 9.9 %copy-start.1 = (bf16[8,32,128]{2,1,0:T(8,128)(2,1)S(1)}, bf16[8,32,128]{2,1,0:T(8,128)(2,1)}, u32[]{:S(2)}) copy-start(bf16[8,32,128]{2,1,0:T(8,128)(2,1)} %param.4) | copy-start | bytes 196612
  4.9 11.5 %copy-start = (bf16[1040,128]{1,0:T(8,128)(2,1)S(1)}, bf16[1040,128]{1,0:T(8,128)(2,1)}, u32[]{:S(2)}) copy-start(bf16[1040,128]{1,0:T(8,128)(2,1)} %pack_docs.1.refs_0_) | copy-start | bytes 798724
  4.9 9.9 %collective-permute-start.5 = (bf16[256,128]{1,0:T(8,128)(2,1)}, bf16[256,128]{1,0:T(8,128)(2,1)S(1)}, u32[]{:S(2)}, u32[]{:S(2)}) collective-permute-start(bf16[256,128]{1,0:T(8,128)(2,1)} %bitcast.1), channel_id=1, source_target_pairs={{0,48},{8,56},{1,49},{9,57},{2,50},{10,58},{3,51},{11,59},{4,52},{... | collective-permute-start | bytes 196616 | tf_op jit(solution)/shard_map/ppermute | solution.py:42
  10.6 11.5 %collective-permute-start.1 = (bf16[2080,128]{1,0:T(8,128)(2,1)S(1)}, bf16[2080,128]{1,0:T(8,128)(2,1)S(1)}, u32[]{:S(2)}, u32[]{:S(2)}) collective-permute-start(bf16[2080,128]{1,0:T(8,128)(2,1)S(1)} %pad_maximum_fusion), channel_id=1, source_target_pairs={{0,3},{8,76},{1,2},{9,77},{2,1},{10,78},{3,0},{11,79},{4,7},{12,72... | collective-permute-start | bytes 1597448 | tf_op jit(solution)/shard_map/ppermute | solution.py:42
  14.8 5.0 %collective-permute-start.6 = (bf16[512,128]{1,0:T(8,128)(2,1)S(1)}, bf16[512,128]{1,0:T(8,128)(2,1)S(1)}, u32[]{:S(2)}, u32[]{:S(2)}) collective-permute-start(bf16[512,128]{1,0:T(8,128)(2,1)S(1)} %pad_maximum_fusion.3), channel_id=1, source_target_pairs={{0,16},{8,12},{1,17},{9,13},{2,18},{10,14},{3,19},{11,15},{4,20},{... | collective-permute-start | bytes 393224 | tf_op jit(solution)/shard_map/ppermute | solution.py:42
  16.4 6.2 %collective-permute-start.2 = (bf16[1040,128]{1,0:T(8,128)(2,1)S(1)}, bf16[1040,128]{1,0:T(8,128)(2,1)S(1)}, u32[]{:S(2)}, u32[]{:S(2)}) collective-permute-start(bf16[1040,128]{1,0:T(8,128)(2,1)S(1)} %copy-done), channel_id=1, source_target_pairs={{0,8},{8,0},{1,9},{9,1},{2,10},{10,2},{3,11},{11,3},{4,12},{12,4},... | collective-permute-start | bytes 798728 | tf_op jit(solution)/shard_map/ppermute | solution.py:47
  19.9 6.5 %collective-permute-start.7 = (bf16[1024,128]{1,0:T(8,128)(2,1)S(1)}, bf16[1024,128]{1,0:T(8,128)(2,1)S(1)}, u32[]{:S(2)}, u32[]{:S(2)}) collective-permute-start(bf16[1024,128]{1,0:T(8,128)(2,1)S(1)} %pad_maximum_fusion.2), channel_id=1, source_target_pairs={{0,4},{8,9},{1,5},{9,8},{2,6},{10,11},{3,7},{11,10},{4,0},{12,13},... | collective-permute-start | bytes 786440 | tf_op jit(solution)/shard_map/ppermute | solution.py:42
  22.0 4.5 %collective-permute-start.4 = (bf16[2080,128]{1,0:T(8,128)(2,1)S(1)}, bf16[2080,128]{1,0:T(8,128)(2,1)S(1)}, u32[]{:S(2)}, u32[]{:S(2)}) collective-permute-start(bf16[2080,128]{1,0:T(8,128)(2,1)S(1)} %collective-permute-done.1.refs_2_), channel_id=1, source_target_pairs={{0,8},{8,0},{1,9},{9,1},{2,10},{10,2},{3,11},{11,3},{4,12},{12,4},... | collective-permute-start | bytes 1597448 | tf_op jit(solution)/shard_map/ppermute | solution.py:47
  22.0 4.4 %collective-permute-start.3 = (bf16[1040,128]{1,0:T(8,128)(2,1)S(1)}, bf16[1040,128]{1,0:T(8,128)(2,1)S(1)}, u32[]{:S(2)}, u32[]{:S(2)}) collective-permute-start(bf16[1040,128]{1,0:T(8,128)(2,1)S(1)} %collective-permute-done.refs_1_), channel_id=1, source_target_pairs={{0,8},{8,0},{1,9},{9,1},{2,10},{10,2},{3,11},{11,3},{4,12},{12,4},... | collective-permute-start | bytes 798728 | tf_op jit(solution)/shard_map/ppermute | solution.py:47
  26.4 9.3 %collective-permute-start.8 = (bf16[2048,128]{1,0:T(8,128)(2,1)S(1)}, bf16[2048,128]{1,0:T(8,128)(2,1)S(1)}, u32[]{:S(2)}, u32[]{:S(2)}) collective-permute-start(bf16[2048,128]{1,0:T(8,128)(2,1)S(1)} %pad_maximum_fusion.1.refs_6_), channel_id=1, source_target_pairs={{0,1},{8,24},{1,0},{9,25},{2,3},{10,26},{3,2},{11,27},{4,5},{12,28... | collective-permute-start | bytes 1572872 | tf_op jit(solution)/shard_map/ppermute | solution.py:42

commit v4 on v3

--- a/solution.py
+++ b/solution.py
@@ -33,8 +33,8 @@
     return ((0, 1, 1, 0) if dim[1] == "a" else (0, 0, 1, 1))[at]
 
 
-DOC_STEPS = (("yb", "zb"), ("zb", "yb"))
-QUERY_STEPS = (("xb", "xa", "ya", "za"), ("xb", "ya", "za", "xa"))
+DOC_STEPS = (("xb", "yb", "zb"), ("yb", "zb", "xb"))
+QUERY_STEPS = (("xa", "ya", "za"), ("ya", "za", "xa"))
 
 
 def swap(array, steps, at):
@@ -51,10 +51,14 @@
     return sum(side(dim, place) << k for k, dim in enumerate(QUERY_STEPS[place[3]]))
 
 
+def member(place):
+    return place[3] * 8 + sum(side(dim, place) << k for k, dim in enumerate(QUERY_STEPS[0]))
+
+
 def owner_groups():
     groups = {}
     for p in everywhere():
-        groups.setdefault((p[3], side("yb", p), side("zb", p)), []).append(p)
+        groups.setdefault(tuple(side(dim, p) for dim in DOC_STEPS[0]), []).append(p)
     return [[index(*p) for p in sorted(g, key=member)] for g in groups.values()]
 
 
@@ -78,7 +82,7 @@
 def pack_docs(lengths, docs):
     return pl.pallas_call(
         pack_docs_kernel,
-        out_shape=jax.ShapeDtypeStruct((PAY, DIM), jnp.bfloat16),
+        out_shape=pltpu.VMEM((PAY, DIM), jnp.bfloat16),
         in_specs=[spec(pltpu.SMEM), spec(pltpu.VMEM)],
         out_specs=spec(pltpu.VMEM),
         cost_estimate=pl.CostEstimate(flops=10**6, bytes_accessed=10**6, transcendentals=0),
@@ -100,26 +104,30 @@
 
 
 def doc_sources(me):
-    core = (me >> 3) & 1
-    y_pair, z_pair = 68, 3
-    one = jnp.where(core == 0, y_pair, z_pair)
-    two = jnp.where(core == 0, z_pair, y_pair)
-    both = y_pair ^ z_pair
-    masks = [0, one, two, both, 8, 8 ^ two, 8 ^ one, 8 ^ both]
-    return [me ^ m for m in masks]
-
-
-def my_member(me):
+    flips = {"xb": 48, "yb": 68, "zb": 3}
+    first, second, third = (
+        jnp.where((me >> 3) & 1 == 0, flips[a], flips[b]) for a, b in zip(DOC_STEPS[0], DOC_STEPS[1])
+    )
+    masks = [0, first, second, first ^ second]
+    return [me ^ m for m in masks] + [me ^ third ^ m for m in masks]
+
+
+def block_member(me, block):
     yh, x1, x0, core, yl, z1, z0 = [(me >> k) & 1 for k in (6, 5, 4, 3, 2, 1, 0)]
-    bits = {"xb": x1, "xa": x0 ^ x1, "ya": yl ^ yh, "za": z0 ^ z1}
-    places = [sum(bits[dim] << k for k, dim in enumerate(steps)) for steps in QUERY_STEPS]
-    return jnp.where(core == 0, places[0], places[1])
-
-
-def score_kernel(sizes, blocks, first_block, aliased, facts_ref, *refs):
-    doc_refs, rest = refs[: len(sizes)], refs[len(sizes) + aliased :]
-    query_ref, out_ref, rows, best, owner, carry, scores, turned = rest
-    me = lax.axis_index("d")
+    mine = (x0 ^ x1) | (yl ^ yh) << 1 | (z0 ^ z1) << 2
+    flips = []
+    for steps in QUERY_STEPS:
+        flips.append(sum(((block >> k) & 1) << QUERY_STEPS[0].index(dim) for k, dim in enumerate(steps)))
+    other = block >> 3
+    return ((core ^ other) << 3) | (mine ^ jnp.where(core == other, flips[0], flips[1]))
+
+
+def score_kernel(sizes, blocks, final, facts_ref, *refs):
+    doc_refs, rest = refs[: len(sizes)], refs[len(sizes) :]
+    query_ref, rest = rest[0], rest[1:]
+    if final:
+        earlier_ref, rest = rest[0], rest[1:]
+    out_ref, rows, best, owner, carry = rest[:5]
     doc_count = DOCS * sum(sizes)
     total = jnp.int32(0)
     first = 0
@@ -162,7 +170,7 @@
     small = (total - large * LARGE + SMALL - 1) >> 4
     lax.fori_loop(0, small, lambda i, last: step(SMALL, large * LARGE + i * SMALL, last), last)
 
-    for part, source in enumerate(doc_sources(me)):
+    for part in range(sum(sizes)):
         columns = []
         for half in range(2 * blocks):
             v = [best[half, (part * 8 + d) * 8 : (part * 8 + d + 1) * 8, :] for d in range(8)]
@@ -170,43 +178,51 @@
                 v = [merge_max(v[2 * k], v[2 * k + 1], shift) for k in range(len(v) // 2)]
             columns.append(v[0])
         for shift in (1, 2, 4, 8, 16):
-            columns = [merge_sum(a, b, shift) for a, b in zip(columns[::2], columns[-1:] if len(columns) == 1 else columns[1::2])]
-        scores[part * 8 : part * 8 + 8, :] = columns[0]
-        ids = source * DOCS + lax.broadcasted_iota(jnp.int32, (8, 128), 0)
-        scores[doc_count + part * 8 : doc_count + part * 8 + 8, :] = ids.astype(jnp.float32)
-    turned[...] = scores[...].T
-    at = my_member(me)
-    for b in range(blocks):
-        quarters = [turned[pl.ds(2 * b + h, 4, stride=32), :] for h in range(2)]
-        out_ref[(b + first_block) ^ at] = jnp.concatenate(quarters)
-
-
-def score(facts, docs, queries, first_block, so_far=None):
+            columns = [merge_sum(columns[2 * k], columns[2 * k + 1], shift) for k in range(len(columns) // 2)]
+        if final:
+            rest[5][doc_count + part * 8 : doc_count + part * 8 + 8, :] = columns[0]
+        else:
+            out_ref[part * 8 : part * 8 + 8, :] = columns[0]
+    if final:
+        scores, turned = rest[5:]
+        me = lax.axis_index("d")
+        scores[:doc_count, :] = earlier_ref[...]
+        for part, source in enumerate(doc_sources(me)):
+            ids = source * DOCS + lax.broadcasted_iota(jnp.int32, (8, 128), 0)
+            scores[64 + part * 8 : 64 + part * 8 + 8, :] = ids.astype(jnp.float32)
+        turned[...] = scores[...].T
+        for b in range(blocks):
+            quarters = [turned[pl.ds(2 * b + h, 4, stride=32), :] for h in range(2)]
+            out_ref[block_member(me, b)] = jnp.concatenate(quarters)
+
+
+def score(facts, docs, queries, earlier=None):
     sizes = [d.shape[0] // PAY for d in docs]
     doc_count = DOCS * sum(sizes)
     blocks = queries.shape[0] // 256
-    extra = [] if so_far is None else [so_far]
+    final = earlier is not None
+    operands = [*docs, queries] + ([earlier] if final else [])
     return pl.pallas_call(
-        functools.partial(score_kernel, sizes, blocks, first_block, len(extra)),
-        out_shape=jax.ShapeDtypeStruct((16, 8, 128), jnp.float32),
-        in_specs=[spec(pltpu.SMEM)]
-        + [spec(pltpu.VMEM)] * len(docs)
-        + [spec(pltpu.VMEM)] * len(extra)
-        + [spec(pltpu.VMEM)],
+        functools.partial(score_kernel, sizes, blocks, final),
+        out_shape=pltpu.VMEM((16, 8, 128) if final else (doc_count, 128), jnp.float32),
+        in_specs=[spec(pltpu.SMEM)] + [spec(pltpu.VMEM)] * len(operands),
         out_specs=spec(pltpu.VMEM),
-        input_output_aliases={1 + len(docs): 0} if extra else {},
         scratch_shapes=[
             pltpu.VMEM((doc_count * SLOTS + SMALL * 16, DIM), jnp.bfloat16),
             pltpu.VMEM((blocks * 2, (doc_count + 1) * 8, 128), jnp.float32),
             pltpu.SMEM((doc_count * 8 + SMALL,), jnp.int32),
             pltpu.VMEM((blocks * 2, 8, 128), jnp.float32),
-            pltpu.VMEM((2 * doc_count, 128), jnp.float32),
-            pltpu.VMEM((128, 128), jnp.float32),
-        ],
+        ]
+        + ([pltpu.VMEM((128, 128), jnp.float32)] * 2 if final else []),
         compiler_params=pltpu.CompilerParams(vmem_limit_bytes=24 * 2**20),
         cost_estimate=pl.CostEstimate(flops=6 * 10**9, bytes_accessed=10**6, transcendentals=0),
         name="score",
-    )(facts, *docs, *extra, queries)
+    )(facts, *operands)
+
+
+def lengths_of(docs):
+    facts = [d[(k + 1) * PAY - 16, :DOCS] for d in docs for k in range(d.shape[0] // PAY)]
+    return jnp.stack(facts).astype(jnp.int32).reshape(-1)
 
 
 def finish_kernel(positives_ref, given_ref, out_ref):
@@ -237,20 +253,17 @@
 
 
 def local(queries, documents, lengths, positives):
-    query = [queries.reshape(QUERIES * TOKENS, DIM)]
     own = pack_docs(lengths, documents)
-    for at in range(4):
-        held = query[0] if at == 0 else jnp.concatenate(query)
-        query = [held, swap(held, QUERY_STEPS, at)]
-        if at == 0:
-            near = swap(own, DOC_STEPS, 0)
-        if at == 1:
-            far = swap(jnp.concatenate([own, near]), DOC_STEPS, 1)
-    docs = [own, near, far] + [swap_cores(d) for d in (own, near, far)]
-    facts = jnp.stack([d[(k + 1) * PAY - 16, :8] for d in docs for k in range(d.shape[0] // PAY)])
-    facts = facts.astype(jnp.int32).reshape(-1)
-    given = score(facts, docs, query[0], 0)
-    given = score(facts, docs, query[1], 8, given)
+    query = queries.reshape(QUERIES * TOKENS, DIM)
+    near = swap(own, DOC_STEPS, 0)
+    for at in range(3):
+        query = jnp.concatenate([query, swap(query, QUERY_STEPS, at)])
+    query = jnp.concatenate([query, swap_cores(query)])
+    both = jnp.concatenate([own, near])
+    far = swap(both, DOC_STEPS, 1)
+    docs = [both, far], [swap(both, DOC_STEPS, 2), swap(far, DOC_STEPS, 2)]
+    given = score(lengths_of(docs[0]), docs[0], query)
+    given = score(lengths_of(docs[1]), docs[1], query, given)
     given = lax.all_to_all(given, "d", 0, 0, tiled=True, axis_index_groups=owner_groups())
     return finish(positives, given)
 

time: 59.4 us -> 56.9 us (0.958)
  blocking collectives: 13.9 us -> 8.9 us
  waiting for transfers between devices: 11.5 us -> 7.5 us
  starting transfers between devices: 12.7 us -> 15.7 us
  local copies, waits for them, and re-layouts: 0.14 us -> 2.28 us
  other arithmetic: 1.06 us -> 2.59 us
    all_to_all x1, blocking collectives: 13.9 us -> 8.9 us  [local(): lax.all_to_all(given, 'd', 0, 0, tiled=True, axis_index_groups=owner_grou...]
    ppermute x6 -> x7, waiting for transfers between devices: 11.5 us -> 7.5 us  [swap(): return lax.ppermute(array, 'd', pairs)]
    ppermute x6 -> x7, starting transfers between devices: 12.2 us -> 15.7 us  [swap(): return lax.ppermute(array, 'd', pairs)]
    concatenate x4, other arithmetic: 1.05 us -> 2.57 us  [the longest x3 2.53 us: local(): query = jnp.concatenate([query, swap(query, QUERY_STEPS, at)])]
    concatenate x0 -> x1, local copies, waits for them, and re-layouts: none -> 1.11 us  [local(): query = jnp.concatenate([query, swap_cores(query)])]
    unnamed x4 -> x6, local copies, waits for them, and re-layouts: 0.01 us -> 0.99 us
  transfers between devices with their start and end apart: 9 -> 8, of which waited for: 5 -> 3; matrix products, arithmetic and copies ran while one was open for 2% -> 8% of each run, Pallas kernels for 14% -> 17%
where the time goes in v4:
time: 56.9 us; the launch traced here: 56.7 us
  Pallas kernels  19.7 us (35%)
  starting transfers between devices  15.7 us (28%)
  blocking collectives  8.9 us (16%)
  waiting for transfers between devices  7.5 us (13%)
  other arithmetic  2.59 us (5%)
  local copies, waits for them, and re-layouts  2.28 us (4%)
    pallas_call x2, Pallas kernels, score(): pl.pallas_call(functools.partial(score_kernel, sizes, blocks, final), out...  17.1 us
    ppermute x7, starting transfers between devices, swap(): return lax.ppermute(array, 'd', pairs)  15.7 us
    all_to_all x1, blocking collectives, local(): lax.all_to_all(given, 'd', 0, 0, tiled=True, axis_index_groups=owner_grou...  8.9 us
    ppermute x7, waiting for transfers between devices, swap(): return lax.ppermute(array, 'd', pairs)  7.5 us
    concatenate x3, other arithmetic, local(): query = jnp.concatenate([query, swap(query, QUERY_STEPS, at)])  2.53 us
    pallas_call x1, Pallas kernels, finish(): pl.pallas_call(finish_kernel, out_shape=jax.ShapeDtypeStruct((QUERIES,),...  1.57 us
  transfers between devices with their start and end apart: 8, of which 3 were waited for; matrix products, arithmetic and copies ran while one was open for 8% of the time, Pallas kernels for 17%

profile of v4, /device:TPU:0, one launch (start us, length us, event | category | flops | bytes accessed | tf_op | source)
XLA Modules:
  0.0 56.7 jit_solution(7668357970225107708)
XLA Ops:
  0.0 1.6 %collective-permute-start.4 = (bf16[256,128]{1,0:T(8,128)(2,1)}, bf16[256,128]{1,0:T(8,128)(2,1)S(1)}, u32[]{:S(2)}, u32[]{:S(2)}) collective-permute-start(bf16[256,128]{1,0:T(8,128)(2,1)} %bitcast.1), channel_id=1, source_target_pairs={{0,16},{8,12},{1,17},{9,13},{2,18},{10,14},{3,19},{11,15},{4,20},{... | collective-permute-start | bytes 196616 | tf_op jit(solution)/shard_map/ppermute | solution.py:42
  1.6 1.0 %pack_docs.1 = bf16[1040,128]{1,0:T(8,128)(2,1)S(1)} custom-call(s32[8]{0:T(128)} %lengths_ref.1, bf16[8,128,128]{2,1,0:T(8,128)(2,1)} %docs_ref.1), custom_call_target="tpu_custom_call" | custom-call | flops 1000000 | bytes 1000000 | tf_op jit(solution)/shard_map/pack_docs/pallas_call | solution.py:83
  2.6 2.2 %collective-permute-start = (bf16[1040,128]{1,0:T(8,128)(2,1)S(1)}, bf16[1040,128]{1,0:T(8,128)(2,1)S(1)}, u32[]{:S(2)}, u32[]{:S(2)}) collective-permute-start(bf16[1040,128]{1,0:T(8,128)(2,1)S(1)} %pack_docs.1), channel_id=1, source_target_pairs={{0,48},{8,76},{1,49},{9,77},{2,50},{10,78},{3,51},{11,79},{4,52},{... | collective-permute-start | bytes 798728 | tf_op jit(solution)/shard_map/ppermute | solution.py:42
  4.8 0.0 collective-permute-done.4
  4.8 0.8 %pad_maximum_fusion.3 = bf16[512,128]{1,0:T(8,128)(2,1)S(1)} fusion(bf16[256,128]{1,0:T(8,128)(2,1)S(1)} %collective-permute-done.4, bf16[256,128]{1,0:T(8,128)(2,1)} %bitcast.2), kind=kLoop, calls=%fused_computation.3 | loop fusion | flops 262144 | bytes 262144 | tf_op jit(solution)/shard_map/concatenate | solution.py:260
  5.7 1.7 %collective-permute-start.5 = (bf16[512,128]{1,0:T(8,128)(2,1)S(1)}, bf16[512,128]{1,0:T(8,128)(2,1)S(1)}, u32[]{:S(2)}, u32[]{:S(2)}) collective-permute-start(bf16[512,128]{1,0:T(8,128)(2,1)S(1)} %pad_maximum_fusion.3), channel_id=1, source_target_pairs={{0,4},{8,9},{1,5},{9,8},{2,6},{10,11},{3,7},{11,10},{4,0},{12,13},... | collective-permute-start | bytes 393224 | tf_op jit(solution)/shard_map/ppermute | solution.py:42
  7.3 0.0 copy-start
  7.3 0.9 %constant_dynamic-update-slice_fusion.4 = bf16[4096,128]{1,0:T(8,128)(2,1)S(1)} fusion(bf16[256,128]{1,0:T(8,128)(2,1)} %bitcast.3), kind=kLoop, calls=%fused_computation.8 | loop fusion | bytes 131072
  8.2 2.5 %collective-permute-done.5 = bf16[512,128]{1,0:T(8,128)(2,1)S(1)} collective-permute-done((bf16[512,128]{1,0:T(8,128)(2,1)S(1)}, bf16[512,128]{1,0:T(8,128)(2,1)S(1)}, u32[]{:S(2)}, u32[]{:S(2)}) %collective-permute-start.5) | collective-permute-done | bytes 131104 | tf_op jit(solution)/shard_map/ppermute | solution.py:42
  10.7 0.9 %pad_maximum_fusion.2 = bf16[1024,128]{1,0:T(8,128)(2,1)S(1)} fusion(bf16[512,128]{1,0:T(8,128)(2,1)S(1)} %collective-permute-done.5, bf16[256,128]{1,0:T(8,128)(2,1)S(1)} %collective-permute-done.4, bf16[256,128]{1,0:T(8,128)(2,1)} %bitcast.4), kind=kLoop, calls=%fused_computation.2 | loop fusion | flops 786432 | bytes 524288 | tf_op jit(solution)/shard_map/concatenate | solution.py:260
  11.6 2.0 %collective-permute-start.6 = (bf16[1024,128]{1,0:T(8,128)(2,1)S(1)}, bf16[1024,128]{1,0:T(8,128)(2,1)S(1)}, u32[]{:S(2)}, u32[]{:S(2)}) collective-permute-start(bf16[1024,128]{1,0:T(8,128)(2,1)S(1)} %pad_maximum_fusion.2), channel_id=1, source_target_pairs={{0,1},{8,24},{1,0},{9,25},{2,3},{10,26},{3,2},{11,27},{4,5},{12,28... | collective-permute-start | bytes 786440 | tf_op jit(solution)/shard_map/ppermute | solution.py:42
  13.6 0.0 collective-permute-done
  13.6 3.1 %collective-permute-start.2 = (bf16[2080,128]{1,0:T(8,128)(2,1)S(1)}, bf16[2080,128]{1,0:T(8,128)(2,1)S(1)}, u32[]{:S(2)}, u32[]{:S(2)}) collective-permute-start(bf16[2080,128]{1,0:T(8,128)(2,1)S(1)} %pad_maximum_fusion.refs_0_), channel_id=1, source_target_pairs={{0,68},{8,11},{1,69},{9,10},{2,70},{10,9},{3,71},{11,8},{4,64},{12... | collective-permute-start | bytes 1597448 | tf_op jit(solution)/shard_map/ppermute | solution.py:42
  16.8 2.6 %collective-permute-start.1 = (bf16[2080,128]{1,0:T(8,128)(2,1)S(1)}, bf16[2080,128]{1,0:T(8,128)(2,1)S(1)}, u32[]{:S(2)}, u32[]{:S(2)}) collective-permute-start(bf16[2080,128]{1,0:T(8,128)(2,1)S(1)} %pad_maximum_fusion.refs_0_), channel_id=1, source_target_pairs={{0,3},{8,56},{1,2},{9,57},{2,1},{10,58},{3,0},{11,59},{4,7},{12,60... | collective-permute-start | bytes 1597448 | tf_op jit(solution)/shard_map/ppermute | solution.py:42
  19.4 0.0 collective-permute-done.6
  19.4 0.0 copy-done
  19.4 0.8 %pad_maximum_fusion.1 = bf16[2048,128]{1,0:T(8,128)(2,1)} fusion(bf16[1024,128]{1,0:T(8,128)(2,1)S(1)} %collective-permute-done.6, bf16[512,128]{1,0:T(8,128)(2,1)S(1)} %collective-permute-done.5, bf16[256,128]{1,0:T(8,128)(2,1)S(1)} %collective-permute-done.4, bf16[256,128]{1,0:T(8,128)(2,1)S(1)} %bitcast.5), kind=kLoop, calls=%fused_computation.1 | loop fusion | flops 2097152 | bytes 1048576 | tf_op jit(solution)/shard_map/concatenate | solution.py:260
  20.2 0.0 collective-permute-start.7
  20.2 3.9 %collective-permute-done.2.refs_1_ = bf16[2080,128]{1,0:T(8,128)(2,1)S(1)} collective-permute-done((bf16[2080,128]{1,0:T(8,128)(2,1)S(1)}, bf16[2080,128]{1,0:T(8,128)(2,1)S(1)}, u32[]{:S(2)}, u32[]{:S(2)}) %collective-permute-start.2) | collective-permute-done | bytes 532512 | tf_op jit(solution)/shard_map/ppermute | solution.py:42
  24.2 0.1 reshape.13.facts_ref
  24.3 2.5 %collective-permute-start.3 = (bf16[2080,128]{1,0:T(8,128)(2,1)S(1)}, bf16[2080,128]{1,0:T(8,128)(2,1)S(1)}, u32[]{:S(2)}, u32[]{:S(2)}) collective-permute-start(bf16[2080,128]{1,0:T(8,128)(2,1)S(1)} %collective-permute-done.2.refs_1_), channel_id=1, source_target_pairs={{0,3},{8,56},{1,2},{9,57},{2,1},{10,58},{3,0},{11,59},{4,7},{12,60... | collective-permute-start | bytes 1597448 | tf_op jit(solution)/shard_map/ppermute | solution.py:42
  26.8 1.1 %collective-permute-done.1.refs_0_ = bf16[2080,128]{1,0:T(8,128)(2,1)S(1)} collective-permute-done((bf16[2080,128]{1,0:T(8,128)(2,1)S(1)}, bf16[2080,128]{1,0:T(8,128)(2,1)S(1)}, u32[]{:S(2)}, u32[]{:S(2)}) %collective-permute-start.1) | collective-permute-done | bytes 532512 | tf_op jit(solution)/shard_map/ppermute | solution.py:42
  27.9 0.0 collective-permute-done.7
  27.9 1.1 %constant_dynamic-update-slice_fusion.refs_2_ = bf16[4096,128]{1,0:T(8,128)(2,1)S(1)} fusion(bf16[4096,128]{1,0:T(8,128)(2,1)S(1)} %constant_dynamic-update-slice_fusion.1, bf16[2048,128]{1,0:T(8,128)(2,1)} %collective-permute-done.7), kind=kLoop, calls=%fused_computation.4 | loop fusion | bytes 1048576 | tf_op jit(solution)/shard_map/concatenate | solution.py:261
  29.0 8.9 %score.2.refs_3_ = f32[32,128]{1,0:T(8,128)S(1)} custom-call(s32[32]{0:T(128)S(1)} %reshape.13.facts_ref, bf16[2080,128]{1,0:T(8,128)(2,1)S(1)} %pad_maximum_fusion.refs_0_, bf16[2080,128]{1,0:T(8,128)(2,1)S(1)} %collective-permute-done.2.refs_1_, bf16[4096,128]{1,0:T(8,128)(2,1)S(1)} %constant_dynamic-update-slice_fusion.refs_2_), custom_call_target="tpu_custom_call" | custom-call | flops 6000000000 | bytes 1000000 | tf_op jit(solution)/shard_map/score/pallas_call | solution.py:205
  37.9 0.0 collective-permute-done.3.refs_1_
  37.9 0.1 reshape.12.facts_ref
  38.0 8.2 %score.3 = f32[16,8,128]{2,1,0:T(8,128)S(1)} custom-call(s32[32]{0:T(128)S(1)} %reshape.12.facts_ref, bf16[2080,128]{1,0:T(8,128)(2,1)S(1)} %collective-permute-done.1.refs_0_, bf16[2080,128]{1,0:T(8,128)(2,1)S(1)} %collective-permute-done.3.refs_1_, bf16[4096,128]{1,0:T(8,128)(2,1)S(1)} %constant_dynamic-update-slice_fusion.refs_2_, f32[32,128]{1,0:T(8,128)S(1)} %score.2.refs_3_), custom_call_target="tpu_custom_call" | custom-call | flops 6000000000 | bytes 1000000 | tf_op jit(solution)/shard_map/score/pallas_call | solution.py:205
  46.2 8.9 %all_to_all.5.given_ref = f32[16,8,128]{2,1,0:T(8,128)} all-to-all(f32[16,8,128]{2,1,0:T(8,128)S(1)} %score.3), channel_id=1, replica_groups={{0,16,4,20,1,17,5,21,8,24,12,28,9,25,13,29},{3,19,7,23,2,18,6,22,11,27,..., dimensions={0} | all-to-all | bytes 131072 | tf_op jit(solution)/shard_map/all_to_all | solution.py:267
  55.1 1.6 %finish.1 = f32[8]{0:T(128)} custom-call(s32[8]{0:T(128)} %positives_ref.1, f32[16,8,128]{2,1,0:T(8,128)} %all_to_all.5.given_ref), custom_call_target="tpu_custom_call" | custom-call | tf_op jit(solution)/shard_map/finish/pallas_call | solution.py:246
  (11 shorter events, 0.1 us)
Async XLA Ops:
  0.0 4.8 %collective-permute-start.4 = (bf16[256,128]{1,0:T(8,128)(2,1)}, bf16[256,128]{1,0:T(8,128)(2,1)S(1)}, u32[]{:S(2)}, u32[]{:S(2)}) collective-permute-start(bf16[256,128]{1,0:T(8,128)(2,1)} %bitcast.1), channel_id=1, source_target_pairs={{0,16},{8,12},{1,17},{9,13},{2,18},{10,14},{3,19},{11,15},{4,20},{... | collective-permute-start | bytes 196616 | tf_op jit(solution)/shard_map/ppermute | solution.py:42
  2.6 10.9 %collective-permute-start = (bf16[1040,128]{1,0:T(8,128)(2,1)S(1)}, bf16[1040,128]{1,0:T(8,128)(2,1)S(1)}, u32[]{:S(2)}, u32[]{:S(2)}) collective-permute-start(bf16[1040,128]{1,0:T(8,128)(2,1)S(1)} %pack_docs.1), channel_id=1, source_target_pairs={{0,48},{8,76},{1,49},{9,77},{2,50},{10,78},{3,51},{11,79},{4,52},{... | collective-permute-start | bytes 798728 | tf_op jit(solution)/shard_map/ppermute | solution.py:42
  5.7 5.0 %collective-permute-start.5 = (bf16[512,128]{1,0:T(8,128)(2,1)S(1)}, bf16[512,128]{1,0:T(8,128)(2,1)S(1)}, u32[]{:S(2)}, u32[]{:S(2)}) collective-permute-start(bf16[512,128]{1,0:T(8,128)(2,1)S(1)} %pad_maximum_fusion.3), channel_id=1, source_target_pairs={{0,4},{8,9},{1,5},{9,8},{2,6},{10,11},{3,7},{11,10},{4,0},{12,13},... | collective-permute-start | bytes 393224 | tf_op jit(solution)/shard_map/ppermute | solution.py:42
  7.3 12.0 %copy-start = (bf16[8,32,128]{2,1,0:T(8,128)(2,1)S(1)}, bf16[8,32,128]{2,1,0:T(8,128)(2,1)}, u32[]{:S(2)}) copy-start(bf16[8,32,128]{2,1,0:T(8,128)(2,1)} %param.4) | copy-start | bytes 196612
  11.6 7.8 %collective-permute-start.6 = (bf16[1024,128]{1,0:T(8,128)(2,1)S(1)}, bf16[1024,128]{1,0:T(8,128)(2,1)S(1)}, u32[]{:S(2)}, u32[]{:S(2)}) collective-permute-start(bf16[1024,128]{1,0:T(8,128)(2,1)S(1)} %pad_maximum_fusion.2), channel_id=1, source_target_pairs={{0,1},{8,24},{1,0},{9,25},{2,3},{10,26},{3,2},{11,27},{4,5},{12,28... | collective-permute-start | bytes 786440 | tf_op jit(solution)/shard_map/ppermute | solution.py:42
  13.6 10.6 %collective-permute-start.2 = (bf16[2080,128]{1,0:T(8,128)(2,1)S(1)}, bf16[2080,128]{1,0:T(8,128)(2,1)S(1)}, u32[]{:S(2)}, u32[]{:S(2)}) collective-permute-start(bf16[2080,128]{1,0:T(8,128)(2,1)S(1)} %pad_maximum_fusion.refs_0_), channel_id=1, source_target_pairs={{0,68},{8,11},{1,69},{9,10},{2,70},{10,9},{3,71},{11,8},{4,64},{12... | collective-permute-start | bytes 1597448 | tf_op jit(solution)/shard_map/ppermute | solution.py:42
  16.8 11.1 %collective-permute-start.1 = (bf16[2080,128]{1,0:T(8,128)(2,1)S(1)}, bf16[2080,128]{1,0:T(8,128)(2,1)S(1)}, u32[]{:S(2)}, u32[]{:S(2)}) collective-permute-start(bf16[2080,128]{1,0:T(8,128)(2,1)S(1)} %pad_maximum_fusion.refs_0_), channel_id=1, source_target_pairs={{0,3},{8,56},{1,2},{9,57},{2,1},{10,58},{3,0},{11,59},{4,7},{12,60... | collective-permute-start | bytes 1597448 | tf_op jit(solution)/shard_map/ppermute | solution.py:42
  20.2 7.7 %collective-permute-start.7 = (bf16[2048,128]{1,0:T(8,128)(2,1)}, bf16[2048,128]{1,0:T(8,128)(2,1)}, u32[]{:S(2)}, u32[]{:S(2)}) collective-permute-start(bf16[2048,128]{1,0:T(8,128)(2,1)} %pad_maximum_fusion.1), channel_id=1, source_target_pairs={{0,8},{8,0},{1,9},{9,1},{2,10},{10,2},{3,11},{11,3},{4,12},{12,4},... | collective-permute-start | bytes 1572872 | tf_op jit(solution)/shard_map/ppermute | solution.py:47
  24.3 13.6 %collective-permute-start.3 = (bf16[2080,128]{1,0:T(8,128)(2,1)S(1)}, bf16[2080,128]{1,0:T(8,128)(2,1)S(1)}, u32[]{:S(2)}, u32[]{:S(2)}) collective-permute-start(bf16[2080,128]{1,0:T(8,128)(2,1)S(1)} %collective-permute-done.2.refs_1_), channel_id=1, source_target_pairs={{0,3},{8,56},{1,2},{9,57},{2,1},{10,58},{3,0},{11,59},{4,7},{12,60... | collective-permute-start | bytes 1597448 | tf_op jit(solution)/shard_map/ppermute | solution.py:42

commit v5 on v4

--- a/solution.py
+++ b/solution.py
@@ -7,6 +7,7 @@
 from jax.experimental.pallas import tpu as pltpu
 from jax.sharding import Mesh, PartitionSpec as P
 
+
 neg_fill = -1e30
 QUERIES, TOKENS, DOCS, SLOTS, DIM = 8, 32, 8, 128, 128
 PAY = DOCS * SLOTS + 16
@@ -66,7 +67,8 @@
     return pl.BlockSpec(memory_space=space)
 
 
-def pack_docs_kernel(lengths_ref, docs_ref, out_ref):
+def pack_kernel(lengths_ref, docs_ref, queries_ref, out_ref, query_out):
+    query_out[...] = queries_ref[...]
     row = lax.broadcasted_iota(jnp.int32, (SLOTS, DIM), 0)
     for d in range(DOCS):
         doc = docs_ref[d].astype(jnp.float32)
@@ -79,15 +81,15 @@
     out_ref[DOCS * SLOTS :, :] = facts.astype(jnp.float32).astype(jnp.bfloat16)
 
 
-def pack_docs(lengths, docs):
+def pack(lengths, docs, queries):
     return pl.pallas_call(
-        pack_docs_kernel,
-        out_shape=pltpu.VMEM((PAY, DIM), jnp.bfloat16),
-        in_specs=[spec(pltpu.SMEM), spec(pltpu.VMEM)],
-        out_specs=spec(pltpu.VMEM),
+        pack_kernel,
+        out_shape=(pltpu.VMEM((PAY, DIM), jnp.bfloat16), pltpu.VMEM(queries.shape, jnp.bfloat16)),
+        in_specs=[spec(pltpu.SMEM), spec(pltpu.VMEM), spec(pltpu.VMEM)],
+        out_specs=(spec(pltpu.VMEM), spec(pltpu.VMEM)),
         cost_estimate=pl.CostEstimate(flops=10**6, bytes_accessed=10**6, transcendentals=0),
-        name="pack_docs",
-    )(lengths, docs)
+        name="pack",
+    )(lengths, docs, queries)
 
 
 def lower_half(shift, axis):
@@ -124,7 +126,7 @@
 
 def score_kernel(sizes, blocks, final, facts_ref, *refs):
     doc_refs, rest = refs[: len(sizes)], refs[len(sizes) :]
-    query_ref, rest = rest[0], rest[1:]
+    query_refs, rest = rest[:2], rest[2:]
     if final:
         earlier_ref, rest = rest[0], rest[1:]
     out_ref, rows, best, owner, carry = rest[:5]
@@ -152,7 +154,7 @@
         for b in range(blocks):
             similar = lax.dot_general(
                 block_rows,
-                query_ref[b * 256 : (b + 1) * 256, :],
+                query_refs[b // 8][b % 8 * 256 : (b % 8 + 1) * 256, :],
                 (((1,), (1,)), ((), ())),
                 preferred_element_type=jnp.float32,
             )
@@ -199,9 +201,9 @@
 def score(facts, docs, queries, earlier=None):
     sizes = [d.shape[0] // PAY for d in docs]
     doc_count = DOCS * sum(sizes)
-    blocks = queries.shape[0] // 256
+    blocks = sum(q.shape[0] for q in queries) // 256
     final = earlier is not None
-    operands = [*docs, queries] + ([earlier] if final else [])
+    operands = [*docs, *queries] + ([earlier] if final else [])
     return pl.pallas_call(
         functools.partial(score_kernel, sizes, blocks, final),
         out_shape=pltpu.VMEM((16, 8, 128) if final else (doc_count, 128), jnp.float32),
@@ -253,17 +255,22 @@
 
 
 def local(queries, documents, lengths, positives):
-    own = pack_docs(lengths, documents)
-    query = queries.reshape(QUERIES * TOKENS, DIM)
+    own, query = pack(lengths, documents, queries.reshape(QUERIES * TOKENS, DIM))
     near = swap(own, DOC_STEPS, 0)
-    for at in range(3):
-        query = jnp.concatenate([query, swap(query, QUERY_STEPS, at)])
-    query = jnp.concatenate([query, swap_cores(query)])
+    got = swap(query, QUERY_STEPS, 0)
+    query = jnp.concatenate([query, got])
+    got = swap(query, QUERY_STEPS, 1)
     both = jnp.concatenate([own, near])
     far = swap(both, DOC_STEPS, 1)
-    docs = [both, far], [swap(both, DOC_STEPS, 2), swap(far, DOC_STEPS, 2)]
-    given = score(lengths_of(docs[0]), docs[0], query)
-    given = score(lengths_of(docs[1]), docs[1], query, given)
+    query = jnp.concatenate([query, got])
+    got = swap(query, QUERY_STEPS, 2)
+    third = swap(both, DOC_STEPS, 2)
+    query = jnp.concatenate([query, got])
+    got = swap_cores(query)
+    fourth = swap(far, DOC_STEPS, 2)
+    queries = [query, got]
+    given = score(lengths_of([both, far]), [both, far], queries)
+    given = score(lengths_of([third, fourth]), [third, fourth], queries, given)
     given = lax.all_to_all(given, "d", 0, 0, tiled=True, axis_index_groups=owner_groups())
     return finish(positives, given)
 

time: 56.9 us -> 52.3 us (0.919)
  other arithmetic: 2.59 us -> 0.06 us
  Pallas kernels: 19.7 us -> 17.5 us
  local copies, waits for them, and re-layouts: 2.28 us -> 0.31 us
  starting transfers between devices: 15.7 us -> 17.4 us
    concatenate x4 -> x2, other arithmetic: 2.57 us -> 0.03 us  [local(): query = jnp.concatenate([query, got])]
    pallas_call x2, Pallas kernels: 17.1 us -> 14.9 us  [score(): pl.pallas_call(functools.partial(score_kernel, sizes, blocks, final), out...]
    ppermute x7, starting transfers between devices: 15.7 us -> 17.3 us  [swap(): return lax.ppermute(array, 'd', pairs)]
    concatenate x1 -> x2, local copies, waits for them, and re-layouts: 1.11 us -> 0.07 us  [the longest x1 0.04 us: local(): both = jnp.concatenate([own, near])]
    unnamed x6 -> x4, local copies, waits for them, and re-layouts: 0.99 us -> 0.05 us
  transfers between devices with their start and end apart: 8 -> 8, of which waited for: 3 -> 5; matrix products, arithmetic and copies ran while one was open for 8% -> 1% of each run, Pallas kernels for 17% -> 14%
where the time goes in v5:
time: 52.3 us; the launch traced here: 51.6 us
  Pallas kernels  17.5 us (33%)
  starting transfers between devices  17.4 us (33%)
  blocking collectives  8.9 us (17%)
  waiting for transfers between devices  7.38 us (14%)
    ppermute x7, starting transfers between devices, swap(): return lax.ppermute(array, 'd', pairs)  17.3 us
    pallas_call x2, Pallas kernels, score(): pl.pallas_call(functools.partial(score_kernel, sizes, blocks, final), out...  14.9 us
    all_to_all x1, blocking collectives, local(): lax.all_to_all(given, 'd', 0, 0, tiled=True, axis_index_groups=owner_grou...  8.9 us
    ppermute x7, waiting for transfers between devices, swap(): return lax.ppermute(array, 'd', pairs)  7.37 us
    pallas_call x1, Pallas kernels, finish(): pl.pallas_call(finish_kernel, out_shape=jax.ShapeDtypeStruct((QUERIES,),...  1.57 us
  transfers between devices with their start and end apart: 8, of which 5 were waited for; matrix products, arithmetic and copies ran while one was open for 1% of the time, Pallas kernels for 14%

profile of v5, /device:TPU:0, one launch (start us, length us, event | category | flops | bytes accessed | tf_op | source)
XLA Modules:
  0.0 51.6 jit_solution(14968007887698877438)
XLA Ops:
  0.0 1.0 %pack.1 = (bf16[1040,128]{1,0:T(8,128)(2,1)S(1)}, bf16[256,128]{1,0:T(8,128)(2,1)S(1)}) custom-call(s32[8]{0:T(128)} %lengths_ref.1, bf16[8,128,128]{2,1,0:T(8,128)(2,1)} %docs_ref.1, bf16[256,128]{1,0:T(8,128)(2,1)} %bitcast.1), custom_call_target="tpu_custom_call" | custom-call | flops 1000000 | bytes 1000000 | tf_op jit(solution)/shard_map/pack/pallas_call | solution.py:85
  1.0 1.7 %collective-permute-start.4 = (bf16[256,128]{1,0:T(8,128)(2,1)S(1)}, bf16[256,128]{1,0:T(8,128)(2,1)S(1)}, u32[]{:S(2)}, u32[]{:S(2)}) collective-permute-start(bf16[256,128]{1,0:T(8,128)(2,1)S(1)} %get-tuple-element.8), channel_id=1, source_target_pairs={{0,16},{8,12},{1,17},{9,13},{2,18},{10,14},{3,19},{11,15},{4,20},{... | collective-permute-start | bytes 196616 | tf_op jit(solution)/shard_map/ppermute | solution.py:43
  2.7 2.1 %collective-permute-start = (bf16[1040,128]{1,0:T(8,128)(2,1)S(1)}, bf16[1040,128]{1,0:T(8,128)(2,1)S(1)}, u32[]{:S(2)}, u32[]{:S(2)}) collective-permute-start(bf16[1040,128]{1,0:T(8,128)(2,1)S(1)} %get-tuple-element.7), channel_id=1, source_target_pairs={{0,48},{8,76},{1,49},{9,77},{2,50},{10,78},{3,51},{11,79},{4,52},{... | collective-permute-start | bytes 798728 | tf_op jit(solution)/shard_map/ppermute | solution.py:43
  4.8 0.5 %collective-permute-done.4 = bf16[256,128]{1,0:T(8,128)(2,1)S(1)} collective-permute-done((bf16[256,128]{1,0:T(8,128)(2,1)S(1)}, bf16[256,128]{1,0:T(8,128)(2,1)S(1)}, u32[]{:S(2)}, u32[]{:S(2)}) %collective-permute-start.4) | collective-permute-done | bytes 65568 | tf_op jit(solution)/shard_map/ppermute | solution.py:43
  5.4 1.8 %collective-permute-start.5 = (bf16[512,128]{1,0:T(8,128)(2,1)S(1)}, bf16[512,128]{1,0:T(8,128)(2,1)S(1)}, u32[]{:S(2)}, u32[]{:S(2)}) collective-permute-start(bf16[512,128]{1,0:T(8,128)(2,1)S(1)} %pad_maximum_fusion.1), channel_id=1, source_target_pairs={{0,4},{8,9},{1,5},{9,8},{2,6},{10,11},{3,7},{11,10},{4,0},{12,13},... | collective-permute-start | bytes 393224 | tf_op jit(solution)/shard_map/ppermute | solution.py:43
  7.2 3.2 %collective-permute-done = bf16[1040,128]{1,0:T(8,128)(2,1)S(1)} collective-permute-done((bf16[1040,128]{1,0:T(8,128)(2,1)S(1)}, bf16[1040,128]{1,0:T(8,128)(2,1)S(1)}, u32[]{:S(2)}, u32[]{:S(2)}) %collective-permute-start) | collective-permute-done | bytes 266272 | tf_op jit(solution)/shard_map/ppermute | solution.py:43
  10.4 3.1 %collective-permute-start.2 = (bf16[2080,128]{1,0:T(8,128)(2,1)S(1)}, bf16[2080,128]{1,0:T(8,128)(2,1)S(1)}, u32[]{:S(2)}, u32[]{:S(2)}) collective-permute-start(bf16[2080,128]{1,0:T(8,128)(2,1)S(1)} %constant_dynamic-update-slice_fusion.refs_0_), channel_id=1, source_target_pairs={{0,68},{8,11},{1,69},{9,10},{2,70},{10,9},{3,71},{11,8},{4,64},{12... | collective-permute-start | bytes 1597448 | tf_op jit(solution)/shard_map/ppermute | solution.py:43
  13.5 0.0 collective-permute-done.5
  13.5 2.0 %collective-permute-start.6 = (bf16[1024,128]{1,0:T(8,128)(2,1)S(1)}, bf16[1024,128]{1,0:T(8,128)(2,1)S(1)}, u32[]{:S(2)}, u32[]{:S(2)}) collective-permute-start(bf16[1024,128]{1,0:T(8,128)(2,1)S(1)} %pad_maximum_fusion), channel_id=1, source_target_pairs={{0,1},{8,24},{1,0},{9,25},{2,3},{10,26},{3,2},{11,27},{4,5},{12,28... | collective-permute-start | bytes 786440 | tf_op jit(solution)/shard_map/ppermute | solution.py:43
  15.5 2.6 %collective-permute-start.1 = (bf16[2080,128]{1,0:T(8,128)(2,1)S(1)}, bf16[2080,128]{1,0:T(8,128)(2,1)S(1)}, u32[]{:S(2)}, u32[]{:S(2)}) collective-permute-start(bf16[2080,128]{1,0:T(8,128)(2,1)S(1)} %constant_dynamic-update-slice_fusion.refs_0_), channel_id=1, source_target_pairs={{0,3},{8,56},{1,2},{9,57},{2,1},{10,58},{3,0},{11,59},{4,7},{12,60... | collective-permute-start | bytes 1597448 | tf_op jit(solution)/shard_map/ppermute | solution.py:43
  18.2 1.8 %collective-permute-done.6 = bf16[1024,128]{1,0:T(8,128)(2,1)S(1)} collective-permute-done((bf16[1024,128]{1,0:T(8,128)(2,1)S(1)}, bf16[1024,128]{1,0:T(8,128)(2,1)S(1)}, u32[]{:S(2)}, u32[]{:S(2)}) %collective-permute-start.6) | collective-permute-done | bytes 262176 | tf_op jit(solution)/shard_map/ppermute | solution.py:43
  20.0 0.1 collective-permute-start.7
  20.1 0.9 %collective-permute-done.2.refs_1_ = bf16[2080,128]{1,0:T(8,128)(2,1)S(1)} collective-permute-done((bf16[2080,128]{1,0:T(8,128)(2,1)S(1)}, bf16[2080,128]{1,0:T(8,128)(2,1)S(1)}, u32[]{:S(2)}, u32[]{:S(2)}) %collective-permute-start.2) | collective-permute-done | bytes 532512 | tf_op jit(solution)/shard_map/ppermute | solution.py:43
  21.0 0.1 reshape.13.facts_ref
  21.1 4.0 %collective-permute-start.3 = (bf16[2080,128]{1,0:T(8,128)(2,1)S(1)}, bf16[2080,128]{1,0:T(8,128)(2,1)S(1)}, u32[]{:S(2)}, u32[]{:S(2)}) collective-permute-start(bf16[2080,128]{1,0:T(8,128)(2,1)S(1)} %collective-permute-done.2.refs_1_), channel_id=1, source_target_pairs={{0,3},{8,56},{1,2},{9,57},{2,1},{10,58},{3,0},{11,59},{4,7},{12,60... | collective-permute-start | bytes 1597448 | tf_op jit(solution)/shard_map/ppermute | solution.py:43
  25.1 1.0 %collective-permute-done.1.refs_0_ = bf16[2080,128]{1,0:T(8,128)(2,1)S(1)} collective-permute-done((bf16[2080,128]{1,0:T(8,128)(2,1)S(1)}, bf16[2080,128]{1,0:T(8,128)(2,1)S(1)}, u32[]{:S(2)}, u32[]{:S(2)}) %collective-permute-start.1) | collective-permute-done | bytes 532512 | tf_op jit(solution)/shard_map/ppermute | solution.py:43
  26.1 0.0 collective-permute-done.7.refs_3_
  26.1 7.4 %score.2.refs_4_ = f32[32,128]{1,0:T(8,128)S(1)} custom-call(s32[32]{0:T(128)S(1)} %reshape.13.facts_ref, bf16[2080,128]{1,0:T(8,128)(2,1)S(1)} %constant_dynamic-update-slice_fusion.refs_0_, bf16[2080,128]{1,0:T(8,128)(2,1)S(1)} %collective-permute-done.2.refs_1_, bf16[2048,128]{1,0:T(8,128)(2,1)S(1)} %constant_dynamic-update-slice_fusion.2.refs_2_, ...), custom_call_target="tpu_custom_call" | custom-call | flops 6000000000 | bytes 1000000 | tf_op jit(solution)/shard_map/score/pallas_call | solution.py:207
  33.5 0.0 collective-permute-done.3.refs_1_
  33.5 0.1 reshape.12.facts_ref
  33.6 7.5 %score.3 = f32[16,8,128]{2,1,0:T(8,128)S(1)} custom-call(s32[32]{0:T(128)S(1)} %reshape.12.facts_ref, bf16[2080,128]{1,0:T(8,128)(2,1)S(1)} %collective-permute-done.1.refs_0_, bf16[2080,128]{1,0:T(8,128)(2,1)S(1)} %collective-permute-done.3.refs_1_, bf16[2048,128]{1,0:T(8,128)(2,1)S(1)} %constant_dynamic-update-slice_fusion.2.refs_2_, ...), custom_call_target="tpu_custom_call" | custom-call | flops 6000000000 | bytes 1000000 | tf_op jit(solution)/shard_map/score/pallas_call | solution.py:207
  41.2 8.9 %all_to_all.5.given_ref = f32[16,8,128]{2,1,0:T(8,128)} all-to-all(f32[16,8,128]{2,1,0:T(8,128)S(1)} %score.3), channel_id=1, replica_groups={{0,16,4,20,1,17,5,21,8,24,12,28,9,25,13,29},{3,19,7,23,2,18,6,22,11,27,..., dimensions={0} | all-to-all | bytes 131072 | tf_op jit(solution)/shard_map/all_to_all | solution.py:274
  50.1 1.6 %finish.1 = f32[8]{0:T(128)} custom-call(s32[8]{0:T(128)} %positives_ref.1, f32[16,8,128]{2,1,0:T(8,128)} %all_to_all.5.given_ref), custom_call_target="tpu_custom_call" | custom-call | tf_op jit(solution)/shard_map/finish/pallas_call | solution.py:248
  (15 shorter events, 0.2 us)
Async XLA Ops:
  1.0 4.3 %collective-permute-start.4 = (bf16[256,128]{1,0:T(8,128)(2,1)S(1)}, bf16[256,128]{1,0:T(8,128)(2,1)S(1)}, u32[]{:S(2)}, u32[]{:S(2)}) collective-permute-start(bf16[256,128]{1,0:T(8,128)(2,1)S(1)} %get-tuple-element.8), channel_id=1, source_target_pairs={{0,16},{8,12},{1,17},{9,13},{2,18},{10,14},{3,19},{11,15},{4,20},{... | collective-permute-start | bytes 196616 | tf_op jit(solution)/shard_map/ppermute | solution.py:43
  2.7 7.6 %collective-permute-start = (bf16[1040,128]{1,0:T(8,128)(2,1)S(1)}, bf16[1040,128]{1,0:T(8,128)(2,1)S(1)}, u32[]{:S(2)}, u32[]{:S(2)}) collective-permute-start(bf16[1040,128]{1,0:T(8,128)(2,1)S(1)} %get-tuple-element.7), channel_id=1, source_target_pairs={{0,48},{8,76},{1,49},{9,77},{2,50},{10,78},{3,51},{11,79},{4,52},{... | collective-permute-start | bytes 798728 | tf_op jit(solution)/shard_map/ppermute | solution.py:43
  5.4 8.1 %collective-permute-start.5 = (bf16[512,128]{1,0:T(8,128)(2,1)S(1)}, bf16[512,128]{1,0:T(8,128)(2,1)S(1)}, u32[]{:S(2)}, u32[]{:S(2)}) collective-permute-start(bf16[512,128]{1,0:T(8,128)(2,1)S(1)} %pad_maximum_fusion.1), channel_id=1, source_target_pairs={{0,4},{8,9},{1,5},{9,8},{2,6},{10,11},{3,7},{11,10},{4,0},{12,13},... | collective-permute-start | bytes 393224 | tf_op jit(solution)/shard_map/ppermute | solution.py:43
  10.4 10.6 %collective-permute-start.2 = (bf16[2080,128]{1,0:T(8,128)(2,1)S(1)}, bf16[2080,128]{1,0:T(8,128)(2,1)S(1)}, u32[]{:S(2)}, u32[]{:S(2)}) collective-permute-start(bf16[2080,128]{1,0:T(8,128)(2,1)S(1)} %constant_dynamic-update-slice_fusion.refs_0_), channel_id=1, source_target_pairs={{0,68},{8,11},{1,69},{9,10},{2,70},{10,9},{3,71},{11,8},{4,64},{12... | collective-permute-start | bytes 1597448 | tf_op jit(solution)/shard_map/ppermute | solution.py:43
  13.5 6.5 %collective-permute-start.6 = (bf16[1024,128]{1,0:T(8,128)(2,1)S(1)}, bf16[1024,128]{1,0:T(8,128)(2,1)S(1)}, u32[]{:S(2)}, u32[]{:S(2)}) collective-permute-start(bf16[1024,128]{1,0:T(8,128)(2,1)S(1)} %pad_maximum_fusion), channel_id=1, source_target_pairs={{0,1},{8,24},{1,0},{9,25},{2,3},{10,26},{3,2},{11,27},{4,5},{12,28... | collective-permute-start | bytes 786440 | tf_op jit(solution)/shard_map/ppermute | solution.py:43
  15.5 10.6 %collective-permute-start.1 = (bf16[2080,128]{1,0:T(8,128)(2,1)S(1)}, bf16[2080,128]{1,0:T(8,128)(2,1)S(1)}, u32[]{:S(2)}, u32[]{:S(2)}) collective-permute-start(bf16[2080,128]{1,0:T(8,128)(2,1)S(1)} %constant_dynamic-update-slice_fusion.refs_0_), channel_id=1, source_target_pairs={{0,3},{8,56},{1,2},{9,57},{2,1},{10,58},{3,0},{11,59},{4,7},{12,60... | collective-permute-start | bytes 1597448 | tf_op jit(solution)/shard_map/ppermute | solution.py:43
  20.0 6.1 %collective-permute-start.7 = (bf16[2048,128]{1,0:T(8,128)(2,1)S(1)}, bf16[2048,128]{1,0:T(8,128)(2,1)S(1)}, u32[]{:S(2)}, u32[]{:S(2)}) collective-permute-start(bf16[2048,128]{1,0:T(8,128)(2,1)S(1)} %constant_dynamic-update-slice_fusion.2.refs_2_), channel_id=1, source_target_pairs={{0,8},{8,0},{1,9},{9,1},{2,10},{10,2},{3,11},{11,3},{4,12},{12,4},... | collective-permute-start | bytes 1572872 | tf_op jit(solution)/shard_map/ppermute | solution.py:48
  21.1 12.4 %collective-permute-start.3 = (bf16[2080,128]{1,0:T(8,128)(2,1)S(1)}, bf16[2080,128]{1,0:T(8,128)(2,1)S(1)}, u32[]{:S(2)}, u32[]{:S(2)}) collective-permute-start(bf16[2080,128]{1,0:T(8,128)(2,1)S(1)} %collective-permute-done.2.refs_1_), channel_id=1, source_target_pairs={{0,3},{8,56},{1,2},{9,57},{2,1},{10,58},{3,0},{11,59},{4,7},{12,60... | collective-permute-start | bytes 1597448 | tf_op jit(solution)/shard_map/ppermute | solution.py:43

commit v6 on v5

--- a/solution.py
+++ b/solution.py
@@ -255,22 +255,19 @@
 
 
 def local(queries, documents, lengths, positives):
-    own, query = pack(lengths, documents, queries.reshape(QUERIES * TOKENS, DIM))
-    near = swap(own, DOC_STEPS, 0)
+    query = queries.reshape(QUERIES * TOKENS, DIM)
     got = swap(query, QUERY_STEPS, 0)
+    own, query = pack(lengths, documents, query)
+    first = swap(own, DOC_STEPS, 0)
+    second = swap(own, DOC_STEPS, 1)
     query = jnp.concatenate([query, got])
-    got = swap(query, QUERY_STEPS, 1)
-    both = jnp.concatenate([own, near])
-    far = swap(both, DOC_STEPS, 1)
-    query = jnp.concatenate([query, got])
-    got = swap(query, QUERY_STEPS, 2)
-    third = swap(both, DOC_STEPS, 2)
-    query = jnp.concatenate([query, got])
-    got = swap_cores(query)
-    fourth = swap(far, DOC_STEPS, 2)
-    queries = [query, got]
-    given = score(lengths_of([both, far]), [both, far], queries)
-    given = score(lengths_of([third, fourth]), [third, fourth], queries, given)
+    query = jnp.concatenate([query, swap(query, QUERY_STEPS, 1)])
+    query = jnp.concatenate([query, swap(query, QUERY_STEPS, 2)])
+    near = [own, first, second, swap(first, DOC_STEPS, 1)]
+    far = [swap(jnp.concatenate(near[:2]), DOC_STEPS, 2), swap(jnp.concatenate(near[2:]), DOC_STEPS, 2)]
+    queries = [query, swap_cores(query)]
+    given = score(lengths_of(near), near, queries)
+    given = score(lengths_of(far), far, queries, given)
     given = lax.all_to_all(given, "d", 0, 0, tiled=True, axis_index_groups=owner_groups())
     return finish(positives, given)
 

time: 52.3 us -> 52.9 us (1.011)
  starting transfers between devices: 17.4 us -> 14.5 us
  waiting for transfers between devices: 7.38 us -> 10.1 us
  other arithmetic: 0.06 us -> 0.91 us
    ppermute x7 -> x8, starting transfers between devices: 17.3 us -> 14.4 us  [swap(): return lax.ppermute(array, 'd', pairs)]
    ppermute x7 -> x8, waiting for transfers between devices: 7.37 us -> 10.1 us  [swap(): return lax.ppermute(array, 'd', pairs)]
    concatenate x0 -> x3, other arithmetic: none -> 0.88 us  [the longest x1 0.82 us: local(): jnp.concatenate(near[:2])]
  transfers between devices with their start and end apart: 8 -> 9, of which waited for: 5 -> 4; matrix products, arithmetic and copies ran while one was open for 1% -> 2% of each run, Pallas kernels for 14% -> 16%
where the time goes in v6:
time: 52.9 us; the launch traced here: 52.2 us
  Pallas kernels  17.5 us (33%)
  starting transfers between devices  14.5 us (27%)
  waiting for transfers between devices  10.1 us (19%)
  blocking collectives  8.9 us (17%)
  other arithmetic  0.91 us (2%)
    pallas_call x2, Pallas kernels, score(): pl.pallas_call(functools.partial(score_kernel, sizes, blocks, final), out...  14.9 us
    ppermute x8, starting transfers between devices, swap(): return lax.ppermute(array, 'd', pairs)  14.4 us
    ppermute x8, waiting for transfers between devices, swap(): return lax.ppermute(array, 'd', pairs)  10.1 us
    all_to_all x1, blocking collectives, local(): lax.all_to_all(given, 'd', 0, 0, tiled=True, axis_index_groups=owner_grou...  8.9 us
    pallas_call x1, Pallas kernels, finish(): pl.pallas_call(finish_kernel, out_shape=jax.ShapeDtypeStruct((QUERIES,),...  1.57 us
  transfers between devices with their start and end apart: 9, of which 4 were waited for; matrix products, arithmetic and copies ran while one was open for 2% of the time, Pallas kernels for 16%

profile of v6, /device:TPU:0, one launch (start us, length us, event | category | flops | bytes accessed | tf_op | source)
XLA Modules:
  0.0 52.2 jit_solution(16807025360503466604)
XLA Ops:
  0.0 1.6 %collective-permute-start.5 = (bf16[256,128]{1,0:T(8,128)(2,1)}, bf16[256,128]{1,0:T(8,128)(2,1)S(1)}, u32[]{:S(2)}, u32[]{:S(2)}) collective-permute-start(bf16[256,128]{1,0:T(8,128)(2,1)} %bitcast.1), channel_id=1, source_target_pairs={{0,16},{8,12},{1,17},{9,13},{2,18},{10,14},{3,19},{11,15},{4,20},{... | collective-permute-start | bytes 196616 | tf_op jit(solution)/shard_map/ppermute | solution.py:43
  1.6 1.0 %pack.1 = (bf16[1040,128]{1,0:T(8,128)(2,1)S(1)}, bf16[256,128]{1,0:T(8,128)(2,1)S(1)}) custom-call(s32[8]{0:T(128)} %lengths_ref.1, bf16[8,128,128]{2,1,0:T(8,128)(2,1)} %docs_ref.1, bf16[256,128]{1,0:T(8,128)(2,1)} %bitcast.2), custom_call_target="tpu_custom_call" | custom-call | flops 1000000 | bytes 1000000 | tf_op jit(solution)/shard_map/pack/pallas_call | solution.py:85
  2.6 2.2 %collective-permute-start = (bf16[1040,128]{1,0:T(8,128)(2,1)S(1)}, bf16[1040,128]{1,0:T(8,128)(2,1)S(1)}, u32[]{:S(2)}, u32[]{:S(2)}) collective-permute-start(bf16[1040,128]{1,0:T(8,128)(2,1)S(1)} %get-tuple-element.7.refs_0_), channel_id=1, source_target_pairs={{0,48},{8,76},{1,49},{9,77},{2,50},{10,78},{3,51},{11,79},{4,52},{... | collective-permute-start | bytes 798728 | tf_op jit(solution)/shard_map/ppermute | solution.py:43
  4.8 3.0 %collective-permute-start.2 = (bf16[1040,128]{1,0:T(8,128)(2,1)S(1)}, bf16[1040,128]{1,0:T(8,128)(2,1)S(1)}, u32[]{:S(2)}, u32[]{:S(2)}) collective-permute-start(bf16[1040,128]{1,0:T(8,128)(2,1)S(1)} %get-tuple-element.7.refs_0_), channel_id=1, source_target_pairs={{0,68},{8,11},{1,69},{9,10},{2,70},{10,9},{3,71},{11,8},{4,64},{12... | collective-permute-start | bytes 798728 | tf_op jit(solution)/shard_map/ppermute | solution.py:43
  7.8 0.0 collective-permute-done.5
  7.9 0.2 collective-permute-start.6
  8.1 4.8 %collective-permute-done.6 = bf16[512,128]{1,0:T(8,128)(2,1)S(1)} collective-permute-done((bf16[512,128]{1,0:T(8,128)(2,1)S(1)}, bf16[512,128]{1,0:T(8,128)(2,1)S(1)}, u32[]{:S(2)}, u32[]{:S(2)}) %collective-permute-start.6) | collective-permute-done | bytes 131104 | tf_op jit(solution)/shard_map/ppermute | solution.py:43
  12.9 2.0 %collective-permute-start.7 = (bf16[1024,128]{1,0:T(8,128)(2,1)S(1)}, bf16[1024,128]{1,0:T(8,128)(2,1)S(1)}, u32[]{:S(2)}, u32[]{:S(2)}) collective-permute-start(bf16[1024,128]{1,0:T(8,128)(2,1)S(1)} %pad_maximum_fusion.2), channel_id=1, source_target_pairs={{0,1},{8,24},{1,0},{9,25},{2,3},{10,26},{3,2},{11,27},{4,5},{12,28... | collective-permute-start | bytes 786440 | tf_op jit(solution)/shard_map/ppermute | solution.py:43
  14.9 0.0 collective-permute-done.refs_1_
  14.9 0.3 collective-permute-start.3
  15.3 0.8 %pad_maximum_fusion = bf16[2080,128]{1,0:T(8,128)(2,1)} fusion(bf16[1040,128]{1,0:T(8,128)(2,1)S(1)} %collective-permute-done.refs_1_, bf16[1040,128]{1,0:T(8,128)(2,1)S(1)} %get-tuple-element.7.refs_0_), kind=kLoop, calls=%fused_computation | loop fusion | flops 1064960 | bytes 1064960 | tf_op jit(solution)/shard_map/concatenate | solution.py:267
  16.1 2.5 %collective-permute-start.1 = (bf16[2080,128]{1,0:T(8,128)(2,1)}, bf16[2080,128]{1,0:T(8,128)(2,1)S(1)}, u32[]{:S(2)}, u32[]{:S(2)}) collective-permute-start(bf16[2080,128]{1,0:T(8,128)(2,1)} %pad_maximum_fusion), channel_id=1, source_target_pairs={{0,3},{8,56},{1,2},{9,57},{2,1},{10,58},{3,0},{11,59},{4,7},{12,60... | collective-permute-start | bytes 1597448 | tf_op jit(solution)/shard_map/ppermute | solution.py:43
  18.6 0.0 collective-permute-done.2.refs_2_
  18.6 0.8 %collective-permute-done.7 = bf16[1024,128]{1,0:T(8,128)(2,1)S(1)} collective-permute-done((bf16[1024,128]{1,0:T(8,128)(2,1)S(1)}, bf16[1024,128]{1,0:T(8,128)(2,1)S(1)}, u32[]{:S(2)}, u32[]{:S(2)}) %collective-permute-start.7) | collective-permute-done | bytes 262176 | tf_op jit(solution)/shard_map/ppermute | solution.py:43
  19.4 0.1 collective-permute-start.8
  19.5 3.2 %collective-permute-done.3.refs_3_ = bf16[1040,128]{1,0:T(8,128)(2,1)S(1)} collective-permute-done((bf16[1040,128]{1,0:T(8,128)(2,1)S(1)}, bf16[1040,128]{1,0:T(8,128)(2,1)S(1)}, u32[]{:S(2)}, u32[]{:S(2)}) %collective-permute-start.3) | collective-permute-done | bytes 266272 | tf_op jit(solution)/shard_map/ppermute | solution.py:43
  22.7 0.1 reshape.13.facts_ref
  22.8 2.6 %collective-permute-start.4 = (bf16[2080,128]{1,0:T(8,128)(2,1)S(1)}, bf16[2080,128]{1,0:T(8,128)(2,1)S(1)}, u32[]{:S(2)}, u32[]{:S(2)}) collective-permute-start(bf16[2080,128]{1,0:T(8,128)(2,1)S(1)} %pad_maximum_fusion.1), channel_id=1, source_target_pairs={{0,3},{8,56},{1,2},{9,57},{2,1},{10,58},{3,0},{11,59},{4,7},{12,60... | collective-permute-start | bytes 1597448 | tf_op jit(solution)/shard_map/ppermute | solution.py:43
  25.4 1.4 %collective-permute-done.1.refs_0_ = bf16[2080,128]{1,0:T(8,128)(2,1)S(1)} collective-permute-done((bf16[2080,128]{1,0:T(8,128)(2,1)}, bf16[2080,128]{1,0:T(8,128)(2,1)S(1)}, u32[]{:S(2)}, u32[]{:S(2)}) %collective-permute-start.1) | collective-permute-done | bytes 532512 | tf_op jit(solution)/shard_map/ppermute | solution.py:43
  26.8 0.0 collective-permute-done.8.refs_5_.refs_3_
  26.8 7.4 %score.2.refs_4_ = f32[32,128]{1,0:T(8,128)S(1)} custom-call(s32[32]{0:T(128)S(1)} %reshape.13.facts_ref, bf16[1040,128]{1,0:T(8,128)(2,1)S(1)} %get-tuple-element.7.refs_0_, bf16[1040,128]{1,0:T(8,128)(2,1)S(1)} %collective-permute-done.refs_1_, bf16[1040,128]{1,0:T(8,128)(2,1)S(1)} %collective-permute-done.2.refs_2_, ...), custom_call_target="tpu_custom_call" | custom-call | flops 6000000000 | bytes 1000000 | tf_op jit(solution)/shard_map/score/pallas_call | solution.py:207
  34.1 0.0 collective-permute-done.4.refs_1_
  34.2 0.1 reshape.12.facts_ref
  34.2 7.5 %score.3 = f32[16,8,128]{2,1,0:T(8,128)S(1)} custom-call(s32[32]{0:T(128)S(1)} %reshape.12.facts_ref, bf16[2080,128]{1,0:T(8,128)(2,1)S(1)} %collective-permute-done.1.refs_0_, bf16[2080,128]{1,0:T(8,128)(2,1)S(1)} %collective-permute-done.4.refs_1_, bf16[2048,128]{1,0:T(8,128)(2,1)S(1)} %constant_dynamic-update-slice_fusion.refs_4_.refs_2_, ...), custom_call_target="tpu_custom_call" | custom-call | flops 6000000000 | bytes 1000000 | tf_op jit(solution)/shard_map/score/pallas_call | solution.py:207
  41.8 8.9 %all_to_all.5.given_ref = f32[16,8,128]{2,1,0:T(8,128)} all-to-all(f32[16,8,128]{2,1,0:T(8,128)S(1)} %score.3), channel_id=1, replica_groups={{0,16,4,20,1,17,5,21,8,24,12,28,9,25,13,29},{3,19,7,23,2,18,6,22,11,27,..., dimensions={0} | all-to-all | bytes 131072 | tf_op jit(solution)/shard_map/all_to_all | solution.py:271
  50.7 1.6 %finish.1 = f32[8]{0:T(128)} custom-call(s32[8]{0:T(128)} %positives_ref.1, f32[16,8,128]{2,1,0:T(8,128)} %all_to_all.5.given_ref), custom_call_target="tpu_custom_call" | custom-call | tf_op jit(solution)/shard_map/finish/pallas_call | solution.py:248
  (15 shorter events, 0.2 us)
Async XLA Ops:
  0.0 7.8 %collective-permute-start.5 = (bf16[256,128]{1,0:T(8,128)(2,1)}, bf16[256,128]{1,0:T(8,128)(2,1)S(1)}, u32[]{:S(2)}, u32[]{:S(2)}) collective-permute-start(bf16[256,128]{1,0:T(8,128)(2,1)} %bitcast.1), channel_id=1, source_target_pairs={{0,16},{8,12},{1,17},{9,13},{2,18},{10,14},{3,19},{11,15},{4,20},{... | collective-permute-start | bytes 196616 | tf_op jit(solution)/shard_map/ppermute | solution.py:43
  2.6 12.3 %collective-permute-start = (bf16[1040,128]{1,0:T(8,128)(2,1)S(1)}, bf16[1040,128]{1,0:T(8,128)(2,1)S(1)}, u32[]{:S(2)}, u32[]{:S(2)}) collective-permute-start(bf16[1040,128]{1,0:T(8,128)(2,1)S(1)} %get-tuple-element.7.refs_0_), channel_id=1, source_target_pairs={{0,48},{8,76},{1,49},{9,77},{2,50},{10,78},{3,51},{11,79},{4,52},{... | collective-permute-start | bytes 798728 | tf_op jit(solution)/shard_map/ppermute | solution.py:43
  4.8 13.8 %collective-permute-start.2 = (bf16[1040,128]{1,0:T(8,128)(2,1)S(1)}, bf16[1040,128]{1,0:T(8,128)(2,1)S(1)}, u32[]{:S(2)}, u32[]{:S(2)}) collective-permute-start(bf16[1040,128]{1,0:T(8,128)(2,1)S(1)} %get-tuple-element.7.refs_0_), channel_id=1, source_target_pairs={{0,68},{8,11},{1,69},{9,10},{2,70},{10,9},{3,71},{11,8},{4,64},{12... | collective-permute-start | bytes 798728 | tf_op jit(solution)/shard_map/ppermute | solution.py:43
  7.9 5.0 %collective-permute-start.6 = (bf16[512,128]{1,0:T(8,128)(2,1)S(1)}, bf16[512,128]{1,0:T(8,128)(2,1)S(1)}, u32[]{:S(2)}, u32[]{:S(2)}) collective-permute-start(bf16[512,128]{1,0:T(8,128)(2,1)S(1)} %pad_maximum_fusion.3), channel_id=1, source_target_pairs={{0,4},{8,9},{1,5},{9,8},{2,6},{10,11},{3,7},{11,10},{4,0},{12,13},... | collective-permute-start | bytes 393224 | tf_op jit(solution)/shard_map/ppermute | solution.py:43
  12.9 6.5 %collective-permute-start.7 = (bf16[1024,128]{1,0:T(8,128)(2,1)S(1)}, bf16[1024,128]{1,0:T(8,128)(2,1)S(1)}, u32[]{:S(2)}, u32[]{:S(2)}) collective-permute-start(bf16[1024,128]{1,0:T(8,128)(2,1)S(1)} %pad_maximum_fusion.2), channel_id=1, source_target_pairs={{0,1},{8,24},{1,0},{9,25},{2,3},{10,26},{3,2},{11,27},{4,5},{12,28... | collective-permute-start | bytes 786440 | tf_op jit(solution)/shard_map/ppermute | solution.py:43
  14.9 7.7 %collective-permute-start.3 = (bf16[1040,128]{1,0:T(8,128)(2,1)S(1)}, bf16[1040,128]{1,0:T(8,128)(2,1)S(1)}, u32[]{:S(2)}, u32[]{:S(2)}) collective-permute-start(bf16[1040,128]{1,0:T(8,128)(2,1)S(1)} %collective-permute-done.refs_1_), channel_id=1, source_target_pairs={{0,68},{8,11},{1,69},{9,10},{2,70},{10,9},{3,71},{11,8},{4,64},{12... | collective-permute-start | bytes 798728 | tf_op jit(solution)/shard_map/ppermute | solution.py:43
  16.1 10.7 %collective-permute-start.1 = (bf16[2080,128]{1,0:T(8,128)(2,1)}, bf16[2080,128]{1,0:T(8,128)(2,1)S(1)}, u32[]{:S(2)}, u32[]{:S(2)}) collective-permute-start(bf16[2080,128]{1,0:T(8,128)(2,1)} %pad_maximum_fusion), channel_id=1, source_target_pairs={{0,3},{8,56},{1,2},{9,57},{2,1},{10,58},{3,0},{11,59},{4,7},{12,60... | collective-permute-start | bytes 1597448 | tf_op jit(solution)/shard_map/ppermute | solution.py:43
  19.4 7.4 %collective-permute-start.8 = (bf16[2048,128]{1,0:T(8,128)(2,1)S(1)}, bf16[2048,128]{1,0:T(8,128)(2,1)S(1)}, u32[]{:S(2)}, u32[]{:S(2)}) collective-permute-start(bf16[2048,128]{1,0:T(8,128)(2,1)S(1)} %constant_dynamic-update-slice_fusion.refs_4_.refs_2_), channel_id=1, source_target_pairs={{0,8},{8,0},{1,9},{9,1},{2,10},{10,2},{3,11},{11,3},{4,12},{12,4},... | collective-permute-start | bytes 1572872 | tf_op jit(solution)/shard_map/ppermute | solution.py:48
  22.8 11.3 %collective-permute-start.4 = (bf16[2080,128]{1,0:T(8,128)(2,1)S(1)}, bf16[2080,128]{1,0:T(8,128)(2,1)S(1)}, u32[]{:S(2)}, u32[]{:S(2)}) collective-permute-start(bf16[2080,128]{1,0:T(8,128)(2,1)S(1)} %pad_maximum_fusion.1), channel_id=1, source_target_pairs={{0,3},{8,56},{1,2},{9,57},{2,1},{10,58},{3,0},{11,59},{4,7},{12,60... | collective-permute-start | bytes 1597448 | tf_op jit(solution)/shard_map/ppermute | solution.py:43

commit v7 on v6

--- a/solution.py
+++ b/solution.py
@@ -11,7 +11,7 @@
 neg_fill = -1e30
 QUERIES, TOKENS, DOCS, SLOTS, DIM = 8, 32, 8, 128, 128
 PAY = DOCS * SLOTS + 16
-LARGE, SMALL = 64, 16
+STEPS = (64, 32, 16)
 
 
 def index(x, y, z, core):
@@ -143,7 +143,7 @@
                     owner[total + k] = part * DOCS + d
                 total = total + ((facts_ref[part * 8 + d] + 15) >> 4)
         first += size
-    for k in range(SMALL):
+    for k in range(STEPS[-1]):
         owner[total + k] = doc_count
     carry[...] = jnp.full_like(carry, neg_fill)
 
@@ -167,10 +167,14 @@
                 carry[2 * b + h] = run
         return ids[-1]
 
-    large = total >> 6
-    last = lax.fori_loop(0, large, lambda i, last: step(LARGE, i * LARGE, last), jnp.int32(-1))
-    small = (total - large * LARGE + SMALL - 1) >> 4
-    lax.fori_loop(0, small, lambda i, last: step(SMALL, large * LARGE + i * SMALL, last), last)
+    base, last = jnp.int32(0), jnp.int32(-1)
+    for groups in STEPS:
+        up = groups - 1 if groups == STEPS[-1] else 0
+        count = (total - base + up) >> (groups.bit_length() - 1)
+        last = lax.fori_loop(
+            0, count, lambda i, last, groups=groups, base=base: step(groups, base + i * groups, last), last
+        )
+        base = base + count * groups
 
     for part in range(sum(sizes)):
         columns = []
@@ -210,9 +214,9 @@
         in_specs=[spec(pltpu.SMEM)] + [spec(pltpu.VMEM)] * len(operands),
         out_specs=spec(pltpu.VMEM),
         scratch_shapes=[
-            pltpu.VMEM((doc_count * SLOTS + SMALL * 16, DIM), jnp.bfloat16),
+            pltpu.VMEM((doc_count * SLOTS + STEPS[-1] * 16, DIM), jnp.bfloat16),
             pltpu.VMEM((blocks * 2, (doc_count + 1) * 8, 128), jnp.float32),
-            pltpu.SMEM((doc_count * 8 + SMALL,), jnp.int32),
+            pltpu.SMEM((doc_count * 8 + STEPS[-1],), jnp.int32),
             pltpu.VMEM((blocks * 2, 8, 128), jnp.float32),
         ]
         + ([pltpu.VMEM((128, 128), jnp.float32)] * 2 if final else []),
@@ -264,7 +268,7 @@
     query = jnp.concatenate([query, swap(query, QUERY_STEPS, 1)])
     query = jnp.concatenate([query, swap(query, QUERY_STEPS, 2)])
     near = [own, first, second, swap(first, DOC_STEPS, 1)]
-    far = [swap(jnp.concatenate(near[:2]), DOC_STEPS, 2), swap(jnp.concatenate(near[2:]), DOC_STEPS, 2)]
+    far = [swap(jnp.concatenate(near[:3]), DOC_STEPS, 2), swap(near[3], DOC_STEPS, 2)]
     queries = [query, swap_cores(query)]
     given = score(lengths_of(near), near, queries)
     given = score(lengths_of(far), far, queries, given)

time: 52.9 us -> 59.1 us (1.12)
  waiting for transfers between devices: 10.1 us -> 13.8 us
  starting transfers between devices: 14.5 us -> 16.6 us
    ppermute x8, waiting for transfers between devices: 10.1 us -> 13.8 us  [swap(): return lax.ppermute(array, 'd', pairs)]
    ppermute x8, starting transfers between devices: 14.4 us -> 16.5 us  [swap(): return lax.ppermute(array, 'd', pairs)]
  transfers between devices with their start and end apart: 9 -> 9, of which waited for: 4 -> 6; matrix products, arithmetic and copies ran while one was open for 2% -> 2% of each run, Pallas kernels for 16% -> 14%
where the time goes in v7:
time: 59.1 us; the launch traced here: 58.3 us
  Pallas kernels  17.7 us (30%)
  starting transfers between devices  16.6 us (28%)
  waiting for transfers between devices  13.8 us (23%)
  blocking collectives  8.91 us (15%)
  other arithmetic  1 us (2%)
    ppermute x8, starting transfers between devices, swap(): return lax.ppermute(array, 'd', pairs)  16.5 us
    pallas_call x2, Pallas kernels, score(): pl.pallas_call(functools.partial(score_kernel, sizes, blocks, final), out...  15.1 us
    ppermute x8, waiting for transfers between devices, swap(): return lax.ppermute(array, 'd', pairs)  13.8 us
    all_to_all x1, blocking collectives, local(): lax.all_to_all(given, 'd', 0, 0, tiled=True, axis_index_groups=owner_grou...  8.91 us
    pallas_call x1, Pallas kernels, finish(): pl.pallas_call(finish_kernel, out_shape=jax.ShapeDtypeStruct((QUERIES,),...  1.57 us
  transfers between devices with their start and end apart: 9, of which 6 were waited for; matrix products, arithmetic and copies ran while one was open for 2% of the time, Pallas kernels for 14%

profile of v7, /device:TPU:0, one launch (start us, length us, event | category | flops | bytes accessed | tf_op | source)
XLA Modules:
  0.0 58.3 jit_solution(5760775879855835417)
XLA Ops:
  0.0 1.6 %collective-permute-start.5 = (bf16[256,128]{1,0:T(8,128)(2,1)}, bf16[256,128]{1,0:T(8,128)(2,1)S(1)}, u32[]{:S(2)}, u32[]{:S(2)}) collective-permute-start(bf16[256,128]{1,0:T(8,128)(2,1)} %bitcast.1), channel_id=1, source_target_pairs={{0,16},{8,12},{1,17},{9,13},{2,18},{10,14},{3,19},{11,15},{4,20},{... | collective-permute-start | bytes 196616 | tf_op jit(solution)/shard_map/ppermute | solution.py:43
  1.6 1.0 %pack.1 = (bf16[1040,128]{1,0:T(8,128)(2,1)S(1)}, bf16[256,128]{1,0:T(8,128)(2,1)S(1)}) custom-call(s32[8]{0:T(128)} %lengths_ref.1, bf16[8,128,128]{2,1,0:T(8,128)(2,1)} %docs_ref.1, bf16[256,128]{1,0:T(8,128)(2,1)} %bitcast.2), custom_call_target="tpu_custom_call" | custom-call | flops 1000000 | bytes 1000000 | tf_op jit(solution)/shard_map/pack/pallas_call | solution.py:85
  2.6 1.8 %collective-permute-done.5 = bf16[256,128]{1,0:T(8,128)(2,1)S(1)} collective-permute-done((bf16[256,128]{1,0:T(8,128)(2,1)}, bf16[256,128]{1,0:T(8,128)(2,1)S(1)}, u32[]{:S(2)}, u32[]{:S(2)}) %collective-permute-start.5) | collective-permute-done | bytes 65568 | tf_op jit(solution)/shard_map/ppermute | solution.py:43
  4.5 1.8 %collective-permute-start.6 = (bf16[512,128]{1,0:T(8,128)(2,1)S(1)}, bf16[512,128]{1,0:T(8,128)(2,1)S(1)}, u32[]{:S(2)}, u32[]{:S(2)}) collective-permute-start(bf16[512,128]{1,0:T(8,128)(2,1)S(1)} %pad_maximum_fusion.2), channel_id=1, source_target_pairs={{0,4},{8,9},{1,5},{9,8},{2,6},{10,11},{3,7},{11,10},{4,0},{12,13},... | collective-permute-start | bytes 393224 | tf_op jit(solution)/shard_map/ppermute | solution.py:43
  6.3 2.8 %collective-permute-start = (bf16[1040,128]{1,0:T(8,128)(2,1)S(1)}, bf16[1040,128]{1,0:T(8,128)(2,1)S(1)}, u32[]{:S(2)}, u32[]{:S(2)}) collective-permute-start(bf16[1040,128]{1,0:T(8,128)(2,1)S(1)} %get-tuple-element.7.refs_0_), channel_id=1, source_target_pairs={{0,48},{8,76},{1,49},{9,77},{2,50},{10,78},{3,51},{11,79},{4,52},{... | collective-permute-start | bytes 798728 | tf_op jit(solution)/shard_map/ppermute | solution.py:43
  9.0 2.2 %collective-permute-start.1 = (bf16[1040,128]{1,0:T(8,128)(2,1)S(1)}, bf16[1040,128]{1,0:T(8,128)(2,1)S(1)}, u32[]{:S(2)}, u32[]{:S(2)}) collective-permute-start(bf16[1040,128]{1,0:T(8,128)(2,1)S(1)} %get-tuple-element.7.refs_0_), channel_id=1, source_target_pairs={{0,68},{8,11},{1,69},{9,10},{2,70},{10,9},{3,71},{11,8},{4,64},{12... | collective-permute-start | bytes 798728 | tf_op jit(solution)/shard_map/ppermute | solution.py:43
  11.2 0.0 collective-permute-done.6
  11.2 2.0 %collective-permute-start.7 = (bf16[1024,128]{1,0:T(8,128)(2,1)S(1)}, bf16[1024,128]{1,0:T(8,128)(2,1)S(1)}, u32[]{:S(2)}, u32[]{:S(2)}) collective-permute-start(bf16[1024,128]{1,0:T(8,128)(2,1)S(1)} %pad_maximum_fusion.1), channel_id=1, source_target_pairs={{0,1},{8,24},{1,0},{9,25},{2,3},{10,26},{3,2},{11,27},{4,5},{12,28... | collective-permute-start | bytes 786440 | tf_op jit(solution)/shard_map/ppermute | solution.py:43
  13.2 0.7 %collective-permute-done.refs_1_ = bf16[1040,128]{1,0:T(8,128)(2,1)S(1)} collective-permute-done((bf16[1040,128]{1,0:T(8,128)(2,1)S(1)}, bf16[1040,128]{1,0:T(8,128)(2,1)S(1)}, u32[]{:S(2)}, u32[]{:S(2)}) %collective-permute-start) | collective-permute-done | bytes 266272 | tf_op jit(solution)/shard_map/ppermute | solution.py:43
  13.9 2.2 %collective-permute-start.3 = (bf16[1040,128]{1,0:T(8,128)(2,1)S(1)}, bf16[1040,128]{1,0:T(8,128)(2,1)S(1)}, u32[]{:S(2)}, u32[]{:S(2)}) collective-permute-start(bf16[1040,128]{1,0:T(8,128)(2,1)S(1)} %collective-permute-done.refs_1_), channel_id=1, source_target_pairs={{0,68},{8,11},{1,69},{9,10},{2,70},{10,9},{3,71},{11,8},{4,64},{12... | collective-permute-start | bytes 798728 | tf_op jit(solution)/shard_map/ppermute | solution.py:43
  16.1 1.6 %collective-permute-done.7 = bf16[1024,128]{1,0:T(8,128)(2,1)S(1)} collective-permute-done((bf16[1024,128]{1,0:T(8,128)(2,1)S(1)}, bf16[1024,128]{1,0:T(8,128)(2,1)S(1)}, u32[]{:S(2)}, u32[]{:S(2)}) %collective-permute-start.7) | collective-permute-done | bytes 262176 | tf_op jit(solution)/shard_map/ppermute | solution.py:43
  17.7 0.1 collective-permute-start.8
  17.8 3.7 %collective-permute-done.3.refs_3_ = bf16[1040,128]{1,0:T(8,128)(2,1)S(1)} collective-permute-done((bf16[1040,128]{1,0:T(8,128)(2,1)S(1)}, bf16[1040,128]{1,0:T(8,128)(2,1)S(1)}, u32[]{:S(2)}, u32[]{:S(2)}) %collective-permute-start.3) | collective-permute-done | bytes 266272 | tf_op jit(solution)/shard_map/ppermute | solution.py:43
  21.5 4.0 %collective-permute-start.4 = (bf16[1040,128]{1,0:T(8,128)(2,1)S(1)}, bf16[1040,128]{1,0:T(8,128)(2,1)S(1)}, u32[]{:S(2)}, u32[]{:S(2)}) collective-permute-start(bf16[1040,128]{1,0:T(8,128)(2,1)S(1)} %collective-permute-done.3.refs_3_), channel_id=1, source_target_pairs={{0,3},{8,56},{1,2},{9,57},{2,1},{10,58},{3,0},{11,59},{4,7},{12,60... | collective-permute-start | bytes 798728 | tf_op jit(solution)/shard_map/ppermute | solution.py:43
  25.6 0.0 collective-permute-done.1.refs_2_
  25.6 0.9 %pad_maximum_fusion = bf16[3120,128]{1,0:T(8,128)(2,1)} fusion(bf16[1040,128]{1,0:T(8,128)(2,1)S(1)} %collective-permute-done.1.refs_2_, bf16[1040,128]{1,0:T(8,128)(2,1)S(1)} %collective-permute-done.refs_1_, bf16[1040,128]{1,0:T(8,128)(2,1)S(1)} %get-tuple-element.7.refs_0_), kind=kLoop, calls=%fused_computation | loop fusion | flops 2396160 | bytes 1597440 | tf_op jit(solution)/shard_map/concatenate | solution.py:271
  26.5 0.0 collective-permute-start.2
  26.5 0.1 reshape.13.facts_ref
  26.6 3.3 %collective-permute-done.4.refs_1_ = bf16[1040,128]{1,0:T(8,128)(2,1)S(1)} collective-permute-done((bf16[1040,128]{1,0:T(8,128)(2,1)S(1)}, bf16[1040,128]{1,0:T(8,128)(2,1)S(1)}, u32[]{:S(2)}, u32[]{:S(2)}) %collective-permute-start.4) | collective-permute-done | bytes 266272 | tf_op jit(solution)/shard_map/ppermute | solution.py:43
  29.9 0.0 collective-permute-done.8.refs_5_.refs_3_
  29.9 7.4 %score.2.refs_4_ = f32[32,128]{1,0:T(8,128)S(1)} custom-call(s32[32]{0:T(128)S(1)} %reshape.13.facts_ref, bf16[1040,128]{1,0:T(8,128)(2,1)S(1)} %get-tuple-element.7.refs_0_, bf16[1040,128]{1,0:T(8,128)(2,1)S(1)} %collective-permute-done.refs_1_, bf16[1040,128]{1,0:T(8,128)(2,1)S(1)} %collective-permute-done.1.refs_2_, ...), custom_call_target="tpu_custom_call" | custom-call | flops 6000000000 | bytes 1000000 | tf_op jit(solution)/shard_map/score/pallas_call | solution.py:211
  37.3 2.7 %collective-permute-done.2.refs_0_ = bf16[3120,128]{1,0:T(8,128)(2,1)S(1)} collective-permute-done((bf16[3120,128]{1,0:T(8,128)(2,1)}, bf16[3120,128]{1,0:T(8,128)(2,1)S(1)}, u32[]{:S(2)}, u32[]{:S(2)}) %collective-permute-start.2) | collective-permute-done | bytes 798752 | tf_op jit(solution)/shard_map/ppermute | solution.py:43
  40.1 0.1 reshape.12.facts_ref
  40.2 7.7 %score.3 = f32[16,8,128]{2,1,0:T(8,128)S(1)} custom-call(s32[32]{0:T(128)S(1)} %reshape.12.facts_ref, bf16[3120,128]{1,0:T(8,128)(2,1)S(1)} %collective-permute-done.2.refs_0_, bf16[1040,128]{1,0:T(8,128)(2,1)S(1)} %collective-permute-done.4.refs_1_, bf16[2048,128]{1,0:T(8,128)(2,1)S(1)} %constant_dynamic-update-slice_fusion.refs_4_.refs_2_, ...), custom_call_target="tpu_custom_call" | custom-call | flops 6000000000 | bytes 1000000 | tf_op jit(solution)/shard_map/score/pallas_call | solution.py:211
  47.9 8.9 %all_to_all.5.given_ref = f32[16,8,128]{2,1,0:T(8,128)} all-to-all(f32[16,8,128]{2,1,0:T(8,128)S(1)} %score.3), channel_id=1, replica_groups={{0,16,4,20,1,17,5,21,8,24,12,28,9,25,13,29},{3,19,7,23,2,18,6,22,11,27,..., dimensions={0} | all-to-all | bytes 131072 | tf_op jit(solution)/shard_map/all_to_all | solution.py:275
  56.8 1.6 %finish.1 = f32[8]{0:T(128)} custom-call(s32[8]{0:T(128)} %positives_ref.1, f32[16,8,128]{2,1,0:T(8,128)} %all_to_all.5.given_ref), custom_call_target="tpu_custom_call" | custom-call | tf_op jit(solution)/shard_map/finish/pallas_call | solution.py:252
  (14 shorter events, 0.1 us)
Async XLA Ops:
  0.0 4.5 %collective-permute-start.5 = (bf16[256,128]{1,0:T(8,128)(2,1)}, bf16[256,128]{1,0:T(8,128)(2,1)S(1)}, u32[]{:S(2)}, u32[]{:S(2)}) collective-permute-start(bf16[256,128]{1,0:T(8,128)(2,1)} %bitcast.1), channel_id=1, source_target_pairs={{0,16},{8,12},{1,17},{9,13},{2,18},{10,14},{3,19},{11,15},{4,20},{... | collective-permute-start | bytes 196616 | tf_op jit(solution)/shard_map/ppermute | solution.py:43
  4.5 6.7 %collective-permute-start.6 = (bf16[512,128]{1,0:T(8,128)(2,1)S(1)}, bf16[512,128]{1,0:T(8,128)(2,1)S(1)}, u32[]{:S(2)}, u32[]{:S(2)}) collective-permute-start(bf16[512,128]{1,0:T(8,128)(2,1)S(1)} %pad_maximum_fusion.2), channel_id=1, source_target_pairs={{0,4},{8,9},{1,5},{9,8},{2,6},{10,11},{3,7},{11,10},{4,0},{12,13},... | collective-permute-start | bytes 393224 | tf_op jit(solution)/shard_map/ppermute | solution.py:43
  6.3 7.6 %collective-permute-start = (bf16[1040,128]{1,0:T(8,128)(2,1)S(1)}, bf16[1040,128]{1,0:T(8,128)(2,1)S(1)}, u32[]{:S(2)}, u32[]{:S(2)}) collective-permute-start(bf16[1040,128]{1,0:T(8,128)(2,1)S(1)} %get-tuple-element.7.refs_0_), channel_id=1, source_target_pairs={{0,48},{8,76},{1,49},{9,77},{2,50},{10,78},{3,51},{11,79},{4,52},{... | collective-permute-start | bytes 798728 | tf_op jit(solution)/shard_map/ppermute | solution.py:43
  9.0 16.5 %collective-permute-start.1 = (bf16[1040,128]{1,0:T(8,128)(2,1)S(1)}, bf16[1040,128]{1,0:T(8,128)(2,1)S(1)}, u32[]{:S(2)}, u32[]{:S(2)}) collective-permute-start(bf16[1040,128]{1,0:T(8,128)(2,1)S(1)} %get-tuple-element.7.refs_0_), channel_id=1, source_target_pairs={{0,68},{8,11},{1,69},{9,10},{2,70},{10,9},{3,71},{11,8},{4,64},{12... | collective-permute-start | bytes 798728 | tf_op jit(solution)/shard_map/ppermute | solution.py:43
  11.2 6.5 %collective-permute-start.7 = (bf16[1024,128]{1,0:T(8,128)(2,1)S(1)}, bf16[1024,128]{1,0:T(8,128)(2,1)S(1)}, u32[]{:S(2)}, u32[]{:S(2)}) collective-permute-start(bf16[1024,128]{1,0:T(8,128)(2,1)S(1)} %pad_maximum_fusion.1), channel_id=1, source_target_pairs={{0,1},{8,24},{1,0},{9,25},{2,3},{10,26},{3,2},{11,27},{4,5},{12,28... | collective-permute-start | bytes 786440 | tf_op jit(solution)/shard_map/ppermute | solution.py:43
  13.9 7.6 %collective-permute-start.3 = (bf16[1040,128]{1,0:T(8,128)(2,1)S(1)}, bf16[1040,128]{1,0:T(8,128)(2,1)S(1)}, u32[]{:S(2)}, u32[]{:S(2)}) collective-permute-start(bf16[1040,128]{1,0:T(8,128)(2,1)S(1)} %collective-permute-done.refs_1_), channel_id=1, source_target_pairs={{0,68},{8,11},{1,69},{9,10},{2,70},{10,9},{3,71},{11,8},{4,64},{12... | collective-permute-start | bytes 798728 | tf_op jit(solution)/shard_map/ppermute | solution.py:43
  17.7 12.2 %collective-permute-start.8 = (bf16[2048,128]{1,0:T(8,128)(2,1)S(1)}, bf16[2048,128]{1,0:T(8,128)(2,1)S(1)}, u32[]{:S(2)}, u32[]{:S(2)}) collective-permute-start(bf16[2048,128]{1,0:T(8,128)(2,1)S(1)} %constant_dynamic-update-slice_fusion.refs_4_.refs_2_), channel_id=1, source_target_pairs={{0,8},{8,0},{1,9},{9,1},{2,10},{10,2},{3,11},{11,3},{4,12},{12,4},... | collective-permute-start | bytes 1572872 | tf_op jit(solution)/shard_map/ppermute | solution.py:48
  21.5 8.4 %collective-permute-start.4 = (bf16[1040,128]{1,0:T(8,128)(2,1)S(1)}, bf16[1040,128]{1,0:T(8,128)(2,1)S(1)}, u32[]{:S(2)}, u32[]{:S(2)}) collective-permute-start(bf16[1040,128]{1,0:T(8,128)(2,1)S(1)} %collective-permute-done.3.refs_3_), channel_id=1, source_target_pairs={{0,3},{8,56},{1,2},{9,57},{2,1},{10,58},{3,0},{11,59},{4,7},{12,60... | collective-permute-start | bytes 798728 | tf_op jit(solution)/shard_map/ppermute | solution.py:43
  26.5 13.5 %collective-permute-start.2 = (bf16[3120,128]{1,0:T(8,128)(2,1)}, bf16[3120,128]{1,0:T(8,128)(2,1)S(1)}, u32[]{:S(2)}, u32[]{:S(2)}) collective-permute-start(bf16[3120,128]{1,0:T(8,128)(2,1)} %pad_maximum_fusion), channel_id=1, source_target_pairs={{0,3},{8,56},{1,2},{9,57},{2,1},{10,58},{3,0},{11,59},{4,7},{12,60... | collective-permute-start | bytes 2396168 | tf_op jit(solution)/shard_map/ppermute | solution.py:43

commit v8 on v7

--- a/solution.py
+++ b/solution.py
@@ -11,7 +11,7 @@
 neg_fill = -1e30
 QUERIES, TOKENS, DOCS, SLOTS, DIM = 8, 32, 8, 128, 128
 PAY = DOCS * SLOTS + 16
-STEPS = (64, 32, 16)
+STEPS = (64, 16)
 
 
 def index(x, y, z, core):
@@ -90,6 +90,23 @@
         cost_estimate=pl.CostEstimate(flops=10**6, bytes_accessed=10**6, transcendentals=0),
         name="pack",
     )(lengths, docs, queries)
+
+
+def join_kernel(a_ref, b_ref, out_ref):
+    count = a_ref.shape[0]
+    out_ref[:count, :] = a_ref[...]
+    out_ref[count:, :] = b_ref[...]
+
+
+def join(a, b):
+    return pl.pallas_call(
+        join_kernel,
+        out_shape=pltpu.VMEM((a.shape[0] + b.shape[0], DIM), jnp.bfloat16),
+        in_specs=[spec(pltpu.VMEM), spec(pltpu.VMEM)],
+        out_specs=spec(pltpu.VMEM),
+        cost_estimate=pl.CostEstimate(flops=10**6, bytes_accessed=10**6, transcendentals=0),
+        name="join",
+    )(a, b)
 
 
 def lower_half(shift, axis):
@@ -264,11 +281,12 @@
     own, query = pack(lengths, documents, query)
     first = swap(own, DOC_STEPS, 0)
     second = swap(own, DOC_STEPS, 1)
+    third = swap(own, DOC_STEPS, 2)
     query = jnp.concatenate([query, got])
     query = jnp.concatenate([query, swap(query, QUERY_STEPS, 1)])
     query = jnp.concatenate([query, swap(query, QUERY_STEPS, 2)])
     near = [own, first, second, swap(first, DOC_STEPS, 1)]
-    far = [swap(jnp.concatenate(near[:3]), DOC_STEPS, 2), swap(near[3], DOC_STEPS, 2)]
+    far = [third, swap(join(first, second), DOC_STEPS, 2), swap(near[3], DOC_STEPS, 2)]
     queries = [query, swap_cores(query)]
     given = score(lengths_of(near), near, queries)
     given = score(lengths_of(far), far, queries, given)

time: 59.1 us -> 58.8 us (level)
  waiting for transfers between devices: 13.8 us -> 6.44 us
  starting transfers between devices: 16.6 us -> 21.2 us
  local copies, waits for them, and re-layouts: 0.25 us -> 1.62 us
  Pallas kernels: 17.7 us -> 19 us
    ppermute x8 -> x9, waiting for transfers between devices: 13.8 us -> 6.44 us  [swap(): return lax.ppermute(array, 'd', pairs)]
    ppermute x8 -> x9, starting transfers between devices: 16.5 us -> 21.1 us  [swap(): return lax.ppermute(array, 'd', pairs)]
    pallas_call x0 -> x1, Pallas kernels: none -> 1.07 us  [join(): pl.pallas_call(join_kernel, out_shape=pltpu.VMEM((a.shape[0] + b.shape[0]...]
    concatenate x1 -> x0, other arithmetic: 0.95 us -> none  [local(): jnp.concatenate(near[:3])]
    concatenate x1, other arithmetic: 0.02 us -> 0.73 us  [local(): query = jnp.concatenate([query, swap(query, QUERY_STEPS, 1)])]
    unnamed x3 -> x7, local copies, waits for them, and re-layouts: 0.04 us -> 0.74 us
    slice x6 -> x7, local copies, waits for them, and re-layouts: 0.01 us -> 0.69 us  [lengths_of(): d[(k + 1) * PAY - 16, :DOCS]]
  transfers between devices with their start and end apart: 9 -> 10, of which waited for: 6 -> 1; matrix products, arithmetic and copies ran while one was open for 2% -> 3% of each run, Pallas kernels for 14% -> 4%
where the time goes in v8:
time: 58.8 us; the launch traced here: 58 us
  starting transfers between devices  21.2 us (36%)
  Pallas kernels  19 us (32%)
  blocking collectives  8.9 us (15%)
  waiting for transfers between devices  6.44 us (11%)
  local copies, waits for them, and re-layouts  1.62 us (3%)
  other arithmetic  0.77 us (1%)
    ppermute x9, starting transfers between devices, swap(): return lax.ppermute(array, 'd', pairs)  21.1 us
    pallas_call x2, Pallas kernels, score(): pl.pallas_call(functools.partial(score_kernel, sizes, blocks, final), out...  15.3 us
    all_to_all x1, blocking collectives, local(): lax.all_to_all(given, 'd', 0, 0, tiled=True, axis_index_groups=owner_grou...  8.9 us
    ppermute x9, waiting for transfers between devices, swap(): return lax.ppermute(array, 'd', pairs)  6.44 us
    pallas_call x1, Pallas kernels, finish(): pl.pallas_call(finish_kernel, out_shape=jax.ShapeDtypeStruct((QUERIES,),...  1.57 us
  transfers between devices with their start and end apart: 10, of which 1 were waited for; matrix products, arithmetic and copies ran while one was open for 3% of the time, Pallas kernels for 4%

profile of v8, /device:TPU:0, one launch (start us, length us, event | category | flops | bytes accessed | tf_op | source)
XLA Modules:
  0.0 58.0 jit_solution(6658431540914660031)
XLA Ops:
  0.0 1.6 %collective-permute-start.6 = (bf16[256,128]{1,0:T(8,128)(2,1)}, bf16[256,128]{1,0:T(8,128)(2,1)S(1)}, u32[]{:S(2)}, u32[]{:S(2)}) collective-permute-start(bf16[256,128]{1,0:T(8,128)(2,1)} %bitcast.1), channel_id=1, source_target_pairs={{0,16},{8,12},{1,17},{9,13},{2,18},{10,14},{3,19},{11,15},{4,20},{... | collective-permute-start | bytes 196616 | tf_op jit(solution)/shard_map/ppermute | solution.py:43
  1.6 1.0 %pack.1 = (bf16[1040,128]{1,0:T(8,128)(2,1)S(1)}, bf16[256,128]{1,0:T(8,128)(2,1)S(1)}) custom-call(s32[8]{0:T(128)} %lengths_ref.1, bf16[8,128,128]{2,1,0:T(8,128)(2,1)} %docs_ref.1, bf16[256,128]{1,0:T(8,128)(2,1)} %bitcast.2), custom_call_target="tpu_custom_call" | custom-call | flops 1000000 | bytes 1000000 | tf_op jit(solution)/shard_map/pack/pallas_call | solution.py:85
  2.6 2.2 %collective-permute-start.1 = (bf16[1040,128]{1,0:T(8,128)(2,1)S(1)}, bf16[1040,128]{1,0:T(8,128)(2,1)}, u32[]{:S(2)}, u32[]{:S(2)}) collective-permute-start(bf16[1040,128]{1,0:T(8,128)(2,1)S(1)} %get-tuple-element.7.refs_0_), channel_id=1, source_target_pairs={{0,48},{8,76},{1,49},{9,77},{2,50},{10,78},{3,51},{11,79},{4,52},{... | collective-permute-start | bytes 798728 | tf_op jit(solution)/shard_map/ppermute | solution.py:43
  4.8 0.0 collective-permute-done.6
  4.8 1.7 %collective-permute-start.7 = (bf16[512,128]{1,0:T(8,128)(2,1)S(1)}, bf16[512,128]{1,0:T(8,128)(2,1)S(1)}, u32[]{:S(2)}, u32[]{:S(2)}) collective-permute-start(bf16[512,128]{1,0:T(8,128)(2,1)S(1)} %pad_maximum_fusion.1), channel_id=1, source_target_pairs={{0,4},{8,9},{1,5},{9,8},{2,6},{10,11},{3,7},{11,10},{4,0},{12,13},... | collective-permute-start | bytes 393224 | tf_op jit(solution)/shard_map/ppermute | solution.py:43
  6.5 2.2 %collective-permute-start.2 = (bf16[1040,128]{1,0:T(8,128)(2,1)S(1)}, bf16[1040,128]{1,0:T(8,128)(2,1)S(1)}, u32[]{:S(2)}, u32[]{:S(2)}) collective-permute-start(bf16[1040,128]{1,0:T(8,128)(2,1)S(1)} %get-tuple-element.7.refs_0_), channel_id=1, source_target_pairs={{0,68},{8,11},{1,69},{9,10},{2,70},{10,9},{3,71},{11,8},{4,64},{12... | collective-permute-start | bytes 798728 | tf_op jit(solution)/shard_map/ppermute | solution.py:43
  8.7 4.0 %collective-permute-start = (bf16[1040,128]{1,0:T(8,128)(2,1)S(1)}, bf16[1040,128]{1,0:T(8,128)(2,1)S(1)}, u32[]{:S(2)}, u32[]{:S(2)}) collective-permute-start(bf16[1040,128]{1,0:T(8,128)(2,1)S(1)} %get-tuple-element.7.refs_0_), channel_id=1, source_target_pairs={{0,3},{8,56},{1,2},{9,57},{2,1},{10,58},{3,0},{11,59},{4,7},{12,60... | collective-permute-start | bytes 798728 | tf_op jit(solution)/shard_map/ppermute | solution.py:43
  12.7 0.0 collective-permute-done.7
  12.7 0.7 %pad_maximum_fusion = bf16[1024,128]{1,0:T(8,128)(2,1)} fusion(bf16[512,128]{1,0:T(8,128)(2,1)S(1)} %collective-permute-done.7, bf16[256,128]{1,0:T(8,128)(2,1)S(1)} %collective-permute-done.6, bf16[256,128]{1,0:T(8,128)(2,1)S(1)} %get-tuple-element.8), kind=kLoop, calls=%fused_computation | loop fusion | flops 786432 | bytes 524288 | tf_op jit(solution)/shard_map/concatenate | solution.py:286
  13.4 0.0 collective-permute-start.8
  13.4 0.0 collective-permute-done.1.a_ref.refs_1_
  13.5 2.1 %collective-permute-start.4 = (bf16[1040,128]{1,0:T(8,128)(2,1)}, bf16[1040,128]{1,0:T(8,128)(2,1)S(1)}, u32[]{:S(2)}, u32[]{:S(2)}) collective-permute-start(bf16[1040,128]{1,0:T(8,128)(2,1)} %collective-permute-done.1.a_ref.refs_1_), channel_id=1, source_target_pairs={{0,68},{8,11},{1,69},{9,10},{2,70},{10,9},{3,71},{11,8},{4,64},{12... | collective-permute-start | bytes 798728 | tf_op jit(solution)/shard_map/ppermute | solution.py:43
  15.6 0.0 collective-permute-done.2.b_ref.refs_2_
  15.6 0.0 copy-start
  15.6 0.7 %copy-done = bf16[1040,128]{1,0:T(8,128)(2,1)} copy-done((bf16[1040,128]{1,0:T(8,128)(2,1)}, bf16[1040,128]{1,0:T(8,128)(2,1)S(1)}, u32[]{:S(2)}) %copy-start) | copy-done | bytes 266264
  16.3 1.1 %join.1 = bf16[2080,128]{1,0:T(8,128)(2,1)S(1)} custom-call(bf16[1040,128]{1,0:T(8,128)(2,1)} %collective-permute-done.1.a_ref.refs_1_, bf16[1040,128]{1,0:T(8,128)(2,1)} %copy-done), custom_call_target="tpu_custom_call" | custom-call | flops 1000000 | bytes 1000000 | tf_op jit(solution)/shard_map/join/pallas_call | solution.py:102
  17.3 4.7 %collective-permute-start.3 = (bf16[2080,128]{1,0:T(8,128)(2,1)S(1)}, bf16[2080,128]{1,0:T(8,128)(2,1)S(1)}, u32[]{:S(2)}, u32[]{:S(2)}) collective-permute-start(bf16[2080,128]{1,0:T(8,128)(2,1)S(1)} %join.1), channel_id=1, source_target_pairs={{0,3},{8,56},{1,2},{9,57},{2,1},{10,58},{3,0},{11,59},{4,7},{12,60... | collective-permute-start | bytes 1597448 | tf_op jit(solution)/shard_map/ppermute | solution.py:43
  22.0 0.0 copy-start.1
  22.0 0.0 collective-permute-done.4.refs_3_
  22.1 2.7 %collective-permute-start.5 = (bf16[1040,128]{1,0:T(8,128)(2,1)S(1)}, bf16[1040,128]{1,0:T(8,128)(2,1)S(1)}, u32[]{:S(2)}, u32[]{:S(2)}) collective-permute-start(bf16[1040,128]{1,0:T(8,128)(2,1)S(1)} %collective-permute-done.4.refs_3_), channel_id=1, source_target_pairs={{0,3},{8,56},{1,2},{9,57},{2,1},{10,58},{3,0},{11,59},{4,7},{12,60... | collective-permute-start | bytes 798728 | tf_op jit(solution)/shard_map/ppermute | solution.py:43
  24.7 0.0 collective-permute-done.8
  24.8 0.1 collective-permute-start.9
  24.9 0.7 %slice.36 = bf16[1,8]{1,0:T(2,128)(2,1)S(1)} slice(bf16[1040,128]{1,0:T(8,128)(2,1)} %collective-permute-done.1.a_ref.refs_1_), slice={[1024:1025], [0:8]} | slice | bytes 32 | tf_op jit(solution)/shard_map/slice | solution.py:247
  25.5 0.0 copy-done.1
  25.6 0.0 collective-permute-done.refs_0_
  25.6 0.1 reshape.13.facts_ref
  25.7 6.4 %collective-permute-done.5.refs_2_ = bf16[1040,128]{1,0:T(8,128)(2,1)S(1)} collective-permute-done((bf16[1040,128]{1,0:T(8,128)(2,1)S(1)}, bf16[1040,128]{1,0:T(8,128)(2,1)S(1)}, u32[]{:S(2)}, u32[]{:S(2)}) %collective-permute-start.5) | collective-permute-done | bytes 266272 | tf_op jit(solution)/shard_map/ppermute | solution.py:43
  32.1 0.0 collective-permute-done.3.refs_1_
  32.1 0.1 reshape.12.facts_ref
  32.2 0.0 collective-permute-done.9.refs_5_.refs_4_
  32.2 7.8 %score.2.refs_5_ = f32[32,128]{1,0:T(8,128)S(1)} custom-call(s32[32]{0:T(128)S(1)} %reshape.13.facts_ref, bf16[1040,128]{1,0:T(8,128)(2,1)S(1)} %get-tuple-element.7.refs_0_, bf16[1040,128]{1,0:T(8,128)(2,1)} %collective-permute-done.1.a_ref.refs_1_, bf16[1040,128]{1,0:T(8,128)(2,1)S(1)} %copy-done.1, bf16[1040,128]{1,0:T(8,128)(2,1)S(1)} %collective-permute-done.4.refs_3_, ...), custom_call_target="tpu_custom_call" | custom-call | flops 6000000000 | bytes 1000000 | tf_op jit(solution)/shard_map/score/pallas_call | solution.py:228
  40.0 7.5 %score.3 = f32[16,8,128]{2,1,0:T(8,128)S(1)} custom-call(s32[32]{0:T(128)S(1)} %reshape.12.facts_ref, bf16[1040,128]{1,0:T(8,128)(2,1)S(1)} %collective-permute-done.refs_0_, bf16[2080,128]{1,0:T(8,128)(2,1)S(1)} %collective-permute-done.3.refs_1_, bf16[1040,128]{1,0:T(8,128)(2,1)S(1)} %collective-permute-done.5.refs_2_, ...), custom_call_target="tpu_custom_call" | custom-call | flops 6000000000 | bytes 1000000 | tf_op jit(solution)/shard_map/score/pallas_call | solution.py:228
  47.5 8.9 %all_to_all.5.given_ref = f32[16,8,128]{2,1,0:T(8,128)} all-to-all(f32[16,8,128]{2,1,0:T(8,128)S(1)} %score.3), channel_id=1, replica_groups={{0,16,4,20,1,17,5,21,8,24,12,28,9,25,13,29},{3,19,7,23,2,18,6,22,11,27,..., dimensions={0} | all-to-all | bytes 131072 | tf_op jit(solution)/shard_map/all_to_all | solution.py:293
  56.4 1.6 %finish.1 = f32[8]{0:T(128)} custom-call(s32[8]{0:T(128)} %positives_ref.1, f32[16,8,128]{2,1,0:T(8,128)} %all_to_all.5.given_ref), custom_call_target="tpu_custom_call" | custom-call | tf_op jit(solution)/shard_map/finish/pallas_call | solution.py:269
  (13 shorter events, 0.1 us)
Async XLA Ops:
  0.0 4.8 %collective-permute-start.6 = (bf16[256,128]{1,0:T(8,128)(2,1)}, bf16[256,128]{1,0:T(8,128)(2,1)S(1)}, u32[]{:S(2)}, u32[]{:S(2)}) collective-permute-start(bf16[256,128]{1,0:T(8,128)(2,1)} %bitcast.1), channel_id=1, source_target_pairs={{0,16},{8,12},{1,17},{9,13},{2,18},{10,14},{3,19},{11,15},{4,20},{... | collective-permute-start | bytes 196616 | tf_op jit(solution)/shard_map/ppermute | solution.py:43
  2.6 10.8 %collective-permute-start.1 = (bf16[1040,128]{1,0:T(8,128)(2,1)S(1)}, bf16[1040,128]{1,0:T(8,128)(2,1)}, u32[]{:S(2)}, u32[]{:S(2)}) collective-permute-start(bf16[1040,128]{1,0:T(8,128)(2,1)S(1)} %get-tuple-element.7.refs_0_), channel_id=1, source_target_pairs={{0,48},{8,76},{1,49},{9,77},{2,50},{10,78},{3,51},{11,79},{4,52},{... | collective-permute-start | bytes 798728 | tf_op jit(solution)/shard_map/ppermute | solution.py:43
  4.8 7.9 %collective-permute-start.7 = (bf16[512,128]{1,0:T(8,128)(2,1)S(1)}, bf16[512,128]{1,0:T(8,128)(2,1)S(1)}, u32[]{:S(2)}, u32[]{:S(2)}) collective-permute-start(bf16[512,128]{1,0:T(8,128)(2,1)S(1)} %pad_maximum_fusion.1), channel_id=1, source_target_pairs={{0,4},{8,9},{1,5},{9,8},{2,6},{10,11},{3,7},{11,10},{4,0},{12,13},... | collective-permute-start | bytes 393224 | tf_op jit(solution)/shard_map/ppermute | solution.py:43
  6.5 9.1 %collective-permute-start.2 = (bf16[1040,128]{1,0:T(8,128)(2,1)S(1)}, bf16[1040,128]{1,0:T(8,128)(2,1)S(1)}, u32[]{:S(2)}, u32[]{:S(2)}) collective-permute-start(bf16[1040,128]{1,0:T(8,128)(2,1)S(1)} %get-tuple-element.7.refs_0_), channel_id=1, source_target_pairs={{0,68},{8,11},{1,69},{9,10},{2,70},{10,9},{3,71},{11,8},{4,64},{12... | collective-permute-start | bytes 798728 | tf_op jit(solution)/shard_map/ppermute | solution.py:43
  8.7 16.9 %collective-permute-start = (bf16[1040,128]{1,0:T(8,128)(2,1)S(1)}, bf16[1040,128]{1,0:T(8,128)(2,1)S(1)}, u32[]{:S(2)}, u32[]{:S(2)}) collective-permute-start(bf16[1040,128]{1,0:T(8,128)(2,1)S(1)} %get-tuple-element.7.refs_0_), channel_id=1, source_target_pairs={{0,3},{8,56},{1,2},{9,57},{2,1},{10,58},{3,0},{11,59},{4,7},{12,60... | collective-permute-start | bytes 798728 | tf_op jit(solution)/shard_map/ppermute | solution.py:43
  13.4 11.3 %collective-permute-start.8 = (bf16[1024,128]{1,0:T(8,128)(2,1)}, bf16[1024,128]{1,0:T(8,128)(2,1)S(1)}, u32[]{:S(2)}, u32[]{:S(2)}) collective-permute-start(bf16[1024,128]{1,0:T(8,128)(2,1)} %pad_maximum_fusion), channel_id=1, source_target_pairs={{0,1},{8,24},{1,0},{9,25},{2,3},{10,26},{3,2},{11,27},{4,5},{12,28... | collective-permute-start | bytes 786440 | tf_op jit(solution)/shard_map/ppermute | solution.py:43
  13.5 8.6 %collective-permute-start.4 = (bf16[1040,128]{1,0:T(8,128)(2,1)}, bf16[1040,128]{1,0:T(8,128)(2,1)S(1)}, u32[]{:S(2)}, u32[]{:S(2)}) collective-permute-start(bf16[1040,128]{1,0:T(8,128)(2,1)} %collective-permute-done.1.a_ref.refs_1_), channel_id=1, source_target_pairs={{0,68},{8,11},{1,69},{9,10},{2,70},{10,9},{3,71},{11,8},{4,64},{12... | collective-permute-start | bytes 798728 | tf_op jit(solution)/shard_map/ppermute | solution.py:43
  15.6 0.7 %copy-start = (bf16[1040,128]{1,0:T(8,128)(2,1)}, bf16[1040,128]{1,0:T(8,128)(2,1)S(1)}, u32[]{:S(2)}) copy-start(bf16[1040,128]{1,0:T(8,128)(2,1)S(1)} %collective-permute-done.2.b_ref.refs_2_) | copy-start | bytes 798724
  17.3 14.8 %collective-permute-start.3 = (bf16[2080,128]{1,0:T(8,128)(2,1)S(1)}, bf16[2080,128]{1,0:T(8,128)(2,1)S(1)}, u32[]{:S(2)}, u32[]{:S(2)}) collective-permute-start(bf16[2080,128]{1,0:T(8,128)(2,1)S(1)} %join.1), channel_id=1, source_target_pairs={{0,3},{8,56},{1,2},{9,57},{2,1},{10,58},{3,0},{11,59},{4,7},{12,60... | collective-permute-start | bytes 1597448 | tf_op jit(solution)/shard_map/ppermute | solution.py:43
  22.0 3.5 %copy-start.1 = (bf16[1040,128]{1,0:T(8,128)(2,1)S(1)}, bf16[1040,128]{1,0:T(8,128)(2,1)}, u32[]{:S(2)}) copy-start(bf16[1040,128]{1,0:T(8,128)(2,1)} %copy-done) | copy-start | bytes 798724
  22.1 10.0 %collective-permute-start.5 = (bf16[1040,128]{1,0:T(8,128)(2,1)S(1)}, bf16[1040,128]{1,0:T(8,128)(2,1)S(1)}, u32[]{:S(2)}, u32[]{:S(2)}) collective-permute-start(bf16[1040,128]{1,0:T(8,128)(2,1)S(1)} %collective-permute-done.4.refs_3_), channel_id=1, source_target_pairs={{0,3},{8,56},{1,2},{9,57},{2,1},{10,58},{3,0},{11,59},{4,7},{12,60... | collective-permute-start | bytes 798728 | tf_op jit(solution)/shard_map/ppermute | solution.py:43
  24.8 7.4 %collective-permute-start.9 = (bf16[2048,128]{1,0:T(8,128)(2,1)S(1)}, bf16[2048,128]{1,0:T(8,128)(2,1)S(1)}, u32[]{:S(2)}, u32[]{:S(2)}) collective-permute-start(bf16[2048,128]{1,0:T(8,128)(2,1)S(1)} %constant_dynamic-update-slice_fusion.refs_4_.refs_3_), channel_id=1, source_target_pairs={{0,8},{8,0},{1,9},{9,1},{2,10},{10,2},{3,11},{11,3},{4,12},{12,4},... | collective-permute-start | bytes 1572872 | tf_op jit(solution)/shard_map/ppermute | solution.py:48

commit v9 on v7

--- a/solution.py
+++ b/solution.py
@@ -11,7 +11,7 @@
 neg_fill = -1e30
 QUERIES, TOKENS, DOCS, SLOTS, DIM = 8, 32, 8, 128, 128
 PAY = DOCS * SLOTS + 16
-STEPS = (64, 32, 16)
+STEPS = (64, 16)
 
 
 def index(x, y, z, core):
@@ -34,7 +34,7 @@
     return ((0, 1, 1, 0) if dim[1] == "a" else (0, 0, 1, 1))[at]
 
 
-DOC_STEPS = (("xb", "yb", "zb"), ("yb", "zb", "xb"))
+DOC_STEPS = (("zb", "yb", "xb"), ("xb", "zb", "yb"))
 QUERY_STEPS = (("xa", "ya", "za"), ("ya", "za", "xa"))
 
 
@@ -264,11 +264,12 @@
     own, query = pack(lengths, documents, query)
     first = swap(own, DOC_STEPS, 0)
     second = swap(own, DOC_STEPS, 1)
+    third = swap(own, DOC_STEPS, 2)
     query = jnp.concatenate([query, got])
     query = jnp.concatenate([query, swap(query, QUERY_STEPS, 1)])
     query = jnp.concatenate([query, swap(query, QUERY_STEPS, 2)])
     near = [own, first, second, swap(first, DOC_STEPS, 1)]
-    far = [swap(jnp.concatenate(near[:3]), DOC_STEPS, 2), swap(near[3], DOC_STEPS, 2)]
+    far = [third, swap(jnp.concatenate(near[1:3]), DOC_STEPS, 2), swap(near[3], DOC_STEPS, 2)]
     queries = [query, swap_cores(query)]
     given = score(lengths_of(near), near, queries)
     given = score(lengths_of(far), far, queries, given)

time: 59.1 us -> 60.1 us (1.017)
    ppermute x8 -> x9, starting transfers between devices: 16.5 us -> 17 us  [swap(): return lax.ppermute(array, 'd', pairs)]
    ppermute x8 -> x9, waiting for transfers between devices: 13.8 us -> 13.9 us  [swap(): return lax.ppermute(array, 'd', pairs)]
  transfers between devices with their start and end apart: 9 -> 10, of which waited for: 6 -> 3; matrix products, arithmetic and copies ran while one was open for 2% -> 2% of each run, Pallas kernels for 14% -> 2%
where the time goes in v9:
time: 60.1 us; the launch traced here: 59.4 us
  Pallas kernels  18.2 us (30%)
  starting transfers between devices  17.1 us (28%)
  waiting for transfers between devices  13.9 us (23%)
  blocking collectives  8.9 us (15%)
  other arithmetic  0.88 us (1%)
    ppermute x9, starting transfers between devices, swap(): return lax.ppermute(array, 'd', pairs)  17 us
    pallas_call x2, Pallas kernels, score(): pl.pallas_call(functools.partial(score_kernel, sizes, blocks, final), out...  15.6 us
    ppermute x9, waiting for transfers between devices, swap(): return lax.ppermute(array, 'd', pairs)  13.9 us
    all_to_all x1, blocking collectives, local(): lax.all_to_all(given, 'd', 0, 0, tiled=True, axis_index_groups=owner_grou...  8.9 us
    pallas_call x1, Pallas kernels, finish(): pl.pallas_call(finish_kernel, out_shape=jax.ShapeDtypeStruct((QUERIES,),...  1.57 us
  transfers between devices with their start and end apart: 10, of which 3 were waited for; matrix products, arithmetic and copies ran while one was open for 2% of the time, Pallas kernels for 2%

profile of v9, /device:TPU:0, one launch (start us, length us, event | category | flops | bytes accessed | tf_op | source)
XLA Modules:
  0.0 59.4 jit_solution(13426362506401138837)
XLA Ops:
  0.0 1.6 %collective-permute-start.6 = (bf16[256,128]{1,0:T(8,128)(2,1)}, bf16[256,128]{1,0:T(8,128)(2,1)S(1)}, u32[]{:S(2)}, u32[]{:S(2)}) collective-permute-start(bf16[256,128]{1,0:T(8,128)(2,1)} %bitcast.1), channel_id=1, source_target_pairs={{0,16},{8,12},{1,17},{9,13},{2,18},{10,14},{3,19},{11,15},{4,20},{... | collective-permute-start | bytes 196616 | tf_op jit(solution)/shard_map/ppermute | solution.py:43
  1.6 1.0 %pack.1 = (bf16[1040,128]{1,0:T(8,128)(2,1)S(1)}, bf16[256,128]{1,0:T(8,128)(2,1)S(1)}) custom-call(s32[8]{0:T(128)} %lengths_ref.1, bf16[8,128,128]{2,1,0:T(8,128)(2,1)} %docs_ref.1, bf16[256,128]{1,0:T(8,128)(2,1)} %bitcast.2), custom_call_target="tpu_custom_call" | custom-call | flops 1000000 | bytes 1000000 | tf_op jit(solution)/shard_map/pack/pallas_call | solution.py:85
  2.6 4.1 %collective-permute-start.1 = (bf16[1040,128]{1,0:T(8,128)(2,1)S(1)}, bf16[1040,128]{1,0:T(8,128)(2,1)S(1)}, u32[]{:S(2)}, u32[]{:S(2)}) collective-permute-start(bf16[1040,128]{1,0:T(8,128)(2,1)S(1)} %get-tuple-element.7.refs_0_), channel_id=1, source_target_pairs={{0,3},{8,56},{1,2},{9,57},{2,1},{10,58},{3,0},{11,59},{4,7},{12,60... | collective-permute-start | bytes 798728 | tf_op jit(solution)/shard_map/ppermute | solution.py:43
  6.8 3.0 %collective-permute-start.2 = (bf16[1040,128]{1,0:T(8,128)(2,1)S(1)}, bf16[1040,128]{1,0:T(8,128)(2,1)S(1)}, u32[]{:S(2)}, u32[]{:S(2)}) collective-permute-start(bf16[1040,128]{1,0:T(8,128)(2,1)S(1)} %get-tuple-element.7.refs_0_), channel_id=1, source_target_pairs={{0,68},{8,11},{1,69},{9,10},{2,70},{10,9},{3,71},{11,8},{4,64},{12... | collective-permute-start | bytes 798728 | tf_op jit(solution)/shard_map/ppermute | solution.py:43
  9.8 0.0 collective-permute-done.6
  9.8 0.2 collective-permute-start.7
  10.0 2.1 %collective-permute-start = (bf16[1040,128]{1,0:T(8,128)(2,1)S(1)}, bf16[1040,128]{1,0:T(8,128)(2,1)S(1)}, u32[]{:S(2)}, u32[]{:S(2)}) collective-permute-start(bf16[1040,128]{1,0:T(8,128)(2,1)S(1)} %get-tuple-element.7.refs_0_), channel_id=1, source_target_pairs={{0,48},{8,76},{1,49},{9,77},{2,50},{10,78},{3,51},{11,79},{4,52},{... | collective-permute-start | bytes 798728 | tf_op jit(solution)/shard_map/ppermute | solution.py:43
  12.1 2.7 %collective-permute-done.7 = bf16[512,128]{1,0:T(8,128)(2,1)S(1)} collective-permute-done((bf16[512,128]{1,0:T(8,128)(2,1)S(1)}, bf16[512,128]{1,0:T(8,128)(2,1)S(1)}, u32[]{:S(2)}, u32[]{:S(2)}) %collective-permute-start.7) | collective-permute-done | bytes 131104 | tf_op jit(solution)/shard_map/ppermute | solution.py:43
  14.9 0.1 collective-permute-start.8
  15.0 0.0 collective-permute-done.1.refs_1_
  15.0 1.5 %collective-permute-start.4 = (bf16[1040,128]{1,0:T(8,128)(2,1)S(1)}, bf16[1040,128]{1,0:T(8,128)(2,1)S(1)}, u32[]{:S(2)}, u32[]{:S(2)}) collective-permute-start(bf16[1040,128]{1,0:T(8,128)(2,1)S(1)} %collective-permute-done.1.refs_1_), channel_id=1, source_target_pairs={{0,68},{8,11},{1,69},{9,10},{2,70},{10,9},{3,71},{11,8},{4,64},{12... | collective-permute-start | bytes 798728 | tf_op jit(solution)/shard_map/ppermute | solution.py:43
  16.4 0.0 collective-permute-done.2.refs_2_
  16.4 0.8 %pad_maximum_fusion = bf16[2080,128]{1,0:T(8,128)(2,1)} fusion(bf16[1040,128]{1,0:T(8,128)(2,1)S(1)} %collective-permute-done.2.refs_2_, bf16[1040,128]{1,0:T(8,128)(2,1)S(1)} %collective-permute-done.1.refs_1_), kind=kLoop, calls=%fused_computation | loop fusion | flops 1064960 | bytes 1064960 | tf_op jit(solution)/shard_map/concatenate | solution.py:272
  17.3 2.3 %collective-permute-start.3 = (bf16[2080,128]{1,0:T(8,128)(2,1)}, bf16[2080,128]{1,0:T(8,128)(2,1)S(1)}, u32[]{:S(2)}, u32[]{:S(2)}) collective-permute-start(bf16[2080,128]{1,0:T(8,128)(2,1)} %pad_maximum_fusion), channel_id=1, source_target_pairs={{0,48},{8,76},{1,49},{9,77},{2,50},{10,78},{3,51},{11,79},{4,52},{... | collective-permute-start | bytes 1597448 | tf_op jit(solution)/shard_map/ppermute | solution.py:43
  19.6 5.9 %collective-permute-done.4.refs_3_ = bf16[1040,128]{1,0:T(8,128)(2,1)S(1)} collective-permute-done((bf16[1040,128]{1,0:T(8,128)(2,1)S(1)}, bf16[1040,128]{1,0:T(8,128)(2,1)S(1)}, u32[]{:S(2)}, u32[]{:S(2)}) %collective-permute-start.4) | collective-permute-done | bytes 266272 | tf_op jit(solution)/shard_map/ppermute | solution.py:43
  25.5 2.1 %collective-permute-start.5 = (bf16[1040,128]{1,0:T(8,128)(2,1)S(1)}, bf16[1040,128]{1,0:T(8,128)(2,1)S(1)}, u32[]{:S(2)}, u32[]{:S(2)}) collective-permute-start(bf16[1040,128]{1,0:T(8,128)(2,1)S(1)} %collective-permute-done.4.refs_3_), channel_id=1, source_target_pairs={{0,48},{8,76},{1,49},{9,77},{2,50},{10,78},{3,51},{11,79},{4,52},{... | collective-permute-start | bytes 798728 | tf_op jit(solution)/shard_map/ppermute | solution.py:43
  27.6 0.0 collective-permute-done.8
  27.7 0.1 collective-permute-start.9
  27.8 0.0 collective-permute-done.refs_0_
  27.8 0.1 reshape.13.facts_ref
  27.9 5.2 %collective-permute-done.5.refs_2_ = bf16[1040,128]{1,0:T(8,128)(2,1)S(1)} collective-permute-done((bf16[1040,128]{1,0:T(8,128)(2,1)S(1)}, bf16[1040,128]{1,0:T(8,128)(2,1)S(1)}, u32[]{:S(2)}, u32[]{:S(2)}) %collective-permute-start.5) | collective-permute-done | bytes 266272 | tf_op jit(solution)/shard_map/ppermute | solution.py:43
  33.2 0.0 collective-permute-done.3.refs_1_
  33.2 0.1 reshape.12.facts_ref
  33.3 0.0 collective-permute-done.9.refs_5_.refs_4_
  33.3 7.4 %score.2.refs_5_ = f32[32,128]{1,0:T(8,128)S(1)} custom-call(s32[32]{0:T(128)S(1)} %reshape.13.facts_ref, bf16[1040,128]{1,0:T(8,128)(2,1)S(1)} %get-tuple-element.7.refs_0_, bf16[1040,128]{1,0:T(8,128)(2,1)S(1)} %collective-permute-done.1.refs_1_, bf16[1040,128]{1,0:T(8,128)(2,1)S(1)} %collective-permute-done.2.refs_2_, ...), custom_call_target="tpu_custom_call" | custom-call | flops 6000000000 | bytes 1000000 | tf_op jit(solution)/shard_map/score/pallas_call | solution.py:211
  40.6 8.2 %score.3 = f32[16,8,128]{2,1,0:T(8,128)S(1)} custom-call(s32[32]{0:T(128)S(1)} %reshape.12.facts_ref, bf16[1040,128]{1,0:T(8,128)(2,1)S(1)} %collective-permute-done.refs_0_, bf16[2080,128]{1,0:T(8,128)(2,1)S(1)} %collective-permute-done.3.refs_1_, bf16[1040,128]{1,0:T(8,128)(2,1)S(1)} %collective-permute-done.5.refs_2_, ...), custom_call_target="tpu_custom_call" | custom-call | flops 6000000000 | bytes 1000000 | tf_op jit(solution)/shard_map/score/pallas_call | solution.py:211
  48.9 8.9 %all_to_all.5.given_ref = f32[16,8,128]{2,1,0:T(8,128)} all-to-all(f32[16,8,128]{2,1,0:T(8,128)S(1)} %score.3), channel_id=1, replica_groups={{0,16,4,20,1,17,5,21,8,24,12,28,9,25,13,29},{3,19,7,23,2,18,6,22,11,27,..., dimensions={0} | all-to-all | bytes 131072 | tf_op jit(solution)/shard_map/all_to_all | solution.py:276
  57.8 1.6 %finish.1 = f32[8]{0:T(128)} custom-call(s32[8]{0:T(128)} %positives_ref.1, f32[16,8,128]{2,1,0:T(8,128)} %all_to_all.5.given_ref), custom_call_target="tpu_custom_call" | custom-call | tf_op jit(solution)/shard_map/finish/pallas_call | solution.py:252
  (15 shorter events, 0.1 us)
Async XLA Ops:
  0.0 9.8 %collective-permute-start.6 = (bf16[256,128]{1,0:T(8,128)(2,1)}, bf16[256,128]{1,0:T(8,128)(2,1)S(1)}, u32[]{:S(2)}, u32[]{:S(2)}) collective-permute-start(bf16[256,128]{1,0:T(8,128)(2,1)} %bitcast.1), channel_id=1, source_target_pairs={{0,16},{8,12},{1,17},{9,13},{2,18},{10,14},{3,19},{11,15},{4,20},{... | collective-permute-start | bytes 196616 | tf_op jit(solution)/shard_map/ppermute | solution.py:43
  2.6 12.3 %collective-permute-start.1 = (bf16[1040,128]{1,0:T(8,128)(2,1)S(1)}, bf16[1040,128]{1,0:T(8,128)(2,1)S(1)}, u32[]{:S(2)}, u32[]{:S(2)}) collective-permute-start(bf16[1040,128]{1,0:T(8,128)(2,1)S(1)} %get-tuple-element.7.refs_0_), channel_id=1, source_target_pairs={{0,3},{8,56},{1,2},{9,57},{2,1},{10,58},{3,0},{11,59},{4,7},{12,60... | collective-permute-start | bytes 798728 | tf_op jit(solution)/shard_map/ppermute | solution.py:43
  6.8 9.7 %collective-permute-start.2 = (bf16[1040,128]{1,0:T(8,128)(2,1)S(1)}, bf16[1040,128]{1,0:T(8,128)(2,1)S(1)}, u32[]{:S(2)}, u32[]{:S(2)}) collective-permute-start(bf16[1040,128]{1,0:T(8,128)(2,1)S(1)} %get-tuple-element.7.refs_0_), channel_id=1, source_target_pairs={{0,68},{8,11},{1,69},{9,10},{2,70},{10,9},{3,71},{11,8},{4,64},{12... | collective-permute-start | bytes 798728 | tf_op jit(solution)/shard_map/ppermute | solution.py:43
  9.8 5.0 %collective-permute-start.7 = (bf16[512,128]{1,0:T(8,128)(2,1)S(1)}, bf16[512,128]{1,0:T(8,128)(2,1)S(1)}, u32[]{:S(2)}, u32[]{:S(2)}) collective-permute-start(bf16[512,128]{1,0:T(8,128)(2,1)S(1)} %pad_maximum_fusion.2), channel_id=1, source_target_pairs={{0,4},{8,9},{1,5},{9,8},{2,6},{10,11},{3,7},{11,10},{4,0},{12,13},... | collective-permute-start | bytes 393224 | tf_op jit(solution)/shard_map/ppermute | solution.py:43
  10.0 17.8 %collective-permute-start = (bf16[1040,128]{1,0:T(8,128)(2,1)S(1)}, bf16[1040,128]{1,0:T(8,128)(2,1)S(1)}, u32[]{:S(2)}, u32[]{:S(2)}) collective-permute-start(bf16[1040,128]{1,0:T(8,128)(2,1)S(1)} %get-tuple-element.7.refs_0_), channel_id=1, source_target_pairs={{0,48},{8,76},{1,49},{9,77},{2,50},{10,78},{3,51},{11,79},{4,52},{... | collective-permute-start | bytes 798728 | tf_op jit(solution)/shard_map/ppermute | solution.py:43
  14.9 12.8 %collective-permute-start.8 = (bf16[1024,128]{1,0:T(8,128)(2,1)S(1)}, bf16[1024,128]{1,0:T(8,128)(2,1)S(1)}, u32[]{:S(2)}, u32[]{:S(2)}) collective-permute-start(bf16[1024,128]{1,0:T(8,128)(2,1)S(1)} %pad_maximum_fusion.1), channel_id=1, source_target_pairs={{0,1},{8,24},{1,0},{9,25},{2,3},{10,26},{3,2},{11,27},{4,5},{12,28... | collective-permute-start | bytes 786440 | tf_op jit(solution)/shard_map/ppermute | solution.py:43
  15.0 10.6 %collective-permute-start.4 = (bf16[1040,128]{1,0:T(8,128)(2,1)S(1)}, bf16[1040,128]{1,0:T(8,128)(2,1)S(1)}, u32[]{:S(2)}, u32[]{:S(2)}) collective-permute-start(bf16[1040,128]{1,0:T(8,128)(2,1)S(1)} %collective-permute-done.1.refs_1_), channel_id=1, source_target_pairs={{0,68},{8,11},{1,69},{9,10},{2,70},{10,9},{3,71},{11,8},{4,64},{12... | collective-permute-start | bytes 798728 | tf_op jit(solution)/shard_map/ppermute | solution.py:43
  17.3 15.9 %collective-permute-start.3 = (bf16[2080,128]{1,0:T(8,128)(2,1)}, bf16[2080,128]{1,0:T(8,128)(2,1)S(1)}, u32[]{:S(2)}, u32[]{:S(2)}) collective-permute-start(bf16[2080,128]{1,0:T(8,128)(2,1)} %pad_maximum_fusion), channel_id=1, source_target_pairs={{0,48},{8,76},{1,49},{9,77},{2,50},{10,78},{3,51},{11,79},{4,52},{... | collective-permute-start | bytes 1597448 | tf_op jit(solution)/shard_map/ppermute | solution.py:43
  25.5 7.6 %collective-permute-start.5 = (bf16[1040,128]{1,0:T(8,128)(2,1)S(1)}, bf16[1040,128]{1,0:T(8,128)(2,1)S(1)}, u32[]{:S(2)}, u32[]{:S(2)}) collective-permute-start(bf16[1040,128]{1,0:T(8,128)(2,1)S(1)} %collective-permute-done.4.refs_3_), channel_id=1, source_target_pairs={{0,48},{8,76},{1,49},{9,77},{2,50},{10,78},{3,51},{11,79},{4,52},{... | collective-permute-start | bytes 798728 | tf_op jit(solution)/shard_map/ppermute | solution.py:43
  27.7 5.6 %collective-permute-start.9 = (bf16[2048,128]{1,0:T(8,128)(2,1)S(1)}, bf16[2048,128]{1,0:T(8,128)(2,1)S(1)}, u32[]{:S(2)}, u32[]{:S(2)}) collective-permute-start(bf16[2048,128]{1,0:T(8,128)(2,1)S(1)} %constant_dynamic-update-slice_fusion.refs_4_.refs_3_), channel_id=1, source_target_pairs={{0,8},{8,0},{1,9},{9,1},{2,10},{10,2},{3,11},{11,3},{4,12},{12,4},... | collective-permute-start | bytes 1572872 | tf_op jit(solution)/shard_map/ppermute | solution.py:48

commit v10 on v9

--- a/solution.py
+++ b/solution.py
@@ -34,7 +34,7 @@
     return ((0, 1, 1, 0) if dim[1] == "a" else (0, 0, 1, 1))[at]
 
 
-DOC_STEPS = (("zb", "yb", "xb"), ("xb", "zb", "yb"))
+DOC_STEPS = (("xb", "yb", "zb"), ("yb", "zb", "xb"))
 QUERY_STEPS = (("xa", "ya", "za"), ("ya", "za", "xa"))
 
 
@@ -269,7 +269,9 @@
     query = jnp.concatenate([query, swap(query, QUERY_STEPS, 1)])
     query = jnp.concatenate([query, swap(query, QUERY_STEPS, 2)])
     near = [own, first, second, swap(first, DOC_STEPS, 1)]
-    far = [third, swap(jnp.concatenate(near[1:3]), DOC_STEPS, 2), swap(near[3], DOC_STEPS, 2)]
+    two = lax.dynamic_update_slice(jnp.zeros((2 * PAY, DIM), jnp.bfloat16), first, (0, 0))
+    two = lax.dynamic_update_slice(lax.optimization_barrier(two), second, (PAY, 0))
+    far = [third, swap(two, DOC_STEPS, 2), swap(near[3], DOC_STEPS, 2)]
     queries = [query, swap_cores(query)]
     given = score(lengths_of(near), near, queries)
     given = score(lengths_of(far), far, queries, given)

time: 60.1 us -> 58.1 us (0.967)
  waiting for transfers between devices: 13.9 us -> 8.25 us
  starting transfers between devices: 17.1 us -> 20.8 us
  local copies, waits for them, and re-layouts: 0.26 us -> 1.81 us
  other arithmetic: 0.88 us -> 0.06 us
  Pallas kernels: 18.2 us -> 17.5 us
    ppermute x9, waiting for transfers between devices: 13.9 us -> 8.24 us  [swap(): return lax.ppermute(array, 'd', pairs)]
    ppermute x9, starting transfers between devices: 17 us -> 20.7 us  [swap(): return lax.ppermute(array, 'd', pairs)]
    dynamic_update_slice x0 -> x2, local copies, waits for them, and re-layouts: none -> 1.56 us  [the longest x1 0.84 us: local(): lax.dynamic_update_slice(jnp.zeros((2 * PAY, DIM), jnp.bfloat16), first,...]
    concatenate x1 -> x0, other arithmetic: 0.82 us -> none  [local(): jnp.concatenate(near[1:3])]
    pallas_call x2, Pallas kernels: 15.6 us -> 14.9 us  [score(): pl.pallas_call(functools.partial(score_kernel, sizes, blocks, final), out...]
  transfers between devices with their start and end apart: 10 -> 10, of which waited for: 3 -> 3; matrix products, arithmetic and copies ran while one was open for 2% -> 3% of each run, Pallas kernels for 2% -> 2%
where the time goes in v10:
time: 58.1 us; the launch traced here: 57.4 us
  starting transfers between devices  20.8 us (36%)
  Pallas kernels  17.5 us (30%)
  blocking collectives  8.9 us (15%)
  waiting for transfers between devices  8.25 us (14%)
  local copies, waits for them, and re-layouts  1.81 us (3%)
    ppermute x9, starting transfers between devices, swap(): return lax.ppermute(array, 'd', pairs)  20.7 us
    pallas_call x2, Pallas kernels, score(): pl.pallas_call(functools.partial(score_kernel, sizes, blocks, final), out...  14.9 us
    all_to_all x1, blocking collectives, local(): lax.all_to_all(given, 'd', 0, 0, tiled=True, axis_index_groups=owner_grou...  8.9 us
    ppermute x9, waiting for transfers between devices, swap(): return lax.ppermute(array, 'd', pairs)  8.24 us
    pallas_call x1, Pallas kernels, finish(): pl.pallas_call(finish_kernel, out_shape=jax.ShapeDtypeStruct((QUERIES,),...  1.57 us
  transfers between devices with their start and end apart: 10, of which 3 were waited for; matrix products, arithmetic and copies ran while one was open for 3% of the time, Pallas kernels for 2%

profile of v10, /device:TPU:0, one launch (start us, length us, event | category | flops | bytes accessed | tf_op | source)
XLA Modules:
  0.0 57.4 jit_solution(2360335080684918673)
XLA Ops:
  0.0 1.6 %collective-permute-start.6 = (bf16[256,128]{1,0:T(8,128)(2,1)}, bf16[256,128]{1,0:T(8,128)(2,1)S(1)}, u32[]{:S(2)}, u32[]{:S(2)}) collective-permute-start(bf16[256,128]{1,0:T(8,128)(2,1)} %bitcast.1), channel_id=1, source_target_pairs={{0,16},{8,12},{1,17},{9,13},{2,18},{10,14},{3,19},{11,15},{4,20},{... | collective-permute-start | bytes 196616 | tf_op jit(solution)/shard_map/ppermute | solution.py:43
  1.6 1.0 %pack.1 = (bf16[1040,128]{1,0:T(8,128)(2,1)S(1)}, bf16[256,128]{1,0:T(8,128)(2,1)S(1)}) custom-call(s32[8]{0:T(128)} %lengths_ref.1, bf16[8,128,128]{2,1,0:T(8,128)(2,1)} %docs_ref.1, bf16[256,128]{1,0:T(8,128)(2,1)} %bitcast.2), custom_call_target="tpu_custom_call" | custom-call | flops 1000000 | bytes 1000000 | tf_op jit(solution)/shard_map/pack/pallas_call | solution.py:85
  2.6 2.2 %collective-permute-start.1 = (bf16[1040,128]{1,0:T(8,128)(2,1)S(1)}, bf16[1040,128]{1,0:T(8,128)(2,1)S(1)}, u32[]{:S(2)}, u32[]{:S(2)}) collective-permute-start(bf16[1040,128]{1,0:T(8,128)(2,1)S(1)} %get-tuple-element.7.refs_0_), channel_id=1, source_target_pairs={{0,48},{8,76},{1,49},{9,77},{2,50},{10,78},{3,51},{11,79},{4,52},{... | collective-permute-start | bytes 798728 | tf_op jit(solution)/shard_map/ppermute | solution.py:43
  4.8 3.0 %collective-permute-start.2 = (bf16[1040,128]{1,0:T(8,128)(2,1)S(1)}, bf16[1040,128]{1,0:T(8,128)(2,1)S(1)}, u32[]{:S(2)}, u32[]{:S(2)}) collective-permute-start(bf16[1040,128]{1,0:T(8,128)(2,1)S(1)} %get-tuple-element.7.refs_0_), channel_id=1, source_target_pairs={{0,68},{8,11},{1,69},{9,10},{2,70},{10,9},{3,71},{11,8},{4,64},{12... | collective-permute-start | bytes 798728 | tf_op jit(solution)/shard_map/ppermute | solution.py:43
  7.8 0.0 collective-permute-done.6
  7.9 0.2 collective-permute-start.7
  8.1 4.0 %collective-permute-start = (bf16[1040,128]{1,0:T(8,128)(2,1)S(1)}, bf16[1040,128]{1,0:T(8,128)(2,1)S(1)}, u32[]{:S(2)}, u32[]{:S(2)}) collective-permute-start(bf16[1040,128]{1,0:T(8,128)(2,1)S(1)} %get-tuple-element.7.refs_0_), channel_id=1, source_target_pairs={{0,3},{8,56},{1,2},{9,57},{2,1},{10,58},{3,0},{11,59},{4,7},{12,60... | collective-permute-start | bytes 798728 | tf_op jit(solution)/shard_map/ppermute | solution.py:43
  12.1 0.8 %collective-permute-done.7 = bf16[512,128]{1,0:T(8,128)(2,1)S(1)} collective-permute-done((bf16[512,128]{1,0:T(8,128)(2,1)S(1)}, bf16[512,128]{1,0:T(8,128)(2,1)S(1)}, u32[]{:S(2)}, u32[]{:S(2)}) %collective-permute-start.7) | collective-permute-done | bytes 131104 | tf_op jit(solution)/shard_map/ppermute | solution.py:43
  12.9 2.0 %collective-permute-start.8 = (bf16[1024,128]{1,0:T(8,128)(2,1)S(1)}, bf16[1024,128]{1,0:T(8,128)(2,1)S(1)}, u32[]{:S(2)}, u32[]{:S(2)}) collective-permute-start(bf16[1024,128]{1,0:T(8,128)(2,1)S(1)} %pad_maximum_fusion), channel_id=1, source_target_pairs={{0,1},{8,24},{1,0},{9,25},{2,3},{10,26},{3,2},{11,27},{4,5},{12,28... | collective-permute-start | bytes 786440 | tf_op jit(solution)/shard_map/ppermute | solution.py:43
  14.9 0.0 collective-permute-done.1.refs_1_
  14.9 0.8 %dynamic_update_slice.6 = bf16[2080,128]{1,0:T(8,128)(2,1)} pad(bf16[1040,128]{1,0:T(8,128)(2,1)S(1)} %collective-permute-done.1.refs_1_, bf16[]{:T(256)} %constant.0.clone.1), padding=0_1040x0_0 | pad | bytes 798722 | tf_op jit(solution)/shard_map/dynamic_update_slice | solution.py:272
  15.8 0.2 collective-permute-start.4
  16.0 0.0 collective-permute-done.2.refs_2_
  16.0 0.7 %constant_dynamic-update-slice_fusion.4 = bf16[2080,128]{1,0:T(8,128)(2,1)} fusion(bf16[2080,128]{1,0:T(8,128)(2,1)} %dynamic_update_slice.6, bf16[1040,128]{1,0:T(8,128)(2,1)S(1)} %collective-permute-done.2.refs_2_), kind=kLoop, calls=%fused_computation.8 | loop fusion | bytes 532480 | tf_op jit(solution)/shard_map/dynamic_update_slice | solution.py:273
  16.7 4.9 %collective-permute-start.3 = (bf16[2080,128]{1,0:T(8,128)(2,1)}, bf16[2080,128]{1,0:T(8,128)(2,1)S(1)}, u32[]{:S(2)}, u32[]{:S(2)}) collective-permute-start(bf16[2080,128]{1,0:T(8,128)(2,1)} %constant_dynamic-update-slice_fusion.4), channel_id=1, source_target_pairs={{0,3},{8,56},{1,2},{9,57},{2,1},{10,58},{3,0},{11,59},{4,7},{12,60... | collective-permute-start | bytes 1597448 | tf_op jit(solution)/shard_map/ppermute | solution.py:43
  21.7 1.7 %collective-permute-done.4.refs_3_ = bf16[1040,128]{1,0:T(8,128)(2,1)S(1)} collective-permute-done((bf16[1040,128]{1,0:T(8,128)(2,1)S(1)}, bf16[1040,128]{1,0:T(8,128)(2,1)S(1)}, u32[]{:S(2)}, u32[]{:S(2)}) %collective-permute-start.4) | collective-permute-done | bytes 266272 | tf_op jit(solution)/shard_map/ppermute | solution.py:43
  23.4 2.5 %collective-permute-start.5 = (bf16[1040,128]{1,0:T(8,128)(2,1)S(1)}, bf16[1040,128]{1,0:T(8,128)(2,1)S(1)}, u32[]{:S(2)}, u32[]{:S(2)}) collective-permute-start(bf16[1040,128]{1,0:T(8,128)(2,1)S(1)} %collective-permute-done.4.refs_3_), channel_id=1, source_target_pairs={{0,3},{8,56},{1,2},{9,57},{2,1},{10,58},{3,0},{11,59},{4,7},{12,60... | collective-permute-start | bytes 798728 | tf_op jit(solution)/shard_map/ppermute | solution.py:43
  25.9 0.0 collective-permute-done.8
  26.0 0.1 collective-permute-start.9
  26.1 0.0 collective-permute-done.refs_0_
  26.1 0.1 reshape.13.facts_ref
  26.2 5.7 %collective-permute-done.5.refs_2_ = bf16[1040,128]{1,0:T(8,128)(2,1)S(1)} collective-permute-done((bf16[1040,128]{1,0:T(8,128)(2,1)S(1)}, bf16[1040,128]{1,0:T(8,128)(2,1)S(1)}, u32[]{:S(2)}, u32[]{:S(2)}) %collective-permute-start.5) | collective-permute-done | bytes 266272 | tf_op jit(solution)/shard_map/ppermute | solution.py:43
  31.9 0.0 collective-permute-done.3.refs_1_
  32.0 0.1 reshape.12.facts_ref
  32.0 0.0 collective-permute-done.9.refs_5_.refs_4_
  32.0 7.4 %score.2.refs_5_ = f32[32,128]{1,0:T(8,128)S(1)} custom-call(s32[32]{0:T(128)S(1)} %reshape.13.facts_ref, bf16[1040,128]{1,0:T(8,128)(2,1)S(1)} %get-tuple-element.7.refs_0_, bf16[1040,128]{1,0:T(8,128)(2,1)S(1)} %collective-permute-done.1.refs_1_, bf16[1040,128]{1,0:T(8,128)(2,1)S(1)} %collective-permute-done.2.refs_2_, ...), custom_call_target="tpu_custom_call" | custom-call | flops 6000000000 | bytes 1000000 | tf_op jit(solution)/shard_map/score/pallas_call | solution.py:211
  39.4 7.5 %score.3 = f32[16,8,128]{2,1,0:T(8,128)S(1)} custom-call(s32[32]{0:T(128)S(1)} %reshape.12.facts_ref, bf16[1040,128]{1,0:T(8,128)(2,1)S(1)} %collective-permute-done.refs_0_, bf16[2080,128]{1,0:T(8,128)(2,1)S(1)} %collective-permute-done.3.refs_1_, bf16[1040,128]{1,0:T(8,128)(2,1)S(1)} %collective-permute-done.5.refs_2_, ...), custom_call_target="tpu_custom_call" | custom-call | flops 6000000000 | bytes 1000000 | tf_op jit(solution)/shard_map/score/pallas_call | solution.py:211
  46.9 8.9 %all_to_all.5.given_ref = f32[16,8,128]{2,1,0:T(8,128)} all-to-all(f32[16,8,128]{2,1,0:T(8,128)S(1)} %score.3), channel_id=1, replica_groups={{0,16,4,20,1,17,5,21,8,24,12,28,9,25,13,29},{3,19,7,23,2,18,6,22,11,27,..., dimensions={0} | all-to-all | bytes 131072 | tf_op jit(solution)/shard_map/all_to_all | solution.py:278
  55.8 1.6 %finish.1 = f32[8]{0:T(128)} custom-call(s32[8]{0:T(128)} %positives_ref.1, f32[16,8,128]{2,1,0:T(8,128)} %all_to_all.5.given_ref), custom_call_target="tpu_custom_call" | custom-call | tf_op jit(solution)/shard_map/finish/pallas_call | solution.py:252
  (15 shorter events, 0.1 us)
Async XLA Ops:
  0.0 7.8 %collective-permute-start.6 = (bf16[256,128]{1,0:T(8,128)(2,1)}, bf16[256,128]{1,0:T(8,128)(2,1)S(1)}, u32[]{:S(2)}, u32[]{:S(2)}) collective-permute-start(bf16[256,128]{1,0:T(8,128)(2,1)} %bitcast.1), channel_id=1, source_target_pairs={{0,16},{8,12},{1,17},{9,13},{2,18},{10,14},{3,19},{11,15},{4,20},{... | collective-permute-start | bytes 196616 | tf_op jit(solution)/shard_map/ppermute | solution.py:43
  2.6 12.3 %collective-permute-start.1 = (bf16[1040,128]{1,0:T(8,128)(2,1)S(1)}, bf16[1040,128]{1,0:T(8,128)(2,1)S(1)}, u32[]{:S(2)}, u32[]{:S(2)}) collective-permute-start(bf16[1040,128]{1,0:T(8,128)(2,1)S(1)} %get-tuple-element.7.refs_0_), channel_id=1, source_target_pairs={{0,48},{8,76},{1,49},{9,77},{2,50},{10,78},{3,51},{11,79},{4,52},{... | collective-permute-start | bytes 798728 | tf_op jit(solution)/shard_map/ppermute | solution.py:43
  4.8 11.2 %collective-permute-start.2 = (bf16[1040,128]{1,0:T(8,128)(2,1)S(1)}, bf16[1040,128]{1,0:T(8,128)(2,1)S(1)}, u32[]{:S(2)}, u32[]{:S(2)}) collective-permute-start(bf16[1040,128]{1,0:T(8,128)(2,1)S(1)} %get-tuple-element.7.refs_0_), channel_id=1, source_target_pairs={{0,68},{8,11},{1,69},{9,10},{2,70},{10,9},{3,71},{11,8},{4,64},{12... | collective-permute-start | bytes 798728 | tf_op jit(solution)/shard_map/ppermute | solution.py:43
  7.9 5.0 %collective-permute-start.7 = (bf16[512,128]{1,0:T(8,128)(2,1)S(1)}, bf16[512,128]{1,0:T(8,128)(2,1)S(1)}, u32[]{:S(2)}, u32[]{:S(2)}) collective-permute-start(bf16[512,128]{1,0:T(8,128)(2,1)S(1)} %pad_maximum_fusion.1), channel_id=1, source_target_pairs={{0,4},{8,9},{1,5},{9,8},{2,6},{10,11},{3,7},{11,10},{4,0},{12,13},... | collective-permute-start | bytes 393224 | tf_op jit(solution)/shard_map/ppermute | solution.py:43
  8.1 18.0 %collective-permute-start = (bf16[1040,128]{1,0:T(8,128)(2,1)S(1)}, bf16[1040,128]{1,0:T(8,128)(2,1)S(1)}, u32[]{:S(2)}, u32[]{:S(2)}) collective-permute-start(bf16[1040,128]{1,0:T(8,128)(2,1)S(1)} %get-tuple-element.7.refs_0_), channel_id=1, source_target_pairs={{0,3},{8,56},{1,2},{9,57},{2,1},{10,58},{3,0},{11,59},{4,7},{12,60... | collective-permute-start | bytes 798728 | tf_op jit(solution)/shard_map/ppermute | solution.py:43
  12.9 13.0 %collective-permute-start.8 = (bf16[1024,128]{1,0:T(8,128)(2,1)S(1)}, bf16[1024,128]{1,0:T(8,128)(2,1)S(1)}, u32[]{:S(2)}, u32[]{:S(2)}) collective-permute-start(bf16[1024,128]{1,0:T(8,128)(2,1)S(1)} %pad_maximum_fusion), channel_id=1, source_target_pairs={{0,1},{8,24},{1,0},{9,25},{2,3},{10,26},{3,2},{11,27},{4,5},{12,28... | collective-permute-start | bytes 786440 | tf_op jit(solution)/shard_map/ppermute | solution.py:43
  15.8 7.6 %collective-permute-start.4 = (bf16[1040,128]{1,0:T(8,128)(2,1)S(1)}, bf16[1040,128]{1,0:T(8,128)(2,1)S(1)}, u32[]{:S(2)}, u32[]{:S(2)}) collective-permute-start(bf16[1040,128]{1,0:T(8,128)(2,1)S(1)} %collective-permute-done.1.refs_1_), channel_id=1, source_target_pairs={{0,68},{8,11},{1,69},{9,10},{2,70},{10,9},{3,71},{11,8},{4,64},{12... | collective-permute-start | bytes 798728 | tf_op jit(solution)/shard_map/ppermute | solution.py:43
  16.7 15.2 %collective-permute-start.3 = (bf16[2080,128]{1,0:T(8,128)(2,1)}, bf16[2080,128]{1,0:T(8,128)(2,1)S(1)}, u32[]{:S(2)}, u32[]{:S(2)}) collective-permute-start(bf16[2080,128]{1,0:T(8,128)(2,1)} %constant_dynamic-update-slice_fusion.4), channel_id=1, source_target_pairs={{0,3},{8,56},{1,2},{9,57},{2,1},{10,58},{3,0},{11,59},{4,7},{12,60... | collective-permute-start | bytes 1597448 | tf_op jit(solution)/shard_map/ppermute | solution.py:43
  23.4 8.5 %collective-permute-start.5 = (bf16[1040,128]{1,0:T(8,128)(2,1)S(1)}, bf16[1040,128]{1,0:T(8,128)(2,1)S(1)}, u32[]{:S(2)}, u32[]{:S(2)}) collective-permute-start(bf16[1040,128]{1,0:T(8,128)(2,1)S(1)} %collective-permute-done.4.refs_3_), channel_id=1, source_target_pairs={{0,3},{8,56},{1,2},{9,57},{2,1},{10,58},{3,0},{11,59},{4,7},{12,60... | collective-permute-start | bytes 798728 | tf_op jit(solution)/shard_map/ppermute | solution.py:43
  26.0 6.1 %collective-permute-start.9 = (bf16[2048,128]{1,0:T(8,128)(2,1)S(1)}, bf16[2048,128]{1,0:T(8,128)(2,1)S(1)}, u32[]{:S(2)}, u32[]{:S(2)}) collective-permute-start(bf16[2048,128]{1,0:T(8,128)(2,1)S(1)} %constant_dynamic-update-slice_fusion.refs_4_.refs_3_), channel_id=1, source_target_pairs={{0,8},{8,0},{1,9},{9,1},{2,10},{10,2},{3,11},{11,3},{4,12},{12,4},... | collective-permute-start | bytes 1572872 | tf_op jit(solution)/shard_map/ppermute | solution.py:48
